TPU v7x, 16 devices: a whole 2x2x2 slice. The times are simulated.
16 devices in a mesh: dp: 2 (over z), ep: 8 (over y, x, core).
Axes of the slice: x: 2, y: 2, z: 2, core: 2. Of those that a mesh axis runs over, the one named last changes fastest.
Arguments:
- x_tokens: bfloat16 [2048, 2048], P(('dp', 'ep')), parts along dimension 0
- dy_tokens: bfloat16 [2048, 2048], P(('dp', 'ep')), parts along dimension 0
- expert_ids: int32 [2048, 10], P(('dp', 'ep')), parts along dimension 0
- gate_vals: float32 [2048, 10], P(('dp', 'ep')), parts along dimension 0
- slot_pos: int32 [2048, 10], P(('dp', 'ep')), parts along dimension 0
- w_gate: bfloat16 [32, 2048, 512], P('ep')
- w_up: bfloat16 [32, 2048, 512], P('ep')
- w_down: bfloat16 [32, 512, 2048], P('ep')
- shared_gate: bfloat16 [2048, 512], replicated
- shared_up: bfloat16 [2048, 512], replicated
- shared_down: bfloat16 [512, 2048], replicated
Outputs:
- output 1: bfloat16 [2048, 2048], P(('dp', 'ep')), parts along dimension 0
- output 2: float32 [64, 2048, 512], P(('dp', 'ep')), parts along dimension 0
- output 3: float32 [64, 2048, 512], P(('dp', 'ep')), parts along dimension 0
- output 4: float32 [64, 512, 2048], P(('dp', 'ep')), parts along dimension 0
- output 5: float32 [16, 2048, 512], P(('dp', 'ep')), parts along dimension 0
- output 6: float32 [16, 2048, 512], P(('dp', 'ep')), parts along dimension 0
- output 7: float32 [16, 512, 2048], P(('dp', 'ep')), parts along dimension 0
There are 2 independent parts. A program takes and returns all parts, laid end to end along the dimension named above; an argument that names none is the same for every part.
All inputs are finite; a program needn't handle non-finite values.
Results may differ from a plain program's by a relative error of at most 0.0104866.
Values are sent between devices in bfloat16 or wider.
A program may use at most 1 GiB of HBM per device.

v0:
```python
import jax
import jax.numpy as jnp
from jax import lax
from jax.sharding import PartitionSpec as P


def swiglu_parts(act_gate, act_up, grad_hidden):
    gate_f32 = act_gate.astype(jnp.float32)
    up_f32 = act_up.astype(jnp.float32)
    sigma = jax.nn.sigmoid(gate_f32)
    silu_gate = gate_f32 * sigma
    hidden = (silu_gate * up_f32).astype(jnp.bfloat16)
    grad_gate = (grad_hidden * up_f32 * sigma * (1.0 + gate_f32 * (1.0 - sigma))).astype(jnp.bfloat16)
    grad_up = (grad_hidden * silu_gate).astype(jnp.bfloat16)
    return hidden, grad_gate, grad_up


def slot_tables(expert_ids, slot_pos, gate_vals, num_experts, capacity):
    tok_count, top_k = expert_ids.shape
    slot_total = num_experts * capacity
    copy_slot = jnp.where(slot_pos >= 0, expert_ids * capacity + slot_pos, slot_total).reshape(-1)
    copy_token = jnp.broadcast_to(jnp.arange(tok_count, dtype=jnp.int32)[:, None], (tok_count, top_k)).reshape(-1)
    slot_token = jnp.full((slot_total + 1,), tok_count, jnp.int32).at[copy_slot].set(copy_token)[:slot_total]
    slot_gate = jnp.zeros((slot_total + 1,), jnp.float32).at[copy_slot].set(gate_vals.reshape(-1))[:slot_total]
    return copy_slot, slot_token, slot_gate


def take_rows(rows, row_index):
    return jnp.take(rows, row_index, axis=0, mode='fill', fill_value=0)


def shared_backward(x_tokens, dy_tokens, shared_gate, shared_up, shared_down):
    act_gate = jnp.dot(x_tokens, shared_gate, preferred_element_type=jnp.float32).astype(jnp.bfloat16)
    act_up = jnp.dot(x_tokens, shared_up, preferred_element_type=jnp.float32).astype(jnp.bfloat16)
    grad_hidden = jnp.einsum('td,fd->tf', dy_tokens, shared_down, preferred_element_type=jnp.float32)
    hidden, grad_gate, grad_up = swiglu_parts(act_gate, act_up, grad_hidden)
    grad_gate_w = jnp.einsum('td,tf->df', x_tokens, grad_gate, preferred_element_type=jnp.float32)
    grad_up_w = jnp.einsum('td,tf->df', x_tokens, grad_up, preferred_element_type=jnp.float32)
    grad_down_w = jnp.einsum('tf,td->fd', hidden, dy_tokens, preferred_element_type=jnp.float32)
    grad_input = jnp.einsum('tf,df->td', grad_gate, shared_gate, preferred_element_type=jnp.float32) + jnp.einsum('tf,df->td', grad_up, shared_up, preferred_element_type=jnp.float32)
    return grad_input, grad_gate_w, grad_up_w, grad_down_w


def solution(mesh):
    group = mesh.shape['ep']
    token_spec = P(('dp', 'ep'), None)
    expert_spec = P('ep', None, None)
    whole_spec = P(None, None)
    grad_spec = P(('dp', 'ep'), None, None)

    def local_backward(x_tokens, dy_tokens, expert_ids, gate_vals, slot_pos, w_gate, w_up, w_down, shared_gate, shared_up, shared_down):
        tok_count, top_k = expert_ids.shape
        local_experts, model_dim, expert_ff = w_gate.shape
        num_experts = local_experts * group
        capacity = (3 * tok_count * top_k + 2 * num_experts - 1) // (2 * num_experts)
        copy_slot, slot_token, slot_gate = slot_tables(expert_ids, slot_pos, gate_vals, num_experts, capacity)
        send_x = take_rows(x_tokens, slot_token).reshape(num_experts, capacity, model_dim)
        dy_rows = take_rows(dy_tokens, slot_token)
        send_dz = (dy_rows.astype(jnp.float32) * slot_gate[:, None]).astype(jnp.bfloat16).reshape(num_experts, capacity, model_dim)
        x_exp = lax.all_to_all(send_x, 'ep', 0, 1, tiled=True)
        dz_exp = lax.all_to_all(send_dz, 'ep', 0, 1, tiled=True)
        act_gate = jnp.einsum('erd,edf->erf', x_exp, w_gate, preferred_element_type=jnp.float32).astype(jnp.bfloat16)
        act_up = jnp.einsum('erd,edf->erf', x_exp, w_up, preferred_element_type=jnp.float32).astype(jnp.bfloat16)
        grad_hidden = jnp.einsum('erd,efd->erf', dz_exp, w_down, preferred_element_type=jnp.float32)
        hidden, grad_gate, grad_up = swiglu_parts(act_gate, act_up, grad_hidden)
        grad_w_gate = jnp.einsum('erd,erf->edf', x_exp, grad_gate, preferred_element_type=jnp.float32)
        grad_w_up = jnp.einsum('erd,erf->edf', x_exp, grad_up, preferred_element_type=jnp.float32)
        grad_w_down = jnp.einsum('erf,erd->efd', hidden, dz_exp, preferred_element_type=jnp.float32)
        grad_exp = (jnp.einsum('erf,edf->erd', grad_gate, w_gate, preferred_element_type=jnp.float32) + jnp.einsum('erf,edf->erd', grad_up, w_up, preferred_element_type=jnp.float32)).astype(jnp.bfloat16)
        returned = lax.all_to_all(grad_exp, 'ep', 1, 0, tiled=True).reshape(num_experts * capacity, model_dim)
        copies = take_rows(returned, copy_slot).reshape(tok_count, top_k, model_dim)
        routed_sum = jnp.sum(copies.astype(jnp.float32), axis=1)
        shared_dx, grad_shared_gate, grad_shared_up, grad_shared_down = shared_backward(x_tokens, dy_tokens, shared_gate, shared_up, shared_down)
        grad_x = (routed_sum + shared_dx).astype(jnp.bfloat16)
        return grad_x, grad_w_gate, grad_w_up, grad_w_down, grad_shared_gate[None], grad_shared_up[None], grad_shared_down[None]

    return jax.shard_map(local_backward, mesh=mesh, in_specs=(token_spec, token_spec, token_spec, token_spec, token_spec, expert_spec, expert_spec, expert_spec, whole_spec, whole_spec, whole_spec), out_specs=(token_spec, grad_spec, grad_spec, grad_spec, grad_spec, grad_spec, grad_spec), check_vma=False)
```

profile of v0, /device:TPU:0, one launch (start us, length us, event | category | flops | bytes accessed | tf_op | source)
XLA Modules:
  0.0 480.0 jit_solution(5884400968919220925)
XLA Ops:
  2.5 5.2 %scatter_custom_fusion = s32[1921]{0:T(1024)S(1)} fusion(s32[1280]{0:T(1024)S(1)} %get-tuple-element.30, s32[1280]{0:T(1024)S(1)} %reshape.135, s32[]{:T(128)} %constant.14.clone.1), kind=kCustom, calls=%fused_computation.65 | custom fusion | bytes 7688 | tf_op jit(solution)/shard_map/scatter | solution.py:23
  7.8 17.4 %gather_fusion.2 = bf16[1920,2048]{1,0:T(8,128)(2,1)} fusion(bf16[128,2048]{1,0:T(8,128)(2,1)} %param.13, s32[2048]{0:T(1024)S(1)} %pad_clamp_fusion.1), kind=kCustom, calls=%fused_computation.1.clone | custom fusion | bytes 15736320 | tf_op jit(solution)/shard_map/jit(_take)/gather | solution.py:29
  25.2 7.1 %broadcast_select_fusion = bf16[1920,2048]{1,0:T(8,128)(2,1)} fusion(bf16[1920,2048]{1,0:T(8,128)(2,1)} %gather_fusion.2, pred[1920]{0:T(1024)(128)(4,1)S(1)} %compare_and_fusion), kind=kLoop, calls=%fused_computation.8 | loop fusion | flops 3932160 | bytes 15730560 | tf_op jit(solution)/shard_map/jit(_take)/select_n | solution.py:29
  32.3 9.1 %reshape.105 = bf16[32,60,2048]{2,1,0:T(8,128)(2,1)} reshape(bf16[1920,2048]{1,0:T(8,128)(2,1)} %broadcast_select_fusion) | data formatting | bytes 15728640 | tf_op jit(solution)/shard_map/reshape | solution.py:57
  41.4 5.6 %all-to-all-start.1 = ((bf16[32,60,2048]{2,1,0:T(8,128)(2,1)}), bf16[32,60,2048]{2,1,0:T(8,128)(2,1)}, u32[]{:S(2)}, u32[]{:S(2)}) async-start(bf16[32,60,2048]{2,1,0:T(8,128)(2,1)} %reshape.105), calls=%async_computation.1 | async-start | bytes 16777216 | tf_op jit(solution)/shard_map/all_to_all | solution.py:60
  47.0 8.6 %gather_fusion.1 = bf16[1920,2048]{1,0:T(8,128)(2,1)} fusion(bf16[128,2048]{1,0:T(8,128)(2,1)S(1)} %copy-done.2, s32[2048]{0:T(1024)S(1)} %pad_clamp_fusion.1), kind=kCustom, calls=%fused_computation.clone | custom fusion | bytes 15736320 | tf_op jit(solution)/shard_map/jit(_take)/gather | solution.py:29
  55.9 5.2 %scatter_custom_fusion.1 = f32[1921]{0:T(1024)S(1)} fusion(s32[1280]{0:T(1024)S(1)} %get-tuple-element.30, f32[1280]{0:T(1024)S(1)} %reshape.143, f32[]{:T(128)} %constant.23.clone.1), kind=kCustom, calls=%fused_computation.63 | custom fusion | bytes 7688 | tf_op jit(solution)/shard_map/scatter | solution.py:24
  61.2 7.6 %multiply_convert_fusion = bf16[1920,2048]{1,0:T(8,128)(2,1)} fusion(bf16[1920,2048]{1,0:T(8,128)(2,1)} %gather_fusion.1, f32[1920]{0:T(1024)S(1)} %bitcast.52, pred[1920]{0:T(1024)(128)(4,1)S(1)} %compare_and_fusion), kind=kLoop, calls=%fused_computation.7 | loop fusion | flops 15728640 | bytes 15738240 | tf_op jit(solution)/shard_map/convert_element_type | solution.py:59
  68.8 9.1 %reshape.104 = bf16[32,60,2048]{2,1,0:T(8,128)(2,1)} reshape(bf16[1920,2048]{1,0:T(8,128)(2,1)} %multiply_convert_fusion) | data formatting | bytes 15728640 | tf_op jit(solution)/shard_map/reshape | solution.py:59
  77.9 63.6 %all-to-all-done.1 = bf16[32,60,2048]{2,1,0:T(8,128)(2,1)} async-done(((bf16[32,60,2048]{2,1,0:T(8,128)(2,1)}), bf16[32,60,2048]{2,1,0:T(8,128)(2,1)}, u32[]{:S(2)}, u32[]{:S(2)}) %all-to-all-start.1) | async-done | bytes 7864352 | tf_op jit(solution)/shard_map/all_to_all | solution.py:60
  141.5 5.4 %all-to-all-start = ((bf16[32,60,2048]{2,1,0:T(8,128)(2,1)}), bf16[32,60,2048]{2,1,0:T(8,128)(2,1)}, u32[]{:S(2)}, u32[]{:S(2)}) async-start(bf16[32,60,2048]{2,1,0:T(8,128)(2,1)} %reshape.104), calls=%async_computation | async-start | bytes 16777216 | tf_op jit(solution)/shard_map/all_to_all | solution.py:61
  146.9 9.5 %copy.59 = bf16[8,4,60,2048]{3,1,2,0:T(4,128)(2,1)S(1)} copy(bf16[8,4,60,2048]{3,2,1,0:T(8,128)(2,1)} %bitcast.4) | data formatting | bytes 15728640 | tf_op jit(solution)/shard_map/all_to_all | solution.py:60
  156.4 16.6 %fusion.26 = bf16[4,480,512]{2,1,0:T(8,128)(2,1)} fusion(bf16[4,2048,512]{2,1,0:T(8,128)(2,1)} %param.18, bf16[4,480,2048]{2,0,1:T(4,128)(2,1)S(1)} %bitcast.46), kind=kOutput, calls=%fused_computation.42 | convolution fusion | flops 4027514880 | bytes 18219008 | tf_op jit(solution)/shard_map/erd,edf->erf/dot_general | solution.py:62
  173.0 13.7 %fusion.23 = bf16[4,480,512]{2,1,0:T(8,128)(2,1)} fusion(bf16[4,2048,512]{2,1,0:T(8,128)(2,1)} %param.19, bf16[4,480,2048]{2,0,1:T(4,128)(2,1)S(1)} %bitcast.47), kind=kOutput, calls=%fused_computation.41 | convolution fusion | flops 4027514880 | bytes 18219008 | tf_op jit(solution)/shard_map/erd,edf->erf/dot_general | solution.py:63
  186.8 54.1 %all-to-all-done = bf16[32,60,2048]{2,1,0:T(8,128)(2,1)} async-done(((bf16[32,60,2048]{2,1,0:T(8,128)(2,1)}), bf16[32,60,2048]{2,1,0:T(8,128)(2,1)}, u32[]{:S(2)}, u32[]{:S(2)}) %all-to-all-start) | async-done | bytes 7864352 | tf_op jit(solution)/shard_map/all_to_all | solution.py:61
  240.9 11.6 %copy.57 = bf16[8,4,60,2048]{3,1,2,0:T(4,128)(2,1)} copy(bf16[8,4,60,2048]{3,2,1,0:T(8,128)(2,1)} %bitcast) | data formatting | bytes 15728640 | tf_op jit(solution)/shard_map/all_to_all | solution.py:61
  252.5 19.6 %fusion.14 = (bf16[4,480,512]{2,1,0:T(8,128)(2,1)}, f32[4,480,512]{2,1,0:T(8,128)}) fusion(bf16[4,480,512]{2,1,0:T(8,128)(2,1)} %fusion.23, bf16[4,480,512]{2,1,0:T(8,128)(2,1)} %fusion.26, bf16[4,512,2048]{2,1,0:T(8,128)(2,1)} %param.20, bf16[4,480,2048]{2,0,1:T(4,128)(2,1)} %bitcast.50), kind=kOutput, calls=%fused_computation.28 | convolution fusion | flops 4038328320 | bytes 26083328 | tf_op jit(solution)/shard_map/erd,efd->erf/dot_general | solution.py:64
  272.1 14.5 %fusion.41 = f32[4,480,2048]{2,1,0:T(8,128)} fusion(bf16[4,480,512]{2,1,0:T(8,128)(2,1)} %get-tuple-element.35, bf16[4,2048,512]{2,1,0:T(8,128)(2,1)} %param.18), kind=kOutput, calls=%fused_computation.69 | convolution fusion | flops 4026531840 | bytes 26083328 | tf_op jit(solution)/shard_map/erf,edf->erd/dot_general | solution.py:69
  286.7 14.1 %add_convert_fusion = bf16[4,480,2048]{2,1,0:T(8,128)(2,1)} fusion(f32[4,480,2048]{2,1,0:T(8,128)} %fusion.41, bf16[4,2048,512]{2,1,0:T(8,128)(2,1)} %param.19, f32[4,480,512]{2,1,0:T(8,128)} %get-tuple-element.36, bf16[4,480,512]{2,1,0:T(8,128)(2,1)} %fusion.26), kind=kOutput, calls=%fused_computation.6 | convolution fusion | flops 4041277440 | bytes 37879808 | tf_op jit(solution)/shard_map/erf,edf->erd/dot_general | solution.py:69
  300.7 12.5 %copy.49 = bf16[4,480,2048]{2,0,1:T(4,128)(2,1)} copy(bf16[4,480,2048]{2,1,0:T(8,128)(2,1)} %add_convert_fusion) | data formatting | bytes 15728640 | tf_op jit(solution)/shard_map/convert_element_type | solution.py:69
  313.2 5.0 %all-to-all-start.2 = ((bf16[4,480,2048]{2,0,1:T(4,128)(2,1)}), bf16[4,480,2048]{2,0,1:T(4,128)(2,1)}, u32[]{:S(2)}, u32[]{:S(2)}) async-start(bf16[4,480,2048]{2,0,1:T(4,128)(2,1)} %copy.49), calls=%async_computation.2 | async-start | bytes 15728640 | tf_op jit(solution)/shard_map/all_to_all | solution.py:70
  326.1 5.3 %copy.54 = f32[1,2048,512]{2,1,0:T(8,128)} copy(f32[1,2048,512]{1,2,0:T(8,128)} %convolution_bitcast_fusion.2) | data formatting | bytes 8388608
  334.2 5.4 %copy.55 = f32[1,2048,512]{2,1,0:T(8,128)} copy(f32[1,2048,512]{1,2,0:T(8,128)} %convolution_bitcast_fusion.1) | data formatting | bytes 8388608
  339.6 2.8 convolution_bitcast_fusion
  344.2 31.5 %fusion.6 = f32[4,2048,512]{2,1,0:T(8,128)} fusion(bf16[4,480,512]{2,1,0:T(8,128)(2,1)S(1)} %copy-done.5, bf16[4,480,2048]{2,0,1:T(4,128)(2,1)} %bitcast.48), kind=kOutput, calls=%fused_computation.18 | convolution fusion | flops 4026531840 | bytes 26607616 | tf_op jit(solution)/shard_map/erd,erf->edf/dot_general | solution.py:66
  375.7 21.6 %fusion = f32[4,512,2048]{2,1,0:T(8,128)} fusion(bf16[4,480,2048]{2,0,1:T(4,128)(2,1)} %bitcast.51, bf16[4,480,512]{2,1,0:T(8,128)(2,1)} %fusion.23, bf16[4,480,512]{2,1,0:T(8,128)(2,1)} %fusion.26), kind=kOutput, calls=%fused_computation.9 | convolution fusion | flops 4034396160 | bytes 28573696 | tf_op jit(solution)/shard_map/erf,erd->efd/dot_general | solution.py:68
  397.3 26.0 %fusion.4 = f32[4,2048,512]{2,1,0:T(8,128)} fusion(bf16[4,480,2048]{2,0,1:T(4,128)(2,1)} %bitcast.49, f32[4,480,512]{2,1,0:T(8,128)} %get-tuple-element.36, bf16[4,480,512]{2,1,0:T(8,128)(2,1)} %fusion.26), kind=kOutput, calls=%fused_computation.16 | convolution fusion | flops 4033413120 | bytes 30539776 | tf_op jit(solution)/shard_map/erd,erf->edf/dot_general | solution.py:67
  423.3 11.3 %copy.50 = bf16[8,4,60,2048]{3,2,1,0:T(8,128)(2,1)} copy(bf16[8,4,60,2048]{3,1,2,0:T(4,128)(2,1)} %bitcast.10) | data formatting | bytes 15728640 | tf_op jit(solution)/shard_map/all_to_all | solution.py:70
  434.6 9.2 %reshape.106 = bf16[1920,2048]{1,0:T(8,128)(2,1)} reshape(bf16[8,4,60,2048]{3,2,1,0:T(8,128)(2,1)} %copy.50) | data formatting | bytes 15728640 | tf_op jit(solution)/shard_map/reshape | solution.py:70
  443.8 15.1 %gather_fusion = bf16[1280,2048]{1,0:T(8,128)(2,1)} fusion(bf16[1920,2048]{1,0:T(8,128)(2,1)} %reshape.106, s32[2048]{0:T(1024)S(1)} %pad_clamp_fusion), kind=kCustom, calls=%fused_computation.2 | custom fusion | bytes 10490880 | tf_op jit(solution)/shard_map/jit(_take)/gather | solution.py:29
  458.9 9.8 %gather.10 = bf16[128,10,2048]{2,1,0:T(8,128)(2,1)} reshape(bf16[1280,2048]{1,0:T(8,128)(2,1)} %gather_fusion) | data formatting | bytes 10485760 | tf_op jit(solution)/shard_map/jit(_take)/gather | solution.py:29
  468.6 9.3 %convert_reduce_fusion = f32[128,2048]{1,0:T(8,128)S(1)} fusion(bf16[128,10,2048]{2,1,0:T(8,128)(2,1)} %gather.10, pred[128,10]{1,0:T(8,128)(4,1)S(1)} %copy.39), kind=kLoop, calls=%fused_computation.5 | loop fusion | flops 7602176 | bytes 6292736 | tf_op jit(solution)/shard_map/reduce_sum | solution.py:72
  (49 shorter events, 16.1 us)
Async XLA Ops:
  0.6 317.8 %copy-start = (bf16[2048,512]{1,0:T(8,128)(2,1)S(1)}, bf16[2048,512]{1,0:T(8,128)(2,1)}, u32[]{:S(2)}) copy-start(bf16[2048,512]{1,0:T(8,128)(2,1)} %param.21) | copy-start | bytes 6291460
  41.4 5.6 %copy-start.2 = (bf16[128,2048]{1,0:T(8,128)(2,1)S(1)}, bf16[128,2048]{1,0:T(8,128)(2,1)}, u32[]{:S(2)}) copy-start(bf16[128,2048]{1,0:T(8,128)(2,1)} %param.14) | copy-start | bytes 1572868
  41.4 100.1 %all-to-all-start.1 = ((bf16[32,60,2048]{2,1,0:T(8,128)(2,1)}), bf16[32,60,2048]{2,1,0:T(8,128)(2,1)}, u32[]{:S(2)}, u32[]{:S(2)}) async-start(bf16[32,60,2048]{2,1,0:T(8,128)(2,1)} %reshape.105), calls=%async_computation.1 | async-start | bytes 16777216 | tf_op jit(solution)/shard_map/all_to_all | solution.py:60
  47.0 8.7 %copy-start.12 = (f32[128,10]{0,1:T(8,128)S(1)}, f32[128,10]{0,1:T(8,128)}, u32[]{:S(2)}) copy-start(f32[128,10]{0,1:T(8,128)} %param.16) | copy-start | bytes 15364
  141.5 99.4 %all-to-all-start = ((bf16[32,60,2048]{2,1,0:T(8,128)(2,1)}), bf16[32,60,2048]{2,1,0:T(8,128)(2,1)}, u32[]{:S(2)}, u32[]{:S(2)}) async-start(bf16[32,60,2048]{2,1,0:T(8,128)(2,1)} %reshape.104), calls=%async_computation | async-start | bytes 16777216 | tf_op jit(solution)/shard_map/all_to_all | solution.py:61
  156.4 16.6 %copy-start.3 = (bf16[8,4,60,2048]{3,1,2,0:T(4,128)(2,1)}, bf16[8,4,60,2048]{3,1,2,0:T(4,128)(2,1)S(1)}, u32[]{:S(2)}) copy-start(bf16[8,4,60,2048]{3,1,2,0:T(4,128)(2,1)S(1)} %copy.59) | copy-start | bytes 23592964
  313.2 5.2 %copy-start.1 = (bf16[128,2048]{1,0:T(8,128)(2,1)S(1)}, bf16[128,2048]{1,0:T(8,128)(2,1)}, u32[]{:S(2)}) copy-start(bf16[128,2048]{1,0:T(8,128)(2,1)} %param.13) | copy-start | bytes 1572868
  313.2 110.1 %all-to-all-start.2 = ((bf16[4,480,2048]{2,0,1:T(4,128)(2,1)}), bf16[4,480,2048]{2,0,1:T(4,128)(2,1)}, u32[]{:S(2)}, u32[]{:S(2)}) async-start(bf16[4,480,2048]{2,0,1:T(4,128)(2,1)} %copy.49), calls=%async_computation.2 | async-start | bytes 15728640 | tf_op jit(solution)/shard_map/all_to_all | solution.py:70
  318.4 3.4 copy-start.13
  321.1 0.7 copy-start.7
  322.7 0.7 copy-start.9
  334.2 5.4 %copy-start.11 = (s32[1280]{0:T(1024)S(1)}, s32[1280]{0:T(1024)}, u32[]{:S(2)}) copy-start(s32[1280]{0:T(1024)} %get-tuple-element.29) | copy-start | bytes 15364
  334.2 5.4 %copy-start.8 = (f32[128,512]{1,0:T(8,128)S(1)}, f32[128,512]{1,0:T(8,128)}, u32[]{:S(2)}) copy-start(f32[128,512]{1,0:T(8,128)} %copy-done.7) | copy-start | bytes 786436
  339.6 2.8 copy-start.10
  339.6 4.6 copy-start.5
  468.6 9.3 %copy-start.4 = (bf16[2048,512]{1,0:T(8,128)(2,1)S(1)}, bf16[2048,512]{1,0:T(8,128)(2,1)}, u32[]{:S(2)}) copy-start(bf16[2048,512]{1,0:T(8,128)(2,1)} %param.22) | copy-start | bytes 6291460
  468.6 9.3 %copy-start.6 = (f32[128,2048]{1,0:T(8,128)S(1)}, f32[128,2048]{1,0:T(8,128)}, u32[]{:S(2)}) copy-start(f32[128,2048]{1,0:T(8,128)} %fusion.42) | copy-start | bytes 3145732
where the time goes:
time: 487 us; the launch traced here: 480 us
  matrix products  173 us (36%)
  local copies, waits for them, and re-layouts  147 us (30%)
  waiting for transfers between devices  118 us (24%)
  other arithmetic  25.5 us (5%)
  starting transfers between devices  16 us (3%)
    all_to_all x1, waiting for transfers between devices, local_backward(): x_exp = lax.all_to_all(send_x, 'ep', 0, 1, tiled=True)  63.6 us
    all_to_all x1, waiting for transfers between devices, local_backward(): dz_exp = lax.all_to_all(send_dz, 'ep', 0, 1, tiled=True)  54.1 us
    gather x4, local copies, waits for them, and re-layouts, take_rows(): return jnp.take(rows, row_index, axis=0, mode='fill', fill_value=0)  50.9 us
    dot_general x1, matrix products, local_backward(): jnp.einsum('erd,erf->edf', x_exp, grad_gate, preferred_element_type=jnp.f...  31.5 us
    dot_general x1, matrix products, local_backward(): jnp.einsum('erd,erf->edf', x_exp, grad_up, preferred_element_type=jnp.flo...  26 us
    dot_general x1, matrix products, local_backward(): jnp.einsum('erf,erd->efd', hidden, dz_exp, preferred_element_type=jnp.flo...  21.6 us
    dot_general x1, matrix products, local_backward(): jnp.einsum('erd,efd->erf', dz_exp, w_down, preferred_element_type=jnp.flo...  19.6 us
    dot_general x1, matrix products, local_backward(): jnp.einsum('erd,edf->erf', x_exp, w_gate, preferred_element_type=jnp.floa...  16.6 us
  transfers between devices with their start and end apart: 3, of which 2 were waited for; matrix products, arithmetic and copies ran while one was open for 36% of the time, Pallas kernels for 0%

commit v1 on v0

v1 whole, which is shorter than its diff:
```python
import jax
import jax.numpy as jnp
from jax import lax
from jax.experimental import pallas as pl
from jax.experimental.pallas import tpu as pltpu
from jax.sharding import PartitionSpec as P

MESH = pl.DeviceIdType.MESH
SLOT = 64
BF16 = jnp.bfloat16
F32 = jnp.float32


def swiglu_parts(act_gate, act_up, grad_hidden):
    gate_f32 = act_gate.astype(F32)
    up_f32 = act_up.astype(F32)
    sigma = jax.nn.sigmoid(gate_f32)
    silu_gate = gate_f32 * sigma
    hidden = (silu_gate * up_f32).astype(BF16)
    grad_gate = (grad_hidden * up_f32 * sigma * (1.0 + gate_f32 * (1.0 - sigma))).astype(BF16)
    grad_up = (grad_hidden * silu_gate).astype(BF16)
    return hidden, grad_gate, grad_up


def shared_backward(x_tokens, dy_tokens, shared_gate, shared_up, shared_down):
    act_gate = jnp.dot(x_tokens, shared_gate, preferred_element_type=F32).astype(BF16)
    act_up = jnp.dot(x_tokens, shared_up, preferred_element_type=F32).astype(BF16)
    grad_hidden = jnp.einsum('td,fd->tf', dy_tokens, shared_down, preferred_element_type=F32)
    hidden, grad_gate, grad_up = swiglu_parts(act_gate, act_up, grad_hidden)
    grad_gate_w = jnp.einsum('td,tf->df', x_tokens, grad_gate, preferred_element_type=F32)
    grad_up_w = jnp.einsum('td,tf->df', x_tokens, grad_up, preferred_element_type=F32)
    grad_down_w = jnp.einsum('tf,td->fd', hidden, dy_tokens, preferred_element_type=F32)
    grad_input = jnp.einsum('tf,df->td', grad_gate, shared_gate, preferred_element_type=F32) + jnp.einsum('tf,df->td', grad_up, shared_up, preferred_element_type=F32)
    return grad_input, grad_gate_w, grad_up_w, grad_down_w


def dot_nn(a, b):
    return lax.dot_general(a, b, (((1,), (0,)), ((), ())), preferred_element_type=F32)


def dot_nt(a, b):
    return lax.dot_general(a, b, (((1,), (1,)), ((), ())), preferred_element_type=F32)


def dot_tn(a, b):
    return lax.dot_general(a, b, (((0,), (0,)), ((), ())), preferred_element_type=F32)


def places():
    me = lax.axis_index('ep')
    core = lax.rem(me, 2)
    flip_x = 2 - 4 * lax.rem(me // 2, 2)
    flip_y = 4 - 8 * (me // 4)
    first = me + flip_x * (1 - core) + flip_y * core
    second = me + flip_y * (1 - core) + flip_x * core
    diag = me + flip_x + flip_y
    partner = me + 1 - 2 * core
    return me, core, first, second, diag, partner


def remote(src, dst, send_sem, recv_sem, device):
    return pltpu.make_async_remote_copy(src_ref=src, dst_ref=dst, send_sem=send_sem, recv_sem=recv_sem, device_id={'ep': device}, device_id_type=MESH)


def gather_kernel(x_ref, dy_ref, code_ref, gate_ref, xg_ref, dyg_ref, codeg_ref, gateg_ref, xbuf, dybuf, send_sem, recv_sem, meta_send, meta_recv, out_sem):
    me, core, first, second, diag, partner = places()
    barrier = pltpu.get_barrier_semaphore()
    for step in range(1, 8):
        pl.semaphore_signal(barrier, inc=1, device_id={'ep': lax.rem(me + step, 8)}, device_id_type=MESH)
    pl.semaphore_wait(barrier, 7)

    meta = []
    for step in range(1, 8):
        peer = lax.rem(me + step, 8)
        for which, (src, dst) in enumerate(((code_ref, codeg_ref), (gate_ref, gateg_ref))):
            copy = remote(src, dst.at[me], meta_send.at[which, step - 1], meta_recv.at[which, step - 1], peer)
            copy.start()
            meta.append(copy)
    codeg_ref[me] = code_ref[...]
    gateg_ref[me] = gate_ref[...]

    def own(array, src, buf):
        to_first = remote(src, buf.at[me], send_sem.at[array, 0], recv_sem.at[array, 0], first)
        to_second = remote(src, buf.at[me], send_sem.at[array, 1], recv_sem.at[array, 1], second)
        to_partner = remote(src, buf.at[me], send_sem.at[array, 2], recv_sem.at[array, 2], partner)
        to_first.start()
        to_second.start()
        to_partner.start()
        return [to_first, to_second, to_partner]

    def forward(array, buf, block, slot, device):
        copy = remote(buf.at[block], buf.at[block], send_sem.at[array, slot], recv_sem.at[array, slot], device)
        copy.start()
        return copy

    arrays = ((x_ref, xbuf, xg_ref), (dy_ref, dybuf, dyg_ref))
    sent = []
    outs = []
    sent.append(own(0, x_ref, xbuf))
    for array, (src, buf, out) in enumerate(arrays):
        copies = sent[array]
        copies[0].wait_recv()
        copies.append(forward(array, buf, first, 3, second))
        copies.append(forward(array, buf, first, 4, partner))
        if array == 0:
            sent.append(own(1, dy_ref, dybuf))
        copies[1].wait_recv()
        copies.append(forward(array, buf, second, 5, partner))
        copies[3].wait_recv()
        copies.append(forward(array, buf, diag, 6, partner))
        for index in (2, 4, 5, 6):
            copies[index].wait_recv()
        mine = pltpu.make_async_copy(src, out.at[me], out_sem.at[array, 0])
        mine.start()
        outs.append(mine)
        for step in range(1, 8):
            block = lax.rem(me + step, 8)
            copy = pltpu.make_async_copy(buf.at[block], out.at[block], out_sem.at[array, step])
            copy.start()
            outs.append(copy)
    for copies in sent:
        for copy in copies:
            copy.wait_send()
    for copy in meta:
        copy.wait()
    for copy in outs:
        copy.wait()


def gather_tokens(x_tokens, dy_tokens, code, gate):
    tokens, width = x_tokens.shape
    vmem = pl.BlockSpec(memory_space=pltpu.VMEM)
    hbm = pl.BlockSpec(memory_space=pl.ANY)
    return pl.pallas_call(
        gather_kernel,
        out_shape=(
            jax.ShapeDtypeStruct((8, tokens, width), BF16),
            jax.ShapeDtypeStruct((8, tokens, width), BF16),
            jax.ShapeDtypeStruct((8,) + code.shape, jnp.int32),
            jax.ShapeDtypeStruct((8,) + gate.shape, F32),
        ),
        in_specs=[vmem] * 4,
        out_specs=(hbm, hbm, vmem, vmem),
        scratch_shapes=[
            pltpu.VMEM((8, tokens, width), BF16),
            pltpu.VMEM((8, tokens, width), BF16),
            pltpu.SemaphoreType.DMA((2, 7)),
            pltpu.SemaphoreType.DMA((2, 7)),
            pltpu.SemaphoreType.DMA((2, 7)),
            pltpu.SemaphoreType.DMA((2, 7)),
            pltpu.SemaphoreType.DMA((2, 8)),
        ],
        compiler_params=pltpu.CompilerParams(collective_id=0, has_side_effects=True),
        name='gather_tokens',
    )(x_tokens, dy_tokens, code, gate)


TILES = 4


def expert_kernel(xg_ref, dyg_ref, code_ref, gate_ref, w1_ref, w3_ref, w2_ref, dw1_ref, dw3_ref, dw2_ref, part_ref, x_rows, z_rows, hidden_t, grad_gate, grad_up, onehot_t, acc, out_sem):
    expert = pl.program_id(0)
    tile = pl.program_id(1)
    local = lax.axis_index('ep') * 4 + expert

    @pl.when(tile == 0)
    def _():
        def pick(source, carry):
            slot = lax.broadcasted_iota(jnp.int32, (SLOT, 128), 0) + local * SLOT
            onehot = jnp.zeros((SLOT, 128), F32)
            gates = jnp.zeros((SLOT, 128), F32)
            for choice in range(10):
                hit = slot == code_ref[source, choice:choice + 1, :]
                onehot = jnp.where(hit, 1.0, onehot)
                gates = jnp.where(hit, gate_ref[source, choice:choice + 1, :], gates)
            gate_row = jnp.sum(gates, axis=1, keepdims=True)
            select = onehot.astype(BF16)
            onehot_t[source] = onehot.T.astype(BF16)
            rows = pl.ds(pl.multiple_of(source * SLOT, SLOT), SLOT)
            x_rows[rows, :] = dot_nn(select, xg_ref[source]).astype(BF16)
            z_rows[rows, :] = (dot_nn(select, dyg_ref[source]) * gate_row).astype(BF16)
            return carry

        lax.fori_loop(0, 8, pick, 0)
        act_gate = dot_nn(x_rows[...], w1_ref[0]).astype(BF16)
        act_up = dot_nn(x_rows[...], w3_ref[0]).astype(BF16)
        grad_hidden = dot_nt(z_rows[...], w2_ref[0])
        hidden, d_gate, d_up = swiglu_parts(act_gate, act_up, grad_hidden)
        hidden_t[...] = hidden.T
        grad_gate[...] = d_gate
        grad_up[...] = d_up

    cols = pl.ds(pl.multiple_of(tile * 512, 512), 512)
    rows_out = (dot_nt(grad_gate[...], w1_ref[0, cols, :]) + dot_nt(grad_up[...], w3_ref[0, cols, :])).astype(BF16)
    for source in range(8):
        term = dot_nn(onehot_t[source], rows_out[source * SLOT:(source + 1) * SLOT, :])

        @pl.when(expert == 0)
        def _():
            acc[tile, source] = term

        @pl.when(expert > 0)
        def _():
            acc[tile, source] += term

    x_cols_t = x_rows[:, cols].T
    dw1_ref[0] = dot_nn(x_cols_t, grad_gate[...])
    dw3_ref[0] = dot_nn(x_cols_t, grad_up[...])
    dw2_ref[0] = dot_nn(hidden_t[...], z_rows[:, cols])

    @pl.when(expert == 3)
    def _():
        pltpu.make_async_copy(acc.at[tile], part_ref.at[tile], out_sem.at[tile]).start()

    @pl.when(jnp.logical_and(expert == 3, tile == TILES - 1))
    def _():
        for index in range(TILES):
            pltpu.make_async_copy(acc.at[index], part_ref.at[index], out_sem.at[index]).wait()


def expert_backward(xg, dyg, code, gate, w_gate, w_up, w_down):
    experts, width, inner = w_gate.shape
    tokens = xg.shape[1]
    vmem = pl.BlockSpec(memory_space=pltpu.VMEM)
    whole = lambda e, t: (e, 0, 0)
    return pl.pallas_call(
        expert_kernel,
        grid=(experts, TILES),
        out_shape=(
            jax.ShapeDtypeStruct((experts, width, inner), F32),
            jax.ShapeDtypeStruct((experts, width, inner), F32),
            jax.ShapeDtypeStruct((experts, inner, width), F32),
            jax.ShapeDtypeStruct((TILES, 8, tokens, width // TILES), F32),
        ),
        in_specs=[
            pl.BlockSpec((8, tokens, width), lambda e, t: (0, 0, 0), pipeline_mode=pl.Buffered(1)),
            pl.BlockSpec((8, tokens, width), lambda e, t: (0, 0, 0), pipeline_mode=pl.Buffered(1)),
            vmem,
            vmem,
            pl.BlockSpec((1, width, inner), whole),
            pl.BlockSpec((1, width, inner), whole),
            pl.BlockSpec((1, inner, width), whole),
        ],
        out_specs=(
            pl.BlockSpec((1, width // TILES, inner), lambda e, t: (e, t, 0)),
            pl.BlockSpec((1, width // TILES, inner), lambda e, t: (e, t, 0)),
            pl.BlockSpec((1, inner, width // TILES), lambda e, t: (e, 0, t)),
            pl.BlockSpec(memory_space=pl.ANY),
        ),
        scratch_shapes=[
            pltpu.VMEM((8 * SLOT, width), BF16),
            pltpu.VMEM((8 * SLOT, width), BF16),
            pltpu.VMEM((inner, 8 * SLOT), BF16),
            pltpu.VMEM((8 * SLOT, inner), BF16),
            pltpu.VMEM((8 * SLOT, inner), BF16),
            pltpu.VMEM((8, tokens, SLOT), BF16),
            pltpu.VMEM((TILES, 8, tokens, width // TILES), F32),
            pltpu.SemaphoreType.DMA((TILES,)),
        ],
        compiler_params=pltpu.CompilerParams(dimension_semantics=('arbitrary', 'arbitrary'), vmem_limit_bytes=66000000),
        cost_estimate=pl.CostEstimate(flops=40_000_000_000, bytes_accessed=90_000_000, transcendentals=1_000_000),
        name='expert_backward',
    )(xg, dyg, code, gate, w_gate, w_up, w_down)


def scatter_kernel(part_ref, shared_ref, out_ref, mine, pair, got_first, got_second, got_last, load_sem, pair_send, pair_recv, first_send, first_recv, second_send, second_recv, last_send, last_recv):
    me, core, first, second, diag, partner = places()
    chip, first_chip, second_chip, diag_chip = me // 2, first // 2, second // 2, diag // 2
    barrier = pltpu.get_barrier_semaphore()
    for device in (partner, first, second):
        pl.semaphore_signal(barrier, inc=1, device_id={'ep': device}, device_id_type=MESH)
    pl.semaphore_wait(barrier, 3)

    other = 1 - core
    loads, pairs = {}, {}
    for index, (give, take) in enumerate(((diag_chip, diag_chip), (second_chip, first_chip), (first_chip, second_chip), (chip, chip))):
        for half in range(2):
            copy = remote(part_ref.at[other * 2 + half, give], pair.at[half, give], pair_send.at[index, half], pair_recv.at[index, half], partner)
            copy.start()
            pairs[index, half] = copy
            copy = pltpu.make_async_copy(part_ref.at[core * 2 + half, take], mine.at[half, take], load_sem.at[index, half])
            copy.start()
            loads[index, half] = copy

    def both(index, half, block):
        loads[index, half].wait()
        pairs[index, half].wait_recv()
        return mine[half, block] + pair[half, block]

    firsts, seconds = {}, {}
    for index, block in ((0, diag_chip), (1, first_chip)):
        for half in range(2):
            mine[half, block] = both(index, half, block)
            copy = remote(mine.at[half, block], got_first.at[index, half], first_send.at[index, half], first_recv.at[index, half], first)
            copy.start()
            firsts[index, half] = copy
    for half in range(2):
        value = both(2, half, second_chip)
        firsts[0, half].wait_recv()
        mine[half, second_chip] = value + got_first[0, half]
        copy = remote(mine.at[half, second_chip], got_second.at[half], second_send.at[half], second_recv.at[half], second)
        copy.start()
        seconds[half] = copy
    lasts = {}
    for half in range(2):
        value = both(3, half, chip)
        firsts[1, half].wait_recv()
        mine[half, chip] = value + got_first[1, half]
    for half in range(2):
        seconds[half].wait_recv()
        mine[half, chip] += got_second[half]
        copy = remote(mine.at[half, chip, other], got_last.at[half], last_send.at[half], last_recv.at[half], partner)
        copy.start()
        lasts[half] = copy
    for half in range(2):
        cols = pl.ds(pl.multiple_of(core * 1024 + half * 512, 512), 512)
        out_ref[:, cols] = (mine[half, chip, core] + shared_ref[:, cols]).astype(BF16)
    for half in range(2):
        lasts[half].wait_recv()
        cols = pl.ds(pl.multiple_of(other * 1024 + half * 512, 512), 512)
        out_ref[:, cols] = (got_last[half] + shared_ref[:, cols]).astype(BF16)
    for group in (pairs, firsts, seconds, lasts):
        for copy in group.values():
            copy.wait_send()


def scatter_sum(part, shared_dx):
    tokens, width = shared_dx.shape
    vmem = pl.BlockSpec(memory_space=pltpu.VMEM)
    piece = (2, tokens, width // TILES)
    part = part.reshape((TILES, 4) + piece)
    dma = pltpu.SemaphoreType.DMA
    return pl.pallas_call(
        scatter_kernel,
        out_shape=jax.ShapeDtypeStruct((tokens, width), BF16),
        in_specs=[pl.BlockSpec(memory_space=pl.ANY), vmem],
        out_specs=vmem,
        scratch_shapes=[
            pltpu.VMEM((2, 4) + piece, F32),
            pltpu.VMEM((2, 4) + piece, F32),
            pltpu.VMEM((2, 2) + piece, F32),
            pltpu.VMEM((2,) + piece, F32),
            pltpu.VMEM((2, tokens, width // TILES), F32),
            dma((4, 2)),
            dma((4, 2)),
            dma((4, 2)),
            dma((2, 2)),
            dma((2, 2)),
            dma((2,)),
            dma((2,)),
            dma((2,)),
            dma((2,)),
        ],
        compiler_params=pltpu.CompilerParams(collective_id=1, has_side_effects=True),
        name='scatter_sum',
    )(part, shared_dx)


def solution(mesh):
    token_spec = P(('dp', 'ep'), None)
    expert_spec = P('ep', None, None)
    whole_spec = P(None, None)
    grad_spec = P(('dp', 'ep'), None, None)

    def local_backward(x_tokens, dy_tokens, expert_ids, gate_vals, slot_pos, w_gate, w_up, w_down, shared_gate, shared_up, shared_down):
        code = jnp.where(slot_pos >= 0, expert_ids * SLOT + slot_pos, -1)
        code = jnp.pad(code.T, ((0, 6), (0, 0)), constant_values=-1)
        gate = jnp.pad(gate_vals.T, ((0, 6), (0, 0)))
        xg, dyg, codes, gates = gather_tokens(x_tokens, dy_tokens, code, gate)
        grad_w_gate, grad_w_up, grad_w_down, part = expert_backward(xg, dyg, codes, gates, w_gate, w_up, w_down)
        shared_dx, grad_shared_gate, grad_shared_up, grad_shared_down = shared_backward(x_tokens, dy_tokens, shared_gate, shared_up, shared_down)
        grad_x = scatter_sum(part, shared_dx)
        return grad_x, grad_w_gate, grad_w_up, grad_w_down, grad_shared_gate[None], grad_shared_up[None], grad_shared_down[None]

    return jax.shard_map(local_backward, mesh=mesh, in_specs=(token_spec, token_spec, token_spec, token_spec, token_spec, expert_spec, expert_spec, expert_spec, whole_spec, whole_spec, whole_spec), out_specs=(token_spec, grad_spec, grad_spec, grad_spec, grad_spec, grad_spec, grad_spec), check_vma=False)
```

time: 487 us -> 208 us (0.43); the launches traced: 480 us -> 208 us
  Pallas kernels: 0 us -> 176 us
  matrix products: 173 us -> 14.4 us
  local copies, waits for them, and re-layouts: 147 us -> 15.4 us
  waiting for transfers between devices: 118 us -> 0 us
  other arithmetic: 25.5 us -> 0.72 us
  starting transfers between devices: 16 us -> 0 us
    pallas_call x0 -> x3, Pallas kernels: none -> 176 us  [the longest x1 84.7 us: expert_backward(): pl.pallas_call(expert_kernel, grid=(experts, TILES), out_shape=(jax.Shape...]
    dot_general x16 -> x8, matrix products: 173 us -> 14.4 us  [the longest x1 2.76 us: shared_backward(): jnp.einsum('tf,td->fd', hidden, dy_tokens, preferred_element_type=F32)]
    all_to_all x3 -> x0, waiting for transfers between devices: 118 us -> none  [the longest x1 63.6 us: local_backward(): x_exp = lax.all_to_all(send_x, 'ep', 0, 1, tiled=True)]
    gather x4 -> x0, local copies, waits for them, and re-layouts: 50.9 us -> none  [take_rows(): return jnp.take(rows, row_index, axis=0, mode='fill', fill_value=0)]
    all_to_all x3 -> x0, local copies, waits for them, and re-layouts: 32.4 us -> none  [the longest x1 11.6 us: local_backward(): dz_exp = lax.all_to_all(send_dz, 'ep', 0, 1, tiled=True)]
    reshape x6 -> x0, local copies, waits for them, and re-layouts: 27.8 us -> none  [the longest x1 9.18 us: local_backward(): lax.all_to_all(grad_exp, 'ep', 1, 0, tiled=True)]
    all_to_all x3 -> x0, starting transfers between devices: 16 us -> none  [the longest x1 5.59 us: local_backward(): x_exp = lax.all_to_all(send_x, 'ep', 0, 1, tiled=True)]
    convert_element_type x1 -> x0, local copies, waits for them, and re-layouts: 12.5 us -> none  [local_backward(): (jnp.einsum('erf,edf->erd', grad_gate, w_gate, preferred_element_type=jnp...]
  transfers between devices with their start and end apart: 3 -> 0, of which waited for: 2 -> 0; matrix products, arithmetic and copies ran while one was open for 36% -> 0% of each run, Pallas kernels for 0% -> 0%
where the time goes in v1:
time: 208 us
  Pallas kernels  176 us (85%)
  local copies, waits for them, and re-layouts  15.4 us (7%)
  matrix products  14.4 us (7%)
    pallas_call x1, Pallas kernels, expert_backward(): pl.pallas_call(expert_kernel, grid=(experts, TILES), out_shape=(jax.Shape...  84.7 us
    pallas_call x1, Pallas kernels, gather_tokens(): pl.pallas_call(gather_kernel, out_shape=(jax.ShapeDtypeStruct((8, tokens,...  47.6 us
    pallas_call x1, Pallas kernels, scatter_sum(): pl.pallas_call(scatter_kernel, out_shape=jax.ShapeDtypeStruct((tokens, wi...  44.2 us
    unnamed x15, local copies, waits for them, and re-layouts  13.5 us

profile of v1, /device:TPU:0, one launch (start us, length us, event | category | flops | bytes accessed | tf_op | source)
XLA Modules:
  0.0 207.7 jit_solution(4109184928996861662)
XLA Ops:
  0.6 0.7 select_bitcast_fusion
  1.4 0.6 pad.8.code_ref
  2.0 1.3 pad.9.gate_ref
  3.3 47.6 %gather_tokens.1 = (bf16[8,128,2048]{2,1,0:T(8,128)(2,1)}, bf16[8,128,2048]{2,1,0:T(8,128)(2,1)}, s32[8,16,128]{2,1,0:T(8,128)}, f32[8,16,128]{2,1,0:T(8,128)}) custom-call(bf16[128,2048]{1,0:T(8,128)(2,1)} %x_ref.1, bf16[128,2048]{1,0:T(8,128)(2,1)} %dy_ref.1, s32[16,128]{1,0:T(8,128)} %pad.8.code_ref, f32[16,128]{1,0:T(8,128)} %pad.9.gate_ref), custom_call_target="tpu_custom_call" | custom-call | tf_op jit(solution)/shard_map/gather_tokens/pallas_call | solution.py:134
  50.8 0.0 copy-start
  50.9 84.7 %expert_backward.1 = (f32[4,2048,512]{2,1,0:T(8,128)}, f32[4,2048,512]{2,1,0:T(8,128)}, f32[4,512,2048]{2,1,0:T(8,128)}, f32[4,8,128,512]{3,2,1,0:T(8,128)}) custom-call(bf16[8,128,2048]{2,1,0:T(8,128)(2,1)} %get-tuple-element.15.xg_ref, bf16[8,128,2048]{2,1,0:T(8,128)(2,1)} %get-tuple-element.16.dyg_ref, s32[8,16,128]{2,1,0:T(8,128)} %get-tuple-element.17.code_ref, ...), custom_call_target="tpu_custom_call" | custom-call | flops 40000000000 | bytes 90000000 | tf_op jit(solution)/shard_map/expert_backward/pallas_call | solution.py:226
  135.6 0.0 copy-start.2
  135.6 0.0 copy-done
  135.6 2.2 %fusion = f32[128,512]{1,0:T(8,128)S(1)} fusion(bf16[128,2048]{1,0:T(8,128)(2,1)S(1)} %copy-done, bf16[2048,512]{1,0:T(8,128)(2,1)} %param.19), kind=kOutput, calls=%fused_computation.5 | convolution fusion | flops 268566528 | bytes 2883584 | tf_op jit(solution)/shard_map/dot_general | solution.py:26
  137.8 0.0 copy-done.2
  137.8 0.0 copy-start.3
  137.8 0.0 copy-start.5
  137.8 0.5 fusion.1
  138.3 0.5 copy-done.3
  138.8 0.7 copy-done.5
  139.6 0.0 copy-start.1
  139.6 0.9 multiply_convert_fusion.1
  140.5 0.7 copy-done.1
  141.2 0.8 fusion.5
  142.0 1.8 convolution_add_fusion.shared_ref
  143.8 44.2 %scatter_sum.1 = bf16[128,2048]{1,0:T(8,128)(2,1)} custom-call(f32[4,4,2,128,512]{4,3,2,1,0:T(8,128)} %bitcast.29, f32[128,2048]{1,0:T(8,128)} %convolution_add_fusion.shared_ref), custom_call_target="tpu_custom_call" | custom-call | tf_op jit(solution)/shard_map/scatter_sum/pallas_call | solution.py:333
  188.0 2.7 %convolution_bitcast_fusion.2 = f32[1,2048,512]{1,2,0:T(8,128)} fusion(bf16[128,512]{1,0:T(8,128)(2,1)S(1)} %get-tuple-element.31, bf16[128,2048]{1,0:T(8,128)(2,1)S(1)} %copy-done), kind=kOutput, calls=%fused_computation.2 | convolution fusion | flops 268435456 | bytes 4849664 | tf_op jit(solution)/shard_map/td,tf->df/dot_general | solution.py:30
  190.7 5.3 %copy.18 = f32[1,2048,512]{2,1,0:T(8,128)} copy(f32[1,2048,512]{1,2,0:T(8,128)} %convolution_bitcast_fusion.2) | data formatting | bytes 8388608
  196.0 2.7 %convolution_bitcast_fusion.1 = f32[1,2048,512]{1,2,0:T(8,128)} fusion(bf16[128,512]{1,0:T(8,128)(2,1)S(1)} %get-tuple-element.30, bf16[128,2048]{1,0:T(8,128)(2,1)S(1)} %copy-done), kind=kOutput, calls=%fused_computation.1 | convolution fusion | flops 268435456 | bytes 4849664 | tf_op jit(solution)/shard_map/td,tf->df/dot_general | solution.py:31
  198.8 5.3 %copy.19 = f32[1,2048,512]{2,1,0:T(8,128)} copy(f32[1,2048,512]{1,2,0:T(8,128)} %convolution_bitcast_fusion.1) | data formatting | bytes 8388608
  204.1 0.0 copy-start.4
  204.1 2.8 %convolution_bitcast_fusion = f32[1,512,2048]{2,1,0:T(8,128)} fusion(bf16[128,2048]{1,0:T(8,128)(2,1)S(1)} %copy-done.3, f32[128,512]{1,0:T(8,128)S(1)} %fusion.1, f32[128,512]{1,0:T(8,128)S(1)} %fusion), kind=kOutput, calls=%fused_computation | convolution fusion | flops 268828672 | bytes 5242880 | tf_op jit(solution)/shard_map/tf,td->fd/dot_general | solution.py:32
  206.9 0.0 copy-done.4
  206.9 0.8 copy.21
Async XLA Ops:
  50.8 84.7 %copy-start = (bf16[128,2048]{1,0:T(8,128)(2,1)S(1)}, bf16[128,2048]{1,0:T(8,128)(2,1)}, u32[]{:S(2)}) copy-start(bf16[128,2048]{1,0:T(8,128)(2,1)} %x_ref.1) | copy-start | bytes 1572868
  135.6 2.2 %copy-start.2 = (bf16[2048,512]{1,0:T(8,128)(2,1)S(1)}, bf16[2048,512]{1,0:T(8,128)(2,1)}, u32[]{:S(2)}) copy-start(bf16[2048,512]{1,0:T(8,128)(2,1)} %param.20) | copy-start | bytes 6291460
  137.8 1.0 copy-start.3
  137.8 1.8 copy-start.5
  139.6 1.6 copy-start.1
  204.1 2.8 %copy-start.4 = (bf16[128,2048]{1,0:T(8,128)(2,1)S(1)}, bf16[128,2048]{1,0:T(8,128)(2,1)}, u32[]{:S(2)}) copy-start(bf16[128,2048]{1,0:T(8,128)(2,1)} %scatter_sum.1) | copy-start | bytes 1572868

commit v2 on v0

v2 whole, which is shorter than its diff:
```python
import jax
import jax.numpy as jnp
from jax import lax
from jax.experimental import pallas as pl
from jax.experimental.pallas import tpu as pltpu
from jax.sharding import PartitionSpec as P

MESH = pl.DeviceIdType.MESH
SLOT = 64
BF16 = jnp.bfloat16
F32 = jnp.float32


def swiglu_parts(act_gate, act_up, grad_hidden):
    gate_f32 = act_gate.astype(F32)
    up_f32 = act_up.astype(F32)
    sigma = jax.nn.sigmoid(gate_f32)
    silu_gate = gate_f32 * sigma
    hidden = (silu_gate * up_f32).astype(BF16)
    grad_gate = (grad_hidden * up_f32 * sigma * (1.0 + gate_f32 * (1.0 - sigma))).astype(BF16)
    grad_up = (grad_hidden * silu_gate).astype(BF16)
    return hidden, grad_gate, grad_up


def dot_nn(a, b):
    return lax.dot_general(a, b, (((1,), (0,)), ((), ())), preferred_element_type=F32)


def dot_nt(a, b):
    return lax.dot_general(a, b, (((1,), (1,)), ((), ())), preferred_element_type=F32)


def dot_tn(a, b):
    return lax.dot_general(a, b, (((0,), (0,)), ((), ())), preferred_element_type=F32)


def places():
    me = lax.axis_index('ep')
    core = lax.rem(me, 2)
    flip_x = 2 - 4 * lax.rem(me // 2, 2)
    flip_y = 4 - 8 * (me // 4)
    first = me + flip_x * (1 - core) + flip_y * core
    second = me + flip_y * (1 - core) + flip_x * core
    diag = me + flip_x + flip_y
    partner = me + 1 - 2 * core
    return me, core, first, second, diag, partner


def remote(src, dst, send_sem, recv_sem, device):
    return pltpu.make_async_remote_copy(src_ref=src, dst_ref=dst, send_sem=send_sem, recv_sem=recv_sem, device_id={'ep': device}, device_id_type=MESH)


def pair_of(role, step):
    me, core, first, second, diag, partner = places()
    other = 1 - core
    if role == 0:
        return me * (1 - step) + partner * step
    if role == 1:
        return first * (1 - step) + ((second // 2) * 2 + other) * step
    if role == 2:
        return second * (1 - step) + ((first // 2) * 2 + other) * step
    return diag * (1 - step) + ((diag // 2) * 2 + other) * step


def one_hot(code, base, rows):
    slot = lax.broadcasted_iota(jnp.int32, (rows, 128), 0) + base
    hits = jnp.zeros((rows, 128), F32)
    for choice in range(10):
        hits = jnp.where(slot == code[choice:choice + 1, :], 1.0, hits)
    return hits


def gather_kernel(x_ref, dy_ref, code_ref, gate_ref, w1_ref, w3_ref, xr_ref, zr_ref, a_ref, b_ref, codeg_ref, xbuf, dybuf, x_rows, z_rows, w1_buf, w3_buf, a_buf, b_buf, gateg, send_sem, recv_sem, meta_send, meta_recv, load_sem, out_sem, act_sem):
    me, core, first, second, diag, partner = places()
    loads = []
    for expert in range(4):
        for which, (src, dst) in enumerate(((w1_ref, w1_buf), (w3_ref, w3_buf))):
            copy = pltpu.make_async_copy(src.at[expert], dst.at[expert], load_sem.at[which, expert])
            copy.start()
            loads.append(copy)
    barrier = pltpu.get_barrier_semaphore()
    for step in range(1, 8):
        pl.semaphore_signal(barrier, inc=1, device_id={'ep': lax.rem(me + step, 8)}, device_id_type=MESH)
    pl.semaphore_wait(barrier, 7)

    half = 64
    srcs = (x_ref, dy_ref)
    bufs = (xbuf, dybuf)
    copies = {}

    def send(array, part, kind, block, device, own=False):
        rows = pl.ds(part * half, half)
        src = srcs[array].at[rows] if own else bufs[array].at[block, rows]
        copy = remote(src, bufs[array].at[block, rows], send_sem.at[array, part, kind], recv_sem.at[array, part, kind], device)
        copy.start()
        copies[array, part, kind] = copy

    def got(array, part, kind):
        copies[array, part, kind].wait_recv()

    for part in range(2):
        send(0, part, 0, me, first, own=True)
    meta = []
    for step in range(1, 8):
        peer = lax.rem(me + step, 8)
        for which, (src, dst) in enumerate(((code_ref, codeg_ref), (gate_ref, gateg))):
            copy = remote(src, dst.at[me], meta_send.at[which, step - 1], meta_recv.at[which, step - 1], peer)
            copy.start()
            meta.append(copy)
    for array in range(2):
        for part in range(2):
            send(array, part, 2, me, partner, own=True)
    codeg_ref[me] = code_ref[...]
    gateg[me] = gate_ref[...]
    xbuf[me] = x_ref[...]
    dybuf[me] = dy_ref[...]

    outs = []

    def pick(array, role):
        def one(step, carry):
            source = pair_of(role, step)
            hits = one_hot(codeg_ref[source], me * 256, 256)
            select = hits.astype(BF16)
            if array == 1:
                slot = lax.broadcasted_iota(jnp.int32, (256, 128), 0) + me * 256
                gates = jnp.zeros((256, 128), F32)
                for choice in range(10):
                    gates = jnp.where(slot == codeg_ref[source, choice:choice + 1, :], gateg[source, choice:choice + 1, :], gates)
                scale = jnp.sum(gates, axis=1, keepdims=True)
            rows = (x_rows, z_rows)[array]
            for tile in range(4):
                cols = slice(tile * 512, tile * 512 + 512)
                value = dot_nn(select, bufs[array][source, :, cols])
                if array == 1:
                    value = value * scale
                rows[source, :, :, cols] = value.astype(BF16).reshape(4, SLOT, 512)
            return carry

        lax.fori_loop(0, 2, one, 0)
        for step in range(2):
            source = pair_of(role, step)
            copy = pltpu.make_async_copy((x_rows, z_rows)[array].at[source], (xr_ref, zr_ref)[array].at[source], out_sem.at[array, role, step])
            copy.start()
            outs.append(copy)

    def relay_first(array):
        for part in range(2):
            got(array, part, 0)
            send(array, part, 1, me, second, own=True)
            send(array, part, 3, first, second)
            send(array, part, 4, first, partner)

    def relay_rest(array, part):
        got(array, part, 1)
        send(array, part, 5, second, partner)
        got(array, part, 3)
        send(array, part, 6, diag, partner)

    def activations(expert):
        rows = x_rows[:, expert].reshape(8 * SLOT, 2048)
        for which, (w_buf, act, out) in enumerate(((w1_buf, a_buf, a_ref), (w3_buf, b_buf, b_ref))):
            loads[expert * 2 + which].wait()
            act[:, expert] = dot_nn(rows, w_buf[expert]).astype(BF16).reshape(8, SLOT, 512)
            copy = pltpu.make_async_copy(act.at[:, expert], out.at[:, expert], act_sem.at[which, expert])
            copy.start()
            outs.append(copy)

    relay_first(0)
    for copy in meta:
        copy.wait_recv()
    got(0, 0, 2)
    got(0, 1, 2)
    pick(0, 0)
    got(0, 0, 4)
    got(0, 1, 4)
    pick(0, 1)
    for part in range(2):
        relay_rest(0, part)
        send(1, part, 0, me, first, own=True)
    got(1, 0, 2)
    got(1, 1, 2)
    pick(1, 0)
    for part in range(2):
        got(0, part, 5)
        got(0, part, 6)
    pick(0, 2)
    pick(0, 3)
    activations(0)
    relay_first(1)
    activations(1)
    got(1, 0, 4)
    got(1, 1, 4)
    pick(1, 1)
    activations(2)
    relay_rest(1, 0)
    activations(3)
    relay_rest(1, 1)
    for part in range(2):
        got(1, part, 5)
    pick(1, 2)
    for part in range(2):
        got(1, part, 6)
    pick(1, 3)
    for copy in copies.values():
        copy.wait_send()
    for copy in meta:
        copy.wait_send()
    for copy in outs:
        copy.wait()


def gather_rows(x_tokens, dy_tokens, code, gate, w_gate, w_up):
    tokens, width = x_tokens.shape
    experts, _, inner = w_gate.shape
    vmem = pl.BlockSpec(memory_space=pltpu.VMEM)
    hbm = pl.BlockSpec(memory_space=pl.ANY)
    rows = jax.ShapeDtypeStruct((8, experts, SLOT, width), BF16)
    acts = jax.ShapeDtypeStruct((8, experts, SLOT, inner), BF16)
    dma = pltpu.SemaphoreType.DMA
    return pl.pallas_call(
        gather_kernel,
        out_shape=(rows, rows, acts, acts, jax.ShapeDtypeStruct((8,) + code.shape, jnp.int32)),
        in_specs=[vmem] * 4 + [hbm] * 2,
        out_specs=(hbm, hbm, hbm, hbm, vmem),
        scratch_shapes=[
            pltpu.VMEM((8, tokens, width), BF16),
            pltpu.VMEM((8, tokens, width), BF16),
            pltpu.VMEM(rows.shape, BF16),
            pltpu.VMEM(rows.shape, BF16),
            pltpu.VMEM(w_gate.shape, BF16),
            pltpu.VMEM(w_up.shape, BF16),
            pltpu.VMEM(acts.shape, BF16),
            pltpu.VMEM(acts.shape, BF16),
            pltpu.VMEM((8,) + gate.shape, F32),
            dma((2, 2, 7)),
            dma((2, 2, 7)),
            dma((2, 7)),
            dma((2, 7)),
            dma((2, 4)),
            dma((2, 4, 2)),
            dma((2, 4)),
        ],
        compiler_params=pltpu.CompilerParams(collective_id=0, has_side_effects=True, vmem_limit_bytes=64000000),
        name='gather_rows',
    )(x_tokens, dy_tokens, code, gate, w_gate, w_up)


def middle_kernel(z_ref, a_ref, b_ref, code_ref, w1_ref, w3_ref, w2_ref, h_ref, da_ref, db_ref, give_ref, keep_ref, r_mine, r_send, r_got, picks, sums, send_sem, recv_sem, out_sem):
    me, core, first, second, diag, partner = places()
    other = 1 - core
    expert = pl.program_id(0)

    def swap(index):
        return remote(r_send.at[index], r_got.at[index], send_sem.at[index], recv_sem.at[index], partner)

    @pl.when(expert == 0)
    def _():
        barrier = pltpu.get_barrier_semaphore()
        pl.semaphore_signal(barrier, inc=1, device_id={'ep': partner}, device_id_type=MESH)

        def one(source, carry):
            picks[source, :, 0:256] = one_hot(code_ref[source], me * 256, 256).T.astype(BF16)
            picks[source, :, 256:512] = one_hot(code_ref[source], partner * 256, 256).T.astype(BF16)
            return carry

        lax.fori_loop(0, 8, one, 0)
        pl.semaphore_wait(barrier, 1)

    grad_hidden = dot_nt(z_ref[:, 0].reshape(512, 2048), w2_ref[0])
    hidden, d_gate, d_up = swiglu_parts(a_ref[:, 0].reshape(512, 512), b_ref[:, 0].reshape(512, 512), grad_hidden)
    h_ref[:, 0] = hidden.reshape(8, SLOT, 512)
    da_ref[:, 0] = d_gate.reshape(8, SLOT, 512)
    db_ref[:, 0] = d_up.reshape(8, SLOT, 512)

    def rows_back(dst, side):
        for tile in range(2):
            at = pl.ds(pl.multiple_of(side * 1024 + tile * 512, 512), 512)
            value = dot_nt(da_ref[:, 0].reshape(512, 512), w1_ref[0, at, :]) + dot_nt(db_ref[:, 0].reshape(512, 512), w3_ref[0, at, :])
            dst[expert, :, :, tile * 512:(tile + 1) * 512] = value.astype(BF16).reshape(8, SLOT, 512)

    rows_back(r_send, other)
    swap(expert).start()
    rows_back(r_mine, core)

    @pl.when(expert == 3)
    def _():
        for index in range(4):
            swap(index).wait_recv()
        outs = []
        for index, chip in enumerate((diag // 2, first // 2, second // 2, me // 2)):
            for which in range(2):
                source = chip * 2 + which
                pick = picks[source]
                sums[index, which] = dot_nn(pick[:, 0:256], r_mine[:, source].reshape(256, 1024)) + dot_nn(pick[:, 256:512], r_got[:, source].reshape(256, 1024))
            copy = pltpu.make_async_copy(sums.at[index], (give_ref, give_ref, keep_ref, keep_ref)[index].at[index % 2], out_sem.at[index])
            copy.start()
            outs.append(copy)
        for index in range(4):
            swap(index).wait_send()
        for copy in outs:
            copy.wait()


def middle(z_rows, act_gate, act_up, codes, w_gate, w_up, w_down):
    experts, width, inner = w_gate.shape
    tokens = codes.shape[2]
    by_expert = lambda e: (0, e, 0, 0)
    acts = pl.BlockSpec((8, 1, SLOT, inner), by_expert)
    act_shape = jax.ShapeDtypeStruct((8, experts, SLOT, inner), BF16)
    part = jax.ShapeDtypeStruct((2, 2, tokens, width // 2), F32)
    half = (experts, 8, SLOT, width // 2)
    dma = pltpu.SemaphoreType.DMA
    return pl.pallas_call(
        middle_kernel,
        grid=(experts,),
        out_shape=(act_shape, act_shape, act_shape, part, part),
        in_specs=[
            pl.BlockSpec((8, 1, SLOT, width), by_expert),
            acts,
            acts,
            pl.BlockSpec(memory_space=pltpu.VMEM),
            pl.BlockSpec((1, width, inner), lambda e: (e, 0, 0)),
            pl.BlockSpec((1, width, inner), lambda e: (e, 0, 0)),
            pl.BlockSpec((1, inner, width), lambda e: (e, 0, 0)),
        ],
        out_specs=(acts, acts, acts, pl.BlockSpec(memory_space=pl.ANY), pl.BlockSpec(memory_space=pl.ANY)),
        scratch_shapes=[
            pltpu.VMEM(half, BF16),
            pltpu.VMEM(half, BF16),
            pltpu.VMEM(half, BF16),
            pltpu.VMEM((8, tokens, 512), BF16),
            pltpu.VMEM((4, 2, tokens, width // 2), F32),
            dma((4,)),
            dma((4,)),
            dma((4,)),
        ],
        compiler_params=pltpu.CompilerParams(collective_id=1, has_side_effects=True, dimension_semantics=('arbitrary',), vmem_limit_bytes=64000000),
        name='middle',
    )(z_rows, act_gate, act_up, codes, w_gate, w_up, w_down)


TILES = 4


def weight_kernel(x_ref, z_ref, h_ref, da_ref, db_ref, dw1_ref, dw3_ref, dw2_ref, hidden_t):
    tile = pl.program_id(1)
    rows = 8 * SLOT

    @pl.when(tile == 0)
    def _():
        hidden_t[...] = h_ref[:, 0].reshape(rows, 512).T

    cols = pl.ds(pl.multiple_of(tile * 512, 512), 512)
    x_cols_t = x_ref[:, 0, :, cols].reshape(rows, 512).T
    dw1_ref[0] = dot_nn(x_cols_t, da_ref[:, 0].reshape(rows, 512))
    dw3_ref[0] = dot_nn(x_cols_t, db_ref[:, 0].reshape(rows, 512))
    dw2_ref[0] = dot_nn(hidden_t[...], z_ref[:, 0, :, cols].reshape(rows, 512))


def weight_grads(x_rows, z_rows, hidden, d_gate, d_up):
    _, experts, _, width = x_rows.shape
    inner = hidden.shape[3]
    by_expert = lambda e, t: (0, e, 0, 0)
    row_spec = pl.BlockSpec((8, 1, SLOT, width), by_expert)
    act_spec = pl.BlockSpec((8, 1, SLOT, inner), by_expert)
    return pl.pallas_call(
        weight_kernel,
        grid=(experts, TILES),
        out_shape=(
            jax.ShapeDtypeStruct((experts, width, inner), F32),
            jax.ShapeDtypeStruct((experts, width, inner), F32),
            jax.ShapeDtypeStruct((experts, inner, width), F32),
        ),
        in_specs=[row_spec, row_spec, act_spec, act_spec, act_spec],
        out_specs=(
            pl.BlockSpec((1, width // TILES, inner), lambda e, t: (e, t, 0)),
            pl.BlockSpec((1, width // TILES, inner), lambda e, t: (e, t, 0)),
            pl.BlockSpec((1, inner, width // TILES), lambda e, t: (e, 0, t)),
        ),
        scratch_shapes=[pltpu.VMEM((inner, 8 * SLOT), BF16)],
        compiler_params=pltpu.CompilerParams(dimension_semantics=('arbitrary', 'arbitrary'), vmem_limit_bytes=50000000),
        cost_estimate=pl.CostEstimate(flops=12_900_000_000, bytes_accessed=70_000_000, transcendentals=0),
        name='weight_grads',
    )(x_rows, z_rows, hidden, d_gate, d_up)


def shared_kernel(x_ref, dy_ref, w1_ref, w3_ref, w2_ref, dx_ref, dw1_ref, dw3_ref, dw2_ref, hidden_t, grad_gate, grad_up):
    tile = pl.program_id(0)

    @pl.when(tile == 0)
    def _():
        act_gate = dot_nn(x_ref[...], w1_ref[...]).astype(BF16)
        act_up = dot_nn(x_ref[...], w3_ref[...]).astype(BF16)
        hidden, d_gate, d_up = swiglu_parts(act_gate, act_up, dot_nt(dy_ref[...], w2_ref[...]))
        hidden_t[...] = hidden.T
        grad_gate[...] = d_gate
        grad_up[...] = d_up

    cols = pl.ds(pl.multiple_of(tile * 512, 512), 512)
    dx_ref[...] = dot_nt(grad_gate[...], w1_ref[cols, :]) + dot_nt(grad_up[...], w3_ref[cols, :])
    x_cols_t = x_ref[:, cols].T
    dw1_ref[0] = dot_nn(x_cols_t, grad_gate[...])
    dw3_ref[0] = dot_nn(x_cols_t, grad_up[...])
    dw2_ref[0] = dot_nn(hidden_t[...], dy_ref[:, cols])


def shared_backward(x_tokens, dy_tokens, shared_gate, shared_up, shared_down):
    tokens, width = x_tokens.shape
    inner = shared_gate.shape[1]
    vmem = pl.BlockSpec(memory_space=pltpu.VMEM)
    step = width // TILES
    return pl.pallas_call(
        shared_kernel,
        grid=(TILES,),
        out_shape=(
            jax.ShapeDtypeStruct((tokens, width), F32),
            jax.ShapeDtypeStruct((1, width, inner), F32),
            jax.ShapeDtypeStruct((1, width, inner), F32),
            jax.ShapeDtypeStruct((1, inner, width), F32),
        ),
        in_specs=[vmem] * 5,
        out_specs=(
            pl.BlockSpec((tokens, step), lambda t: (0, t)),
            pl.BlockSpec((1, step, inner), lambda t: (0, t, 0)),
            pl.BlockSpec((1, step, inner), lambda t: (0, t, 0)),
            pl.BlockSpec((1, inner, step), lambda t: (0, 0, t)),
        ),
        scratch_shapes=[
            pltpu.VMEM((inner, tokens), BF16),
            pltpu.VMEM((tokens, inner), BF16),
            pltpu.VMEM((tokens, inner), BF16),
        ],
        compiler_params=pltpu.CompilerParams(dimension_semantics=('arbitrary',), vmem_limit_bytes=40000000),
        cost_estimate=pl.CostEstimate(flops=6_000_000_000, bytes_accessed=20_000_000, transcendentals=0),
        name='shared_backward',
    )(x_tokens, dy_tokens, shared_gate, shared_up, shared_down)


def partners(kind):
    pairs = []
    for me in range(8):
        core = me % 2
        along_x, along_y = me ^ 2, me ^ 4
        first, second = (along_x, along_y) if core == 0 else (along_y, along_x)
        pairs.append((me, {'first': first, 'second': second, 'chip': me ^ 1}[kind]))
    return pairs


def solution(mesh):
    token_spec = P(('dp', 'ep'), None)
    expert_spec = P('ep', None, None)
    whole_spec = P(None, None)
    grad_spec = P(('dp', 'ep'), None, None)

    def local_backward(x_tokens, dy_tokens, expert_ids, gate_vals, slot_pos, w_gate, w_up, w_down, shared_gate, shared_up, shared_down):
        code = jnp.where(slot_pos >= 0, expert_ids * SLOT + slot_pos, -1)
        code = jnp.pad(code.T, ((0, 6), (0, 0)), constant_values=-1)
        gate = jnp.pad(gate_vals.T, ((0, 6), (0, 0)))
        x_rows, z_rows, act_gate, act_up, codes = gather_rows(x_tokens, dy_tokens, code, gate, w_gate, w_up)
        hidden, d_gate, d_up, give, keep = middle(z_rows, act_gate, act_up, codes, w_gate, w_up, w_down)
        got = lax.ppermute(give, 'ep', partners('first'))
        grad_w_gate, grad_w_up, grad_w_down = weight_grads(x_rows, z_rows, hidden, d_gate, d_up)
        onward = keep[0] + got[0]
        got_second = lax.ppermute(onward, 'ep', partners('second'))
        x_late, dy_late, _ = lax.optimization_barrier((x_tokens, dy_tokens, onward))
        shared_dx, grad_shared_gate, grad_shared_up, grad_shared_down = shared_backward(x_late, dy_late, shared_gate, shared_up, shared_down)
        mine = keep[1] + got[1] + got_second
        core = lax.rem(lax.axis_index('ep'), 2)
        swapped = lax.ppermute(lax.dynamic_index_in_dim(mine, 1 - core, 0, keepdims=False), 'ep', partners('chip'))
        own = lax.dynamic_index_in_dim(mine, core, 0, keepdims=False)
        left = jnp.where(core == 0, own, swapped)
        right = jnp.where(core == 0, swapped, own)
        grad_x = (jnp.concatenate((left, right), axis=1) + shared_dx).astype(BF16)
        return grad_x, grad_w_gate, grad_w_up, grad_w_down, grad_shared_gate, grad_shared_up, grad_shared_down

    return jax.shard_map(local_backward, mesh=mesh, in_specs=(token_spec, token_spec, token_spec, token_spec, token_spec, expert_spec, expert_spec, expert_spec, whole_spec, whole_spec, whole_spec), out_specs=(token_spec, grad_spec, grad_spec, grad_spec, grad_spec, grad_spec, grad_spec), check_vma=False)
```

time: 487 us -> 158 us (0.32); the launches traced: 480 us -> 158 us
  matrix products: 173 us -> 0 us
  local copies, waits for them, and re-layouts: 147 us -> 6.19 us
  Pallas kernels: 0 us -> 119 us
  waiting for transfers between devices: 118 us -> 25.5 us
  other arithmetic: 25.5 us -> 5.17 us
  starting transfers between devices: 16 us -> 1.35 us
    dot_general x16 -> x0, matrix products: 173 us -> none  [the longest x1 31.5 us: local_backward(): jnp.einsum('erd,erf->edf', x_exp, grad_gate, preferred_element_type=jnp.f...]
    pallas_call x0 -> x4, Pallas kernels: none -> 119 us  [the longest x1 52.7 us: gather_rows(): pl.pallas_call(gather_kernel, out_shape=(rows, rows, acts, acts, jax.Shap...]
    all_to_all x3 -> x0, waiting for transfers between devices: 118 us -> none  [the longest x1 63.6 us: local_backward(): x_exp = lax.all_to_all(send_x, 'ep', 0, 1, tiled=True)]
    gather x4 -> x0, local copies, waits for them, and re-layouts: 50.9 us -> none  [take_rows(): return jnp.take(rows, row_index, axis=0, mode='fill', fill_value=0)]
    all_to_all x3 -> x0, local copies, waits for them, and re-layouts: 32.4 us -> none  [the longest x1 11.6 us: local_backward(): dz_exp = lax.all_to_all(send_dz, 'ep', 0, 1, tiled=True)]
    reshape x6 -> x0, local copies, waits for them, and re-layouts: 27.8 us -> none  [the longest x1 9.18 us: local_backward(): lax.all_to_all(grad_exp, 'ep', 1, 0, tiled=True)]
    ppermute x0 -> x3, waiting for transfers between devices: none -> 25.5 us  [the longest x1 25.5 us: local_backward(): got = lax.ppermute(give, 'ep', partners('first'))]
    all_to_all x3 -> x0, starting transfers between devices: 16 us -> none  [the longest x1 5.59 us: local_backward(): x_exp = lax.all_to_all(send_x, 'ep', 0, 1, tiled=True)]
  transfers between devices with their start and end apart: 3 -> 3, of which waited for: 2 -> 1; matrix products, arithmetic and copies ran while one was open for 36% -> 0% of each run, Pallas kernels for 0% -> 24%
where the time goes in v2:
time: 158 us
  Pallas kernels  119 us (75%)
  waiting for transfers between devices  25.5 us (16%)
  local copies, waits for them, and re-layouts  6.19 us (4%)
  other arithmetic  5.17 us (3%)
    pallas_call x1, Pallas kernels, gather_rows(): pl.pallas_call(gather_kernel, out_shape=(rows, rows, acts, acts, jax.Shap...  52.7 us
    pallas_call x1, Pallas kernels, weight_grads(): pl.pallas_call(weight_kernel, grid=(experts, TILES), out_shape=(jax.Shape...  30.7 us
    pallas_call x1, Pallas kernels, middle(): pl.pallas_call(middle_kernel, grid=(experts,), out_shape=(act_shape, act_...  27.9 us
    ppermute x1, waiting for transfers between devices, local_backward(): got = lax.ppermute(give, 'ep', partners('first'))  25.5 us
    pallas_call x1, Pallas kernels, shared_backward(): pl.pallas_call(shared_kernel, grid=(TILES,), out_shape=(jax.ShapeDtypeStr...  7.5 us
    unnamed x18, local copies, waits for them, and re-layouts  4.24 us
  transfers between devices with their start and end apart: 3, of which 1 were waited for; matrix products, arithmetic and copies ran while one was open for 0% of the time, Pallas kernels for 24%

profile of v2, /device:TPU:0, one launch (start us, length us, event | category | flops | bytes accessed | tf_op | source)
XLA Modules:
  0.0 157.8 jit_solution(3046562639289570865)
XLA Ops:
  0.6 0.7 select_bitcast_fusion
  1.4 0.6 pad.8.code_ref
  2.0 1.3 pad.9.gate_ref
  3.3 52.7 %gather_rows.1 = (bf16[8,4,64,2048]{3,2,1,0:T(8,128)(2,1)}, bf16[8,4,64,2048]{3,2,1,0:T(8,128)(2,1)}, bf16[8,4,64,512]{3,2,1,0:T(8,128)(2,1)}, bf16[8,4,64,512]{3,2,1,0:T(8,128)(2,1)}, s32[8,16,128]{2,1,0:T(8,128)}) custom-call(bf16[128,2048]{1,0:T(8,128)(2,1)} %x_ref.2, bf16[128,2048]{1,0:T(8,128)(2,1)} %dy_ref.2, s32[16,128]{1,0:T(8,128)} %pad.8.code_ref, ...), custom_call_target="tpu_custom_call" | custom-call | tf_op jit(solution)/shard_map/gather_rows/pallas_call | solution.py:221
  56.0 27.9 %middle.1 = (bf16[8,4,64,512]{3,2,1,0:T(8,128)(2,1)}, bf16[8,4,64,512]{3,2,1,0:T(8,128)(2,1)}, bf16[8,4,64,512]{3,2,1,0:T(8,128)(2,1)}, f32[2,2,128,1024]{3,2,1,0:T(8,128)}, f32[2,2,128,1024]{3,2,1,0:T(8,128)}) custom-call(bf16[8,4,64,2048]{3,2,1,0:T(8,128)(2,1)} %get-tuple-element.26.z_ref, bf16[8,4,64,512]{3,2,1,0:T(8,128)(2,1)} %get-tuple-element.27.a_ref, ...), custom_call_target="tpu_custom_call" | custom-call | tf_op jit(solution)/shard_map/middle/pallas_call | solution.py:314
  83.9 0.0 copy-start.5
  83.9 0.6 collective-permute-start
  84.5 25.5 %collective-permute-done = f32[2,2,128,1024]{3,2,1,0:T(8,128)} collective-permute-done((f32[2,2,128,1024]{3,2,1,0:T(8,128)}, f32[2,2,128,1024]{3,2,1,0:T(8,128)}, u32[]{:S(2)}, u32[]{:S(2)}) %collective-permute-start) | collective-permute-done | bytes 2097184 | tf_op jit(solution)/shard_map/ppermute | solution.py:462
  110.0 1.7 %fusion = f32[2,128,1024]{2,1,0:T(8,128)S(1)} fusion(f32[2,2,128,1024]{3,2,1,0:T(8,128)} %collective-permute-done, f32[2,2,128,1024]{3,2,1,0:T(8,128)} %get-tuple-element.30), kind=kLoop, calls=%fused_computation.1 | loop fusion | flops 262144 | bytes 3145728 | tf_op jit(solution)/shard_map/add | solution.py:464
  111.7 0.7 collective-permute-start.1
  112.4 0.0 copy-done.5
  112.4 1.6 %copy-done.6 = bf16[8,4,64,512]{3,2,1,0:T(8,128)(2,1)S(1)} copy-done((bf16[8,4,64,512]{3,2,1,0:T(8,128)(2,1)S(1)}, bf16[8,4,64,512]{3,2,1,0:T(8,128)(2,1)}, u32[]{:S(2)}) %copy-start.6) | copy-done | bytes 2097176
  114.0 0.0 copy-start.7
  114.0 1.6 %copy-done.7 = bf16[8,4,64,512]{3,2,1,0:T(8,128)(2,1)S(1)} copy-done((bf16[8,4,64,512]{3,2,1,0:T(8,128)(2,1)S(1)}, bf16[8,4,64,512]{3,2,1,0:T(8,128)(2,1)}, u32[]{:S(2)}) %copy-start.7) | copy-done | bytes 2097176
  115.6 0.0 copy-start.8
  115.6 0.0 copy-start.4
  115.6 30.7 %weight_grads.1 = (f32[4,2048,512]{2,1,0:T(8,128)}, f32[4,2048,512]{2,1,0:T(8,128)}, f32[4,512,2048]{2,1,0:T(8,128)}) custom-call(bf16[8,4,64,2048]{3,2,1,0:T(8,128)(2,1)} %get-tuple-element.35.x_ref, bf16[8,4,64,2048]{3,2,1,0:T(8,128)(2,1)} %get-tuple-element.26.z_ref, bf16[8,4,64,512]{3,2,1,0:T(8,128)(2,1)S(1)} %copy-done.5, ...), custom_call_target="tpu_custom_call" | custom-call | flops 12899999744 | bytes 70000000 | tf_op jit(solution)/shard_map/weight_grads/pallas_call | solution.py:367
  146.3 0.0 copy-start.3
  146.4 0.0 collective-permute-done.1
  146.4 0.0 copy-done.8
  146.4 1.7 %fusion.2 = f32[2,128,1024]{2,1,0:T(8,128)S(1)} fusion(f32[2,128,1024]{2,1,0:T(8,128)S(1)} %collective-permute-done.1, f32[2,2,128,1024]{3,2,1,0:T(8,128)} %collective-permute-done, f32[2,2,128,1024]{3,2,1,0:T(8,128)S(1)} %copy-done.8), kind=kLoop, calls=%fused_computation.4 | loop fusion | flops 524288 | bytes 4194304 | tf_op jit(solution)/shard_map/add | solution.py:468
  148.0 0.1 dynamic-slice_bitcast_fusion
  148.1 0.0 collective-permute-start.2
  148.1 0.0 copy-done.4
  148.2 0.0 copy-done
  148.2 0.0 copy-done.1
  148.2 0.4 copy-done.2
  148.6 0.6 copy-done.3
  149.2 7.5 %shared_backward.1 = (f32[128,2048]{1,0:T(8,128)S(1)}, f32[1,2048,512]{2,1,0:T(8,128)}, f32[1,2048,512]{2,1,0:T(8,128)}, f32[1,512,2048]{2,1,0:T(8,128)}) custom-call(bf16[128,2048]{1,0:T(8,128)(2,1)S(1)} %copy-done, bf16[128,2048]{1,0:T(8,128)(2,1)S(1)} %copy-done.1, bf16[2048,512]{1,0:T(8,128)(2,1)S(1)} %copy-done.2, bf16[2048,512]{1,0:T(8,128)(2,1)S(1)} %copy-done.3, ...), custom_call_target="tpu_custom_call" | custom-call | flops 6000000000 | bytes 20000000 | tf_op jit(solution)/shard_map/shared_backward/pallas_call | solution.py:413
  156.7 0.0 collective-permute-done.2
  156.7 0.1 bitcast_select_fusion.1
  156.9 0.9 fusion.3
  (4 shorter events, 0.0 us)
Async XLA Ops:
  83.9 28.5 %copy-start.5 = (bf16[8,4,64,512]{3,2,1,0:T(8,128)(2,1)S(1)}, bf16[8,4,64,512]{3,2,1,0:T(8,128)(2,1)}, u32[]{:S(2)}) copy-start(bf16[8,4,64,512]{3,2,1,0:T(8,128)(2,1)} %get-tuple-element.36.h_ref) | copy-start | bytes 6291460
  83.9 26.1 %collective-permute-start = (f32[2,2,128,1024]{3,2,1,0:T(8,128)}, f32[2,2,128,1024]{3,2,1,0:T(8,128)}, u32[]{:S(2)}, u32[]{:S(2)}) collective-permute-start(f32[2,2,128,1024]{3,2,1,0:T(8,128)} %get-tuple-element.31), channel_id=1, source_target_pairs={{0,2},{1,5},{2,0},{3,7},{4,6},{5,1},{6,4},{7,3},{8,10},{9,13},{10,... | collective-permute-start | bytes 6291464 | tf_op jit(solution)/shard_map/ppermute | solution.py:462
  111.7 34.7 %collective-permute-start.1 = (f32[2,128,1024]{2,1,0:T(8,128)S(1)}, f32[2,128,1024]{2,1,0:T(8,128)S(1)}, u32[]{:S(2)}, u32[]{:S(2)}) collective-permute-start(f32[2,128,1024]{2,1,0:T(8,128)S(1)} %fusion), channel_id=1, source_target_pairs={{0,4},{1,3},{2,6},{3,1},{4,0},{5,7},{6,2},{7,5},{8,12},{9,11},{10,... | collective-permute-start | bytes 3145736 | tf_op jit(solution)/shard_map/ppermute | solution.py:465
  112.4 1.6 %copy-start.6 = (bf16[8,4,64,512]{3,2,1,0:T(8,128)(2,1)S(1)}, bf16[8,4,64,512]{3,2,1,0:T(8,128)(2,1)}, u32[]{:S(2)}) copy-start(bf16[8,4,64,512]{3,2,1,0:T(8,128)(2,1)} %get-tuple-element.37.da_ref) | copy-start | bytes 6291460
  114.0 1.6 %copy-start.7 = (bf16[8,4,64,512]{3,2,1,0:T(8,128)(2,1)S(1)}, bf16[8,4,64,512]{3,2,1,0:T(8,128)(2,1)}, u32[]{:S(2)}) copy-start(bf16[8,4,64,512]{3,2,1,0:T(8,128)(2,1)} %get-tuple-element.38.db_ref) | copy-start | bytes 6291460
  115.6 30.8 %copy-start.8 = (f32[2,2,128,1024]{3,2,1,0:T(8,128)S(1)}, f32[2,2,128,1024]{3,2,1,0:T(8,128)}, u32[]{:S(2)}) copy-start(f32[2,2,128,1024]{3,2,1,0:T(8,128)} %get-tuple-element.30) | copy-start | bytes 6291460
  115.6 32.5 %copy-start.4 = (bf16[512,2048]{1,0:T(8,128)(2,1)S(1)}, bf16[512,2048]{1,0:T(8,128)(2,1)}, u32[]{:S(2)}) copy-start(bf16[512,2048]{1,0:T(8,128)(2,1)} %w2_ref.3) | copy-start | bytes 6291460
  146.3 1.8 %copy-start = (bf16[128,2048]{1,0:T(8,128)(2,1)S(1)}, bf16[128,2048]{1,0:T(8,128)(2,1)}, u32[]{:S(2)}) copy-start(bf16[128,2048]{1,0:T(8,128)(2,1)} %x_ref.2) | copy-start | bytes 1572868
  146.3 1.8 %copy-start.1 = (bf16[128,2048]{1,0:T(8,128)(2,1)S(1)}, bf16[128,2048]{1,0:T(8,128)(2,1)}, u32[]{:S(2)}) copy-start(bf16[128,2048]{1,0:T(8,128)(2,1)} %dy_ref.2) | copy-start | bytes 1572868
  146.3 2.2 %copy-start.2 = (bf16[2048,512]{1,0:T(8,128)(2,1)S(1)}, bf16[2048,512]{1,0:T(8,128)(2,1)}, u32[]{:S(2)}) copy-start(bf16[2048,512]{1,0:T(8,128)(2,1)} %w1_ref.5) | copy-start | bytes 6291460
  146.3 2.9 %copy-start.3 = (bf16[2048,512]{1,0:T(8,128)(2,1)S(1)}, bf16[2048,512]{1,0:T(8,128)(2,1)}, u32[]{:S(2)}) copy-start(bf16[2048,512]{1,0:T(8,128)(2,1)} %w3_ref.5) | copy-start | bytes 6291460
  148.1 8.6 %collective-permute-start.2 = (f32[128,1024]{1,0:T(8,128)S(1)}, f32[128,1024]{1,0:T(8,128)S(1)}, u32[]{:S(2)}, u32[]{:S(2)}) collective-permute-start(f32[128,1024]{1,0:T(8,128)S(1)} %dynamic-slice_bitcast_fusion), channel_id=1, source_target_pairs={{0,1},{1,0},{2,3},{3,2},{4,5},{5,4},{6,7},{7,6},{8,9},{9,8},{10,11... | collective-permute-start | bytes 1572872 | tf_op jit(solution)/shard_map/ppermute | solution.py:470

commit v3 on v2

--- a/solution.py
+++ b/solution.py
@@ -460,11 +460,13 @@
         x_rows, z_rows, act_gate, act_up, codes = gather_rows(x_tokens, dy_tokens, code, gate, w_gate, w_up)
         hidden, d_gate, d_up, give, keep = middle(z_rows, act_gate, act_up, codes, w_gate, w_up, w_down)
         got = lax.ppermute(give, 'ep', partners('first'))
-        grad_w_gate, grad_w_up, grad_w_down = weight_grads(x_rows, z_rows, hidden, d_gate, d_up)
+        grads = weight_grads(x_rows, z_rows, hidden, d_gate, d_up)
+        got, grad_w_gate, grad_w_up, grad_w_down = lax.optimization_barrier((got,) + tuple(grads))
         onward = keep[0] + got[0]
         got_second = lax.ppermute(onward, 'ep', partners('second'))
         x_late, dy_late, _ = lax.optimization_barrier((x_tokens, dy_tokens, onward))
         shared_dx, grad_shared_gate, grad_shared_up, grad_shared_down = shared_backward(x_late, dy_late, shared_gate, shared_up, shared_down)
+        got_second, shared_dx = lax.optimization_barrier((got_second, shared_dx))
         mine = keep[1] + got[1] + got_second
         core = lax.rem(lax.axis_index('ep'), 2)
         swapped = lax.ppermute(lax.dynamic_index_in_dim(mine, 1 - core, 0, keepdims=False), 'ep', partners('chip'))

time: 158 us -> 141 us (0.89)
  waiting for transfers between devices: 25.5 us -> 2.99 us
  local copies, waits for them, and re-layouts: 6.19 us -> 12.7 us
  other arithmetic: 5.17 us -> 3.38 us
    ppermute x1, waiting for transfers between devices: 25.5 us -> 0.01 us  [local_backward(): got = lax.ppermute(give, 'ep', partners('first'))]
    unnamed x18 -> x24, local copies, waits for them, and re-layouts: 4.24 us -> 10.7 us
    ppermute x1, waiting for transfers between devices: 0.01 us -> 1.89 us  [local_backward(): lax.ppermute(lax.dynamic_index_in_dim(mine, 1 - core, 0, keepdims=False),...]
  transfers between devices with their start and end apart: 3 -> 3, of which waited for: 1 -> 2; matrix products, arithmetic and copies ran while one was open for 0% -> 0% of each run, Pallas kernels for 24% -> 27%
where the time goes in v3:
time: 141 us
  Pallas kernels  119 us (84%)
  local copies, waits for them, and re-layouts  12.7 us (9%)
  other arithmetic  3.38 us (2%)
  waiting for transfers between devices  2.99 us (2%)
  starting transfers between devices  2.04 us (1%)
    pallas_call x1, Pallas kernels, gather_rows(): pl.pallas_call(gather_kernel, out_shape=(rows, rows, acts, acts, jax.Shap...  52.7 us
    pallas_call x1, Pallas kernels, weight_grads(): pl.pallas_call(weight_kernel, grid=(experts, TILES), out_shape=(jax.Shape...  30.7 us
    pallas_call x1, Pallas kernels, middle(): pl.pallas_call(middle_kernel, grid=(experts,), out_shape=(act_shape, act_...  27.8 us
    unnamed x24, local copies, waits for them, and re-layouts  10.7 us
    pallas_call x1, Pallas kernels, shared_backward(): pl.pallas_call(shared_kernel, grid=(TILES,), out_shape=(jax.ShapeDtypeStr...  7.5 us
  transfers between devices with their start and end apart: 3, of which 2 were waited for; matrix products, arithmetic and copies ran while one was open for 0% of the time, Pallas kernels for 27%

profile of v3, /device:TPU:0, one launch (start us, length us, event | category | flops | bytes accessed | tf_op | source)
XLA Modules:
  0.0 140.6 jit_solution(490847547038002703)
XLA Ops:
  0.6 0.7 select_bitcast_fusion
  1.4 0.6 pad.8.code_ref
  2.0 1.3 pad.9.gate_ref
  3.3 52.7 %gather_rows.1 = (bf16[8,4,64,2048]{3,2,1,0:T(8,128)(2,1)}, bf16[8,4,64,2048]{3,2,1,0:T(8,128)(2,1)}, bf16[8,4,64,512]{3,2,1,0:T(8,128)(2,1)}, bf16[8,4,64,512]{3,2,1,0:T(8,128)(2,1)}, s32[8,16,128]{2,1,0:T(8,128)}) custom-call(bf16[128,2048]{1,0:T(8,128)(2,1)} %x_ref.2, bf16[128,2048]{1,0:T(8,128)(2,1)} %dy_ref.2, s32[16,128]{1,0:T(8,128)} %pad.8.code_ref, ...), custom_call_target="tpu_custom_call" | custom-call | tf_op jit(solution)/shard_map/gather_rows/pallas_call | solution.py:221
  56.0 27.8 %middle.1 = (bf16[8,4,64,512]{3,2,1,0:T(8,128)(2,1)}, bf16[8,4,64,512]{3,2,1,0:T(8,128)(2,1)}, bf16[8,4,64,512]{3,2,1,0:T(8,128)(2,1)}, f32[2,2,128,1024]{3,2,1,0:T(8,128)}, f32[2,2,128,1024]{3,2,1,0:T(8,128)}) custom-call(bf16[8,4,64,2048]{3,2,1,0:T(8,128)(2,1)} %get-tuple-element.32.z_ref, bf16[8,4,64,512]{3,2,1,0:T(8,128)(2,1)} %get-tuple-element.33.a_ref, ...), custom_call_target="tpu_custom_call" | custom-call | tf_op jit(solution)/shard_map/middle/pallas_call | solution.py:314
  83.8 0.6 collective-permute-start
  84.4 0.0 copy-start.5
  84.4 1.6 %copy-done.5 = bf16[8,4,64,512]{3,2,1,0:T(8,128)(2,1)S(1)} copy-done((bf16[8,4,64,512]{3,2,1,0:T(8,128)(2,1)S(1)}, bf16[8,4,64,512]{3,2,1,0:T(8,128)(2,1)}, u32[]{:S(2)}) %copy-start.5) | copy-done | bytes 2097176
  86.0 1.6 %copy-done.6 = bf16[8,4,64,512]{3,2,1,0:T(8,128)(2,1)S(1)} copy-done((bf16[8,4,64,512]{3,2,1,0:T(8,128)(2,1)S(1)}, bf16[8,4,64,512]{3,2,1,0:T(8,128)(2,1)}, u32[]{:S(2)}) %copy-start.6) | copy-done | bytes 2097176
  87.6 1.6 %copy-done.7 = bf16[8,4,64,512]{3,2,1,0:T(8,128)(2,1)S(1)} copy-done((bf16[8,4,64,512]{3,2,1,0:T(8,128)(2,1)S(1)}, bf16[8,4,64,512]{3,2,1,0:T(8,128)(2,1)}, u32[]{:S(2)}) %copy-start.7) | copy-done | bytes 2097176
  89.2 30.7 %weight_grads.1 = (f32[4,2048,512]{2,1,0:T(8,128)}, f32[4,2048,512]{2,1,0:T(8,128)}, f32[4,512,2048]{2,1,0:T(8,128)}) custom-call(bf16[8,4,64,2048]{3,2,1,0:T(8,128)(2,1)} %get-tuple-element.38.x_ref, bf16[8,4,64,2048]{3,2,1,0:T(8,128)(2,1)} %get-tuple-element.32.z_ref, bf16[8,4,64,512]{3,2,1,0:T(8,128)(2,1)S(1)} %copy-done.5, ...), custom_call_target="tpu_custom_call" | custom-call | flops 12899999744 | bytes 70000000 | tf_op jit(solution)/shard_map/weight_grads/pallas_call | solution.py:367
  119.9 0.0 collective-permute-done
  119.9 0.0 copy-start.10
  119.9 0.0 copy-done.8
  119.9 0.1 add_bitcast_fusion
  120.0 1.2 copy-done.10
  121.2 1.4 %collective-permute-start.1 = (f32[2,128,1024]{2,1,0:T(8,128)S(1)}, f32[2,128,1024]{2,1,0:T(8,128)}, u32[]{:S(2)}, u32[]{:S(2)}) collective-permute-start(f32[2,128,1024]{2,1,0:T(8,128)S(1)} %add_bitcast_fusion), channel_id=1, source_target_pairs={{0,4},{1,3},{2,6},{3,1},{4,0},{5,7},{6,2},{7,5},{8,12},{9,11},{10,... | collective-permute-start | bytes 3145736 | tf_op jit(solution)/shard_map/ppermute | solution.py:466
  122.6 0.0 copy-done
  122.6 0.0 copy-done.1
  122.6 1.6 %copy-done.2 = bf16[2048,512]{1,0:T(8,128)(2,1)S(1)} copy-done((bf16[2048,512]{1,0:T(8,128)(2,1)S(1)}, bf16[2048,512]{1,0:T(8,128)(2,1)}, u32[]{:S(2)}) %copy-start.2) | copy-done | bytes 2097176
  124.2 1.6 %copy-done.3 = bf16[2048,512]{1,0:T(8,128)(2,1)S(1)} copy-done((bf16[2048,512]{1,0:T(8,128)(2,1)S(1)}, bf16[2048,512]{1,0:T(8,128)(2,1)}, u32[]{:S(2)}) %copy-start.3) | copy-done | bytes 2097176
  125.8 1.6 %copy-done.4 = bf16[512,2048]{1,0:T(8,128)(2,1)S(1)} copy-done((bf16[512,2048]{1,0:T(8,128)(2,1)S(1)}, bf16[512,2048]{1,0:T(8,128)(2,1)}, u32[]{:S(2)}) %copy-start.4) | copy-done | bytes 2097176
  127.4 7.5 %shared_backward.1 = (f32[128,2048]{1,0:T(8,128)S(1)}, f32[1,2048,512]{2,1,0:T(8,128)}, f32[1,2048,512]{2,1,0:T(8,128)}, f32[1,512,2048]{2,1,0:T(8,128)}) custom-call(bf16[128,2048]{1,0:T(8,128)(2,1)S(1)} %copy-done, bf16[128,2048]{1,0:T(8,128)(2,1)S(1)} %copy-done.1, bf16[2048,512]{1,0:T(8,128)(2,1)S(1)} %copy-done.2, bf16[2048,512]{1,0:T(8,128)(2,1)S(1)} %copy-done.3, ...), custom_call_target="tpu_custom_call" | custom-call | flops 6000000000 | bytes 20000000 | tf_op jit(solution)/shard_map/shared_backward/pallas_call | solution.py:413
  134.9 1.1 collective-permute-done.1
  136.0 0.0 copy-done.9
  136.0 0.0 copy-done.11
  136.0 1.5 %bitcast_add_fusion = f32[2,128,1024]{2,1,0:T(8,128)S(1)} fusion(f32[2,128,1024]{2,1,0:T(8,128)} %collective-permute-done.1, f32[2,2,128,1024]{3,2,1,0:T(8,128)S(1)} %copy-done.11, f32[2,2,128,1024]{3,2,1,0:T(8,128)S(1)} %copy-done.9), kind=kLoop, calls=%fused_computation.2 | loop fusion | flops 524288 | bytes 4194304 | tf_op jit(solution)/shard_map/add | solution.py:470
  137.5 0.1 dynamic-slice_bitcast_fusion
  137.6 0.0 collective-permute-start.2
  137.6 1.9 %collective-permute-done.2 = f32[128,1024]{1,0:T(8,128)S(1)} collective-permute-done((f32[128,1024]{1,0:T(8,128)S(1)}, f32[128,1024]{1,0:T(8,128)S(1)}, u32[]{:S(2)}, u32[]{:S(2)}) %collective-permute-start.2) | collective-permute-done | bytes 524320 | tf_op jit(solution)/shard_map/ppermute | solution.py:472
  139.5 0.1 bitcast_select_fusion.1
  139.6 0.9 fusion
  (10 shorter events, 0.0 us)
Async XLA Ops:
  83.8 36.1 %collective-permute-start = (f32[2,2,128,1024]{3,2,1,0:T(8,128)}, f32[2,2,128,1024]{3,2,1,0:T(8,128)S(1)}, u32[]{:S(2)}, u32[]{:S(2)}) collective-permute-start(f32[2,2,128,1024]{3,2,1,0:T(8,128)} %get-tuple-element.37), channel_id=1, source_target_pairs={{0,2},{1,5},{2,0},{3,7},{4,6},{5,1},{6,4},{7,3},{8,10},{9,13},{10,... | collective-permute-start | bytes 6291464 | tf_op jit(solution)/shard_map/ppermute | solution.py:462
  84.4 1.6 %copy-start.5 = (bf16[8,4,64,512]{3,2,1,0:T(8,128)(2,1)S(1)}, bf16[8,4,64,512]{3,2,1,0:T(8,128)(2,1)}, u32[]{:S(2)}) copy-start(bf16[8,4,64,512]{3,2,1,0:T(8,128)(2,1)} %get-tuple-element.39.h_ref) | copy-start | bytes 6291460
  86.0 1.6 %copy-start.6 = (bf16[8,4,64,512]{3,2,1,0:T(8,128)(2,1)S(1)}, bf16[8,4,64,512]{3,2,1,0:T(8,128)(2,1)}, u32[]{:S(2)}) copy-start(bf16[8,4,64,512]{3,2,1,0:T(8,128)(2,1)} %get-tuple-element.40.da_ref) | copy-start | bytes 6291460
  87.6 1.6 %copy-start.7 = (bf16[8,4,64,512]{3,2,1,0:T(8,128)(2,1)S(1)}, bf16[8,4,64,512]{3,2,1,0:T(8,128)(2,1)}, u32[]{:S(2)}) copy-start(bf16[8,4,64,512]{3,2,1,0:T(8,128)(2,1)} %get-tuple-element.41.db_ref) | copy-start | bytes 6291460
  89.1 30.7 %copy-start.8 = (f32[2,2,128,1024]{3,2,1,0:T(8,128)S(1)}, f32[2,2,128,1024]{3,2,1,0:T(8,128)}, u32[]{:S(2)}) copy-start(f32[2,2,128,1024]{3,2,1,0:T(8,128)} %get-tuple-element.36) | copy-start | bytes 6291460
  119.9 2.8 %copy-start = (bf16[128,2048]{1,0:T(8,128)(2,1)S(1)}, bf16[128,2048]{1,0:T(8,128)(2,1)}, u32[]{:S(2)}) copy-start(bf16[128,2048]{1,0:T(8,128)(2,1)} %x_ref.2) | copy-start | bytes 1572868
  119.9 2.8 %copy-start.1 = (bf16[128,2048]{1,0:T(8,128)(2,1)S(1)}, bf16[128,2048]{1,0:T(8,128)(2,1)}, u32[]{:S(2)}) copy-start(bf16[128,2048]{1,0:T(8,128)(2,1)} %dy_ref.2) | copy-start | bytes 1572868
  119.9 1.3 copy-start.10
  121.2 14.8 %collective-permute-start.1 = (f32[2,128,1024]{2,1,0:T(8,128)S(1)}, f32[2,128,1024]{2,1,0:T(8,128)}, u32[]{:S(2)}, u32[]{:S(2)}) collective-permute-start(f32[2,128,1024]{2,1,0:T(8,128)S(1)} %add_bitcast_fusion), channel_id=1, source_target_pairs={{0,4},{1,3},{2,6},{3,1},{4,0},{5,7},{6,2},{7,5},{8,12},{9,11},{10,... | collective-permute-start | bytes 3145736 | tf_op jit(solution)/shard_map/ppermute | solution.py:466
  122.6 1.6 %copy-start.2 = (bf16[2048,512]{1,0:T(8,128)(2,1)S(1)}, bf16[2048,512]{1,0:T(8,128)(2,1)}, u32[]{:S(2)}) copy-start(bf16[2048,512]{1,0:T(8,128)(2,1)} %w1_ref.5) | copy-start | bytes 6291460
  124.2 1.6 %copy-start.3 = (bf16[2048,512]{1,0:T(8,128)(2,1)S(1)}, bf16[2048,512]{1,0:T(8,128)(2,1)}, u32[]{:S(2)}) copy-start(bf16[2048,512]{1,0:T(8,128)(2,1)} %w3_ref.5) | copy-start | bytes 6291460
  125.8 1.6 %copy-start.4 = (bf16[512,2048]{1,0:T(8,128)(2,1)S(1)}, bf16[512,2048]{1,0:T(8,128)(2,1)}, u32[]{:S(2)}) copy-start(bf16[512,2048]{1,0:T(8,128)(2,1)} %w2_ref.3) | copy-start | bytes 6291460
  127.4 8.6 %copy-start.9 = (f32[2,2,128,1024]{3,2,1,0:T(8,128)S(1)}, f32[2,2,128,1024]{3,2,1,0:T(8,128)}, u32[]{:S(2)}) copy-start(f32[2,2,128,1024]{3,2,1,0:T(8,128)} %get-tuple-element.36) | copy-start | bytes 6291460
  127.4 8.6 %copy-start.11 = (f32[2,2,128,1024]{3,2,1,0:T(8,128)S(1)}, f32[2,2,128,1024]{3,2,1,0:T(8,128)}, u32[]{:S(2)}) copy-start(f32[2,2,128,1024]{3,2,1,0:T(8,128)} %copy-done.10) | copy-start | bytes 6291460
  137.6 1.9 %collective-permute-start.2 = (f32[128,1024]{1,0:T(8,128)S(1)}, f32[128,1024]{1,0:T(8,128)S(1)}, u32[]{:S(2)}, u32[]{:S(2)}) collective-permute-start(f32[128,1024]{1,0:T(8,128)S(1)} %dynamic-slice_bitcast_fusion), channel_id=1, source_target_pairs={{0,1},{1,0},{2,3},{3,2},{4,5},{5,4},{6,7},{7,6},{8,9},{9,8},{10,11... | collective-permute-start | bytes 1572872 | tf_op jit(solution)/shard_map/ppermute | solution.py:472

commit v4 on v0

v4 whole, which is shorter than its diff:
```python
import jax
import jax.numpy as jnp
from jax import lax
from jax.experimental import pallas as pl
from jax.experimental.pallas import tpu as pltpu
from jax.sharding import PartitionSpec as P

MESH = pl.DeviceIdType.MESH
SLOT = 64
BF16 = jnp.bfloat16
F32 = jnp.float32


def swiglu_parts(act_gate, act_up, grad_hidden):
    gate_f32 = act_gate.astype(F32)
    up_f32 = act_up.astype(F32)
    sigma = jax.nn.sigmoid(gate_f32)
    silu_gate = gate_f32 * sigma
    hidden = (silu_gate * up_f32).astype(BF16)
    grad_gate = (grad_hidden * up_f32 * sigma * (1.0 + gate_f32 * (1.0 - sigma))).astype(BF16)
    grad_up = (grad_hidden * silu_gate).astype(BF16)
    return hidden, grad_gate, grad_up


def dot_nn(a, b):
    return lax.dot_general(a, b, (((1,), (0,)), ((), ())), preferred_element_type=F32)


def dot_nt(a, b):
    return lax.dot_general(a, b, (((1,), (1,)), ((), ())), preferred_element_type=F32)


def dot_tn(a, b):
    return lax.dot_general(a, b, (((0,), (0,)), ((), ())), preferred_element_type=F32)


def places():
    me = lax.axis_index('ep')
    core = lax.rem(me, 2)
    flip_x = 2 - 4 * lax.rem(me // 2, 2)
    flip_y = 4 - 8 * (me // 4)
    first = me + flip_x * (1 - core) + flip_y * core
    second = me + flip_y * (1 - core) + flip_x * core
    diag = me + flip_x + flip_y
    partner = me + 1 - 2 * core
    return me, core, first, second, diag, partner


def remote(src, dst, send_sem, recv_sem, device):
    return pltpu.make_async_remote_copy(src_ref=src, dst_ref=dst, send_sem=send_sem, recv_sem=recv_sem, device_id={'ep': device}, device_id_type=MESH)


def one_hot(code, base, rows):
    slot = lax.broadcasted_iota(jnp.int32, (rows, 128), 0) + base
    hits = jnp.zeros((rows, 128), F32)
    for choice in range(10):
        hits = jnp.where(slot == code[choice:choice + 1, :], 1.0, hits)
    return hits


SEEN_AS = {1: 1, 2: 2, 3: 5, 4: 4, 5: 3, 6: 6, 7: 7}
PART = 64


def rows_kernel(x_ref, dy_ref, code_ref, gate_ref, w1_ref, w3_ref, w2_ref, xr_ref, zr_ref, h_ref, da_ref, db_ref, give_ref, keep_ref, xbuf, dybuf, codes, gates, picks, picks_partner, x_rows, z_rows, w1_buf, w3_buf, w2_buf, acts, grads, r_send, r_mine, r_got, sums, own_sem, send_sem, recv_sem, meta_send, meta_recv, load_sem, rows_sem, grads_sem, swap_send, swap_recv, sums_sem):
    me, core, first, second, diag, partner = places()
    other = 1 - core
    bufs = (xbuf, dybuf)

    def own(which):
        src, dst = ((x_ref, xbuf.at[0]), (dy_ref, dybuf.at[0]), (code_ref, codes.at[0]), (gate_ref, gates.at[0]))[which]
        return pltpu.make_async_copy(src, dst, own_sem.at[which])

    def load(which, expert):
        src, dst = ((w1_ref, w1_buf), (w3_ref, w3_buf), (w2_ref, w2_buf))[which]
        return pltpu.make_async_copy(src.at[expert], dst.at[expert], load_sem.at[which, expert])

    def trip(array, part, kind):
        src, dst, device = ((0, 2, first), (0, 4, second), (0, 1, partner), (2, 6, second), (2, 3, partner), (4, 5, partner), (6, 7, partner))[kind]
        rows = pl.ds(part * PART, PART)
        return remote(bufs[array].at[src, rows], bufs[array].at[dst, rows], send_sem.at[array, part, kind], recv_sem.at[array, part, kind], device)

    def meta(which, role):
        device = {1: partner, 2: first, 3: (second // 2) * 2 + other, 4: second, 5: (first // 2) * 2 + other, 6: diag, 7: (diag // 2) * 2 + other}[role]
        table = (codes, gates)[which]
        seen = SEEN_AS[role]
        return remote(table.at[0], table.at[seen], meta_send.at[which, role - 1], meta_recv.at[which, seen - 1], device)

    def relay_first(array, part):
        trip(array, part, 0).wait_recv()
        trip(array, part, 1).start()
        trip(array, part, 3).start()
        trip(array, part, 4).start()

    def relay_rest(array, part):
        trip(array, part, 1).wait_recv()
        trip(array, part, 5).start()
        trip(array, part, 3).wait_recv()
        trip(array, part, 6).start()

    def arrived(array, kind):
        for part in range(2):
            trip(array, part, kind).wait_recv()

    def rows_out(array, half, at):
        return pltpu.make_async_copy((x_rows, z_rows)[array].at[at], (xr_ref, zr_ref)[array].at[half, at], rows_sem.at[array, half, at])

    def pick_x(half, low, high):
        def one(at, carry):
            role = half * 4 + at
            select = one_hot(codes[role], me * 256, 256).astype(BF16)
            picks[role] = select
            picks_partner[role] = one_hot(codes[role], partner * 256, 256).astype(BF16)
            for tile in range(4):
                cols = slice(tile * 512, tile * 512 + 512)
                x_rows[at, :, :, cols] = dot_nn(select, xbuf[role, :, cols]).astype(BF16).reshape(4, SLOT, 512)
            rows_out(0, half, at).start()
            return carry

        lax.fori_loop(low, high, one, 0)

    def pick_z(half, low, high):
        def one(at, carry):
            role = half * 4 + at
            slot = lax.broadcasted_iota(jnp.int32, (256, 128), 0) + me * 256
            spread = jnp.zeros((256, 128), F32)
            for choice in range(10):
                spread = jnp.where(slot == codes[role, choice:choice + 1, :], gates[role, choice:choice + 1, :], spread)
            scale = jnp.sum(spread, axis=1, keepdims=True)
            select = picks[role]
            for tile in range(4):
                cols = slice(tile * 512, tile * 512 + 512)
                value = dot_nn(select, dybuf[role, :, cols]) * scale
                z_rows[at, :, :, cols] = value.astype(BF16).reshape(4, SLOT, 512)
            rows_out(1, half, at).start()
            return carry

        lax.fori_loop(low, high, one, 0)

    def activations(half, after):
        def one(expert, carry):
            if half == 0:
                load(0, expert).wait()
                load(1, expert).wait()
            rows = x_rows[:, expert].reshape(4 * SLOT, 2048)
            acts[0, half, expert] = dot_nn(rows, w1_buf[expert]).astype(BF16)
            acts[1, half, expert] = dot_nn(rows, w3_buf[expert]).astype(BF16)
            for step, action in after.items():
                pl.when(expert == step)(action)
            return carry

        lax.fori_loop(0, 4, one, 0)

    def grads_out(which, half, expert):
        return pltpu.make_async_copy(grads.at[which, expert], (h_ref, da_ref, db_ref)[which].at[half, :, expert], grads_sem.at[which, half, expert])

    def swap(half, expert):
        return remote(r_send.at[expert], r_got.at[half, expert], swap_send.at[half, expert], swap_recv.at[half, expert], partner)

    def back(half, after):
        def one(expert, carry):
            if half == 0:
                load(2, expert).wait()
            grad_hidden = dot_nt(z_rows[:, expert].reshape(4 * SLOT, 2048), w2_buf[expert])
            parts = swiglu_parts(acts[0, half, expert], acts[1, half, expert], grad_hidden)
            for which in range(3):
                if half == 1:
                    grads_out(which, 0, expert).wait()
                grads[which, expert] = parts[which].reshape(4, SLOT, 512)
                grads_out(which, half, expert).start()
            d_gate, d_up = parts[1], parts[2]

            def rows_back(side, tile):
                at = pl.ds(pl.multiple_of(side * 1024 + tile * 512, 512), 512)
                value = dot_nt(d_gate, w1_buf[expert, at, :]) + dot_nt(d_up, w3_buf[expert, at, :])
                return value.astype(BF16).reshape(4, SLOT, 512)

            if half == 1:
                swap(0, expert).wait_send()
            for tile in range(2):
                r_send[expert, :, :, tile * 512:(tile + 1) * 512] = rows_back(other, tile)
            swap(half, expert).start()
            for tile in range(2):
                r_mine[half, expert, :, :, tile * 512:(tile + 1) * 512] = rows_back(core, tile)
            for step, action in after.items():
                pl.when(expert == step)(action)
            return carry

        lax.fori_loop(0, 4, one, 0)

    def sums_out(role):
        ref, index, which = {6: (give_ref, 0, 0), 7: (give_ref, 0, 1), 2: (give_ref, 1, 0), 5: (give_ref, 1, 1), 4: (keep_ref, 0, 0), 3: (keep_ref, 0, 1), 0: (keep_ref, 1, 0), 1: (keep_ref, 1, 1)}[role]
        return pltpu.make_async_copy(sums.at[role % 4], ref.at[index, which], sums_sem.at[role])

    def total(half):
        for expert in range(4):
            swap(half, expert).wait_recv()
        for at in range(4):
            role = half * 4 + at
            if half == 1:
                sums_out(at).wait()
            sums[at] = dot_tn(picks[role], r_mine[half, :, at].reshape(256, 1024)) + dot_tn(picks_partner[role], r_got[half, :, at ^ 1].reshape(256, 1024))
            sums_out(role).start()

    for which in range(4):
        own(which).start()
    for expert in range(4):
        load(0, expert).start()
        load(1, expert).start()
    for expert in range(4):
        load(2, expert).start()
    barrier = pltpu.get_barrier_semaphore()
    for step in range(1, 8):
        pl.semaphore_signal(barrier, inc=1, device_id={'ep': lax.rem(me + step, 8)}, device_id_type=MESH)
    own(0).wait()
    own(1).wait()
    own(2).wait()
    own(3).wait()
    pl.semaphore_wait(barrier, 7)

    for part in range(2):
        trip(0, part, 0).start()
    for array in range(2):
        for part in range(2):
            trip(array, part, 2).start()
    for role in range(1, 8):
        for which in range(2):
            meta(which, role).start()

    relay_first(0, 0)
    for role in range(1, 8):
        for which in range(2):
            meta(which, role).wait_recv()
    arrived(0, 2)
    pick_x(0, 0, 2)
    relay_first(0, 1)
    arrived(0, 4)
    pick_x(0, 2, 4)

    def rest_x(part):
        relay_rest(0, part)
        trip(1, part, 0).start()

    activations(0, {1: lambda: rest_x(0)})
    arrived(1, 2)
    pick_z(0, 0, 2)
    rest_x(1)
    for at in range(4):
        rows_out(0, 0, at).wait()
    arrived(0, 5)
    pick_x(1, 0, 2)
    arrived(0, 6)
    pick_x(1, 2, 4)
    relay_first(1, 0)
    activations(1, {0: lambda: relay_first(1, 1)})
    arrived(1, 4)
    pick_z(0, 2, 4)
    back(0, {0: lambda: relay_rest(1, 0), 2: lambda: relay_rest(1, 1)})
    total(0)
    for at in range(4):
        rows_out(1, 0, at).wait()
    arrived(1, 5)
    pick_z(1, 0, 2)
    arrived(1, 6)
    pick_z(1, 2, 4)
    back(1, {})
    total(1)

    for array in range(2):
        for part in range(2):
            for kind in range(7):
                trip(array, part, kind).wait_send()
    for role in range(1, 8):
        for which in range(2):
            meta(which, role).wait_send()
    for expert in range(4):
        swap(1, expert).wait_send()
        for which in range(3):
            grads_out(which, 1, expert).wait()
    for at in range(4):
        rows_out(0, 1, at).wait()
        rows_out(1, 1, at).wait()
        sums_out(4 + at).wait()


def rows_backward(x_tokens, dy_tokens, code, gate, w_gate, w_up, w_down):
    tokens, width = x_tokens.shape
    experts, _, inner = w_gate.shape
    hbm = pl.BlockSpec(memory_space=pl.ANY)
    rows = (2, 4, experts, SLOT, width)
    grads = (2, 4, experts, SLOT, inner)
    part = (2, 2, tokens, width // 2)
    dma = pltpu.SemaphoreType.DMA
    outs = (rows, rows, grads, grads, grads)
    return pl.pallas_call(
        rows_kernel,
        out_shape=tuple(jax.ShapeDtypeStruct(s, BF16) for s in outs) + (jax.ShapeDtypeStruct(part, F32),) * 2,
        in_specs=[hbm] * 7,
        out_specs=(hbm,) * 7,
        scratch_shapes=[
            pltpu.VMEM((8, tokens, width), BF16),
            pltpu.VMEM((8, tokens, width), BF16),
            pltpu.VMEM((8,) + code.shape, jnp.int32),
            pltpu.VMEM((8,) + gate.shape, F32),
            pltpu.VMEM((8, 256, tokens), BF16),
            pltpu.VMEM((8, 256, tokens), BF16),
            pltpu.VMEM(rows[1:], BF16),
            pltpu.VMEM(rows[1:], BF16),
            pltpu.VMEM(w_gate.shape, BF16),
            pltpu.VMEM(w_up.shape, BF16),
            pltpu.VMEM(w_down.shape, BF16),
            pltpu.VMEM((2, 2, experts, 4 * SLOT, inner), BF16),
            pltpu.VMEM((3, experts, 4, SLOT, inner), BF16),
            pltpu.VMEM((experts, 4, SLOT, width // 2), BF16),
            pltpu.VMEM((2, experts, 4, SLOT, width // 2), BF16),
            pltpu.VMEM((2, experts, 4, SLOT, width // 2), BF16),
            pltpu.VMEM((4, tokens, width // 2), F32),
            dma((4,)),
            dma((2, 2, 7)),
            dma((2, 2, 7)),
            dma((2, 7)),
            dma((2, 7)),
            dma((3, 4)),
            dma((2, 2, 4)),
            dma((3, 2, 4)),
            dma((2, 4)),
            dma((2, 4)),
            dma((8,)),
        ],
        compiler_params=pltpu.CompilerParams(collective_id=0, has_side_effects=True, vmem_limit_bytes=67000000),
        name='rows_backward',
    )(x_tokens, dy_tokens, code, gate, w_gate, w_up, w_down)


TILES = 4


def weight_kernel(x_ref, z_ref, h_ref, da_ref, db_ref, dw1_ref, dw3_ref, dw2_ref, hidden_t):
    tile = pl.program_id(1)
    rows = 8 * SLOT

    @pl.when(tile == 0)
    def _():
        hidden_t[...] = h_ref[:, 0].reshape(rows, 512).T

    cols = pl.ds(pl.multiple_of(tile * 512, 512), 512)
    x_cols_t = x_ref[:, 0, :, cols].reshape(rows, 512).T
    dw1_ref[0] = dot_nn(x_cols_t, da_ref[:, 0].reshape(rows, 512))
    dw3_ref[0] = dot_nn(x_cols_t, db_ref[:, 0].reshape(rows, 512))
    dw2_ref[0] = dot_nn(hidden_t[...], z_ref[:, 0, :, cols].reshape(rows, 512))


def weight_grads(x_rows, z_rows, hidden, d_gate, d_up):
    _, experts, _, width = x_rows.shape
    inner = hidden.shape[3]
    by_expert = lambda e, t: (0, e, 0, 0)
    row_spec = pl.BlockSpec((8, 1, SLOT, width), by_expert)
    act_spec = pl.BlockSpec((8, 1, SLOT, inner), by_expert)
    return pl.pallas_call(
        weight_kernel,
        grid=(experts, TILES),
        out_shape=(
            jax.ShapeDtypeStruct((experts, width, inner), F32),
            jax.ShapeDtypeStruct((experts, width, inner), F32),
            jax.ShapeDtypeStruct((experts, inner, width), F32),
        ),
        in_specs=[row_spec, row_spec, act_spec, act_spec, act_spec],
        out_specs=(
            pl.BlockSpec((1, width // TILES, inner), lambda e, t: (e, t, 0)),
            pl.BlockSpec((1, width // TILES, inner), lambda e, t: (e, t, 0)),
            pl.BlockSpec((1, inner, width // TILES), lambda e, t: (e, 0, t)),
        ),
        scratch_shapes=[pltpu.VMEM((inner, 8 * SLOT), BF16)],
        compiler_params=pltpu.CompilerParams(dimension_semantics=('arbitrary', 'arbitrary'), vmem_limit_bytes=50000000),
        cost_estimate=pl.CostEstimate(flops=12_900_000_000, bytes_accessed=70_000_000, transcendentals=0),
        name='weight_grads',
    )(x_rows, z_rows, hidden, d_gate, d_up)


def shared_kernel(x_ref, dy_ref, w1_ref, w3_ref, w2_ref, dx_ref, dw1_ref, dw3_ref, dw2_ref, hidden_t, grad_gate, grad_up):
    tile = pl.program_id(0)

    @pl.when(tile == 0)
    def _():
        act_gate = dot_nn(x_ref[...], w1_ref[...]).astype(BF16)
        act_up = dot_nn(x_ref[...], w3_ref[...]).astype(BF16)
        hidden, d_gate, d_up = swiglu_parts(act_gate, act_up, dot_nt(dy_ref[...], w2_ref[...]))
        hidden_t[...] = hidden.T
        grad_gate[...] = d_gate
        grad_up[...] = d_up

    cols = pl.ds(pl.multiple_of(tile * 512, 512), 512)
    dx_ref[...] = dot_nt(grad_gate[...], w1_ref[cols, :]) + dot_nt(grad_up[...], w3_ref[cols, :])
    x_cols_t = x_ref[:, cols].T
    dw1_ref[0] = dot_nn(x_cols_t, grad_gate[...])
    dw3_ref[0] = dot_nn(x_cols_t, grad_up[...])
    dw2_ref[0] = dot_nn(hidden_t[...], dy_ref[:, cols])


def shared_backward(x_tokens, dy_tokens, shared_gate, shared_up, shared_down):
    tokens, width = x_tokens.shape
    inner = shared_gate.shape[1]
    vmem = pl.BlockSpec(memory_space=pltpu.VMEM)
    step = width // TILES
    return pl.pallas_call(
        shared_kernel,
        grid=(TILES,),
        out_shape=(
            jax.ShapeDtypeStruct((tokens, width), F32),
            jax.ShapeDtypeStruct((1, width, inner), F32),
            jax.ShapeDtypeStruct((1, width, inner), F32),
            jax.ShapeDtypeStruct((1, inner, width), F32),
        ),
        in_specs=[vmem] * 5,
        out_specs=(
            pl.BlockSpec((tokens, step), lambda t: (0, t)),
            pl.BlockSpec((1, step, inner), lambda t: (0, t, 0)),
            pl.BlockSpec((1, step, inner), lambda t: (0, t, 0)),
            pl.BlockSpec((1, inner, step), lambda t: (0, 0, t)),
        ),
        scratch_shapes=[
            pltpu.VMEM((inner, tokens), BF16),
            pltpu.VMEM((tokens, inner), BF16),
            pltpu.VMEM((tokens, inner), BF16),
        ],
        compiler_params=pltpu.CompilerParams(dimension_semantics=('arbitrary',), vmem_limit_bytes=40000000),
        cost_estimate=pl.CostEstimate(flops=6_000_000_000, bytes_accessed=20_000_000, transcendentals=0),
        name='shared_backward',
    )(x_tokens, dy_tokens, shared_gate, shared_up, shared_down)


def partners(kind):
    pairs = []
    for me in range(8):
        core = me % 2
        along_x, along_y = me ^ 2, me ^ 4
        first, second = (along_x, along_y) if core == 0 else (along_y, along_x)
        pairs.append((me, {'first': first, 'second': second, 'chip': me ^ 1}[kind]))
    return pairs


def solution(mesh):
    token_spec = P(('dp', 'ep'), None)
    expert_spec = P('ep', None, None)
    whole_spec = P(None, None)
    grad_spec = P(('dp', 'ep'), None, None)

    def local_backward(x_tokens, dy_tokens, expert_ids, gate_vals, slot_pos, w_gate, w_up, w_down, shared_gate, shared_up, shared_down):
        code = jnp.where(slot_pos >= 0, expert_ids * SLOT + slot_pos, -1)
        code = jnp.pad(code.T, ((0, 6), (0, 0)), constant_values=-1)
        gate = jnp.pad(gate_vals.T, ((0, 6), (0, 0)))
        *saved, give, keep = rows_backward(x_tokens, dy_tokens, code, gate, w_gate, w_up, w_down)
        saved = [rows.reshape((8,) + rows.shape[2:]) for rows in saved]
        got = lax.ppermute(give, 'ep', partners('first'))
        grads = weight_grads(*saved)
        got, grad_w_gate, grad_w_up, grad_w_down = lax.optimization_barrier((got,) + tuple(grads))
        onward = keep[0] + got[0]
        got_second = lax.ppermute(onward, 'ep', partners('second'))
        x_late, dy_late, _ = lax.optimization_barrier((x_tokens, dy_tokens, onward))
        shared_dx, grad_shared_gate, grad_shared_up, grad_shared_down = shared_backward(x_late, dy_late, shared_gate, shared_up, shared_down)
        got_second, shared_dx = lax.optimization_barrier((got_second, shared_dx))
        mine = keep[1] + got[1] + got_second
        swapped = lax.ppermute(mine[1], 'ep', partners('chip'))
        own = mine[0]
        core = lax.rem(lax.axis_index('ep'), 2)
        left = jnp.where(core == 0, own, swapped)
        right = jnp.where(core == 0, swapped, own)
        grad_x = (jnp.concatenate((left, right), axis=1) + shared_dx).astype(BF16)
        return grad_x, grad_w_gate, grad_w_up, grad_w_down, grad_shared_gate, grad_shared_up, grad_shared_down

    return jax.shard_map(local_backward, mesh=mesh, in_specs=(token_spec, token_spec, token_spec, token_spec, token_spec, expert_spec, expert_spec, expert_spec, whole_spec, whole_spec, whole_spec), out_specs=(token_spec, grad_spec, grad_spec, grad_spec, grad_spec, grad_spec, grad_spec), check_vma=False)
```

time: 487 us -> 129 us (0.26); the launches traced: 480 us -> 128 us
  matrix products: 173 us -> 0 us
  local copies, waits for them, and re-layouts: 147 us -> 7.92 us
  waiting for transfers between devices: 118 us -> 7.09 us
  Pallas kernels: 0 us -> 107 us
  other arithmetic: 25.5 us -> 2.13 us
  starting transfers between devices: 16 us -> 3.02 us
    dot_general x16 -> x0, matrix products: 173 us -> none  [the longest x1 31.5 us: local_backward(): jnp.einsum('erd,erf->edf', x_exp, grad_gate, preferred_element_type=jnp.f...]
    all_to_all x3 -> x0, waiting for transfers between devices: 118 us -> none  [the longest x1 63.6 us: local_backward(): x_exp = lax.all_to_all(send_x, 'ep', 0, 1, tiled=True)]
    pallas_call x0 -> x3, Pallas kernels: none -> 107 us  [the longest x1 69.1 us: rows_backward(): pl.pallas_call(rows_kernel, out_shape=tuple((jax.ShapeDtypeStruct(s, BF16...]
    gather x4 -> x0, local copies, waits for them, and re-layouts: 50.9 us -> none  [take_rows(): return jnp.take(rows, row_index, axis=0, mode='fill', fill_value=0)]
    all_to_all x3 -> x0, local copies, waits for them, and re-layouts: 32.4 us -> none  [the longest x1 11.6 us: local_backward(): dz_exp = lax.all_to_all(send_dz, 'ep', 0, 1, tiled=True)]
    reshape x6 -> x0, local copies, waits for them, and re-layouts: 27.8 us -> none  [the longest x1 9.18 us: local_backward(): lax.all_to_all(grad_exp, 'ep', 1, 0, tiled=True)]
    all_to_all x3 -> x0, starting transfers between devices: 16 us -> none  [the longest x1 5.59 us: local_backward(): x_exp = lax.all_to_all(send_x, 'ep', 0, 1, tiled=True)]
    convert_element_type x1 -> x0, local copies, waits for them, and re-layouts: 12.5 us -> none  [local_backward(): (jnp.einsum('erf,edf->erd', grad_gate, w_gate, preferred_element_type=jnp...]
  transfers between devices with their start and end apart: 3 -> 3, of which waited for: 2 -> 2; matrix products, arithmetic and copies ran while one was open for 36% -> 0% of each run, Pallas kernels for 0% -> 30%
where the time goes in v4:
time: 129 us; the launch traced here: 128 us
  Pallas kernels  107 us (83%)
  local copies, waits for them, and re-layouts  7.92 us (6%)
  waiting for transfers between devices  7.09 us (5%)
  starting transfers between devices  3.02 us (2%)
  other arithmetic  2.13 us (2%)
    pallas_call x1, Pallas kernels, rows_backward(): pl.pallas_call(rows_kernel, out_shape=tuple((jax.ShapeDtypeStruct(s, BF16...  69.1 us
    pallas_call x1, Pallas kernels, weight_grads(): pl.pallas_call(weight_kernel, grid=(experts, TILES), out_shape=(jax.Shape...  30.7 us
    pallas_call x1, Pallas kernels, shared_backward(): pl.pallas_call(shared_kernel, grid=(TILES,), out_shape=(jax.ShapeDtypeStr...  7.54 us
    unnamed x22, local copies, waits for them, and re-layouts  5.98 us
    ppermute x1, waiting for transfers between devices, local_backward(): got_second = lax.ppermute(onward, 'ep', partners('second'))  5.2 us
    ppermute x1, starting transfers between devices, local_backward(): got_second = lax.ppermute(onward, 'ep', partners('second'))  2.6 us
  transfers between devices with their start and end apart: 3, of which 2 were waited for; matrix products, arithmetic and copies ran while one was open for 0% of the time, Pallas kernels for 30%

profile of v4, /device:TPU:0, one launch (start us, length us, event | category | flops | bytes accessed | tf_op | source)
XLA Modules:
  0.0 128.3 jit_solution(14496132661045999222)
XLA Ops:
  0.6 0.7 select_bitcast_fusion
  1.4 0.6 pad.8.code_ref
  2.0 1.3 %pad.9.gate_ref = f32[16,128]{1,0:T(8,128)} pad(f32[10,128]{1,0:T(8,128)} %bitcast.23, f32[]{:T(128)} %constant.16.clone.1), padding=0_6x0_0 | pad | bytes 13316 | tf_op jit(solution)/shard_map/jit(_pad)/pad | solution.py:451
  3.3 69.1 %rows_backward.1 = (bf16[2,4,4,64,2048]{4,3,2,1,0:T(8,128)(2,1)}, bf16[2,4,4,64,2048]{4,3,2,1,0:T(8,128)(2,1)}, bf16[2,4,4,64,512]{4,3,2,1,0:T(8,128)(2,1)}, bf1...) custom-call(bf16[128,2048]{1,0:T(8,128)(2,1)} %x_ref.2, ...), custom_call_target="tpu_custom_call" | custom-call | tf_op jit(solution)/shard_map/rows_backward/pallas_call | solution.py:295
  72.4 0.4 collective-permute-start
  72.8 0.0 copy-start.5
  72.8 1.6 %copy-done.5 = bf16[2,4,4,64,512]{4,3,2,1,0:T(8,128)(2,1)S(1)} copy-done((bf16[2,4,4,64,512]{4,3,2,1,0:T(8,128)(2,1)S(1)}, bf16[2,4,4,64,512]{4,3,2,1,0:T(8,128)(2,1)}, u32[]{:S(2)}) %copy-start.5) | copy-done | bytes 2097176
  74.4 0.0 copy-start.6
  74.4 1.6 %copy-done.6 = bf16[2,4,4,64,512]{4,3,2,1,0:T(8,128)(2,1)S(1)} copy-done((bf16[2,4,4,64,512]{4,3,2,1,0:T(8,128)(2,1)S(1)}, bf16[2,4,4,64,512]{4,3,2,1,0:T(8,128)(2,1)}, u32[]{:S(2)}) %copy-start.6) | copy-done | bytes 2097176
  75.9 0.0 copy-start.7
  75.9 1.6 %copy-done.7 = bf16[2,4,4,64,512]{4,3,2,1,0:T(8,128)(2,1)S(1)} copy-done((bf16[2,4,4,64,512]{4,3,2,1,0:T(8,128)(2,1)S(1)}, bf16[2,4,4,64,512]{4,3,2,1,0:T(8,128)(2,1)}, u32[]{:S(2)}) %copy-start.7) | copy-done | bytes 2097176
  77.5 30.7 %weight_grads.1 = (f32[4,2048,512]{2,1,0:T(8,128)}, f32[4,2048,512]{2,1,0:T(8,128)}, f32[4,512,2048]{2,1,0:T(8,128)}) custom-call(bf16[8,4,64,2048]{3,2,1,0:T(8,128)(2,1)} %bitcast.24, bf16[8,4,64,2048]{3,2,1,0:T(8,128)(2,1)} %bitcast.25, bf16[8,4,64,512]{3,2,1,0:T(8,128)(2,1)S(1)} %bitcast.20, bf16[8,4,64,512]{3,2,1,0:T(8,128)(2,1)S(1)} %bitcast.21, ...), custom_call_target="tpu_custom_call" | custom-call | flops 12899999744 | bytes 70000000 | tf_op jit(solution)/shard_map/weight_grads/pallas_call | solution.py:359
  108.3 0.0 collective-permute-done
  108.3 0.0 copy-start.9
  108.3 0.0 copy-done.8
  108.3 0.1 add_bitcast_fusion
  108.4 1.2 copy-done.9
  109.6 2.6 %collective-permute-start.1 = (f32[2,128,1024]{2,1,0:T(8,128)S(1)}, f32[2,128,1024]{2,1,0:T(8,128)S(1)}, u32[]{:S(2)}, u32[]{:S(2)}) collective-permute-start(f32[2,128,1024]{2,1,0:T(8,128)S(1)} %add_bitcast_fusion), channel_id=1, source_target_pairs={{0,4},{1,3},{2,6},{3,1},{4,0},{5,7},{6,2},{7,5},{8,12},{9,11},{10,... | collective-permute-start | bytes 3145736 | tf_op jit(solution)/shard_map/ppermute | solution.py:458
  112.2 0.0 copy-done.3
  112.2 0.0 copy-done.4
  112.2 0.0 copy-done
  112.2 0.0 copy-done.1
  112.2 0.0 copy-done.2
  112.3 0.0 copy-start.10
  112.3 7.5 %shared_backward.1 = (f32[128,2048]{1,0:T(8,128)S(1)}, f32[1,2048,512]{2,1,0:T(8,128)}, f32[1,2048,512]{2,1,0:T(8,128)}, f32[1,512,2048]{2,1,0:T(8,128)}) custom-call(bf16[128,2048]{1,0:T(8,128)(2,1)S(1)} %copy-done, bf16[128,2048]{1,0:T(8,128)(2,1)S(1)} %copy-done.1, bf16[2048,512]{1,0:T(8,128)(2,1)S(1)} %copy-done.2, bf16[2048,512]{1,0:T(8,128)(2,1)S(1)} %copy-done.3, ...), custom_call_target="tpu_custom_call" | custom-call | flops 6000000000 | bytes 20000000 | tf_op jit(solution)/shard_map/shared_backward/pallas_call | solution.py:405
  119.8 5.2 %collective-permute-done.1 = f32[2,128,1024]{2,1,0:T(8,128)S(1)} collective-permute-done((f32[2,128,1024]{2,1,0:T(8,128)S(1)}, f32[2,128,1024]{2,1,0:T(8,128)S(1)}, u32[]{:S(2)}, u32[]{:S(2)}) %collective-permute-start.1) | collective-permute-done | bytes 1048608 | tf_op jit(solution)/shard_map/ppermute | solution.py:458
  125.0 0.0 copy-done.10
  125.0 0.3 bitcast_add_fusion
  125.3 0.0 collective-permute-start.2
  125.4 1.9 %collective-permute-done.2 = f32[128,1024]{1,0:T(8,128)S(1)} collective-permute-done((f32[128,1024]{1,0:T(8,128)S(1)}, f32[128,1024]{1,0:T(8,128)S(1)}, u32[]{:S(2)}, u32[]{:S(2)}) %collective-permute-start.2) | collective-permute-done | bytes 524320 | tf_op jit(solution)/shard_map/ppermute | solution.py:463
  127.3 0.1 fusion.2
  127.4 0.9 fusion
  (7 shorter events, 0.1 us)
Async XLA Ops:
  72.4 35.9 %collective-permute-start = (f32[2,2,128,1024]{3,2,1,0:T(8,128)}, f32[2,2,128,1024]{3,2,1,0:T(8,128)S(1)}, u32[]{:S(2)}, u32[]{:S(2)}) collective-permute-start(f32[2,2,128,1024]{3,2,1,0:T(8,128)} %get-tuple-element.30), channel_id=1, source_target_pairs={{0,2},{1,5},{2,0},{3,7},{4,6},{5,1},{6,4},{7,3},{8,10},{9,13},{10,... | collective-permute-start | bytes 6291464 | tf_op jit(solution)/shard_map/ppermute | solution.py:454
  72.8 1.6 %copy-start.5 = (bf16[2,4,4,64,512]{4,3,2,1,0:T(8,128)(2,1)S(1)}, bf16[2,4,4,64,512]{4,3,2,1,0:T(8,128)(2,1)}, u32[]{:S(2)}) copy-start(bf16[2,4,4,64,512]{4,3,2,1,0:T(8,128)(2,1)} %get-tuple-element.33) | copy-start | bytes 6291460
  74.4 1.6 %copy-start.6 = (bf16[2,4,4,64,512]{4,3,2,1,0:T(8,128)(2,1)S(1)}, bf16[2,4,4,64,512]{4,3,2,1,0:T(8,128)(2,1)}, u32[]{:S(2)}) copy-start(bf16[2,4,4,64,512]{4,3,2,1,0:T(8,128)(2,1)} %get-tuple-element.34) | copy-start | bytes 6291460
  75.9 1.6 %copy-start.7 = (bf16[2,4,4,64,512]{4,3,2,1,0:T(8,128)(2,1)S(1)}, bf16[2,4,4,64,512]{4,3,2,1,0:T(8,128)(2,1)}, u32[]{:S(2)}) copy-start(bf16[2,4,4,64,512]{4,3,2,1,0:T(8,128)(2,1)} %get-tuple-element.35) | copy-start | bytes 6291460
  77.5 30.8 %copy-start.8 = (f32[2,2,128,1024]{3,2,1,0:T(8,128)S(1)}, f32[2,2,128,1024]{3,2,1,0:T(8,128)}, u32[]{:S(2)}) copy-start(f32[2,2,128,1024]{3,2,1,0:T(8,128)} %get-tuple-element.29) | copy-start | bytes 6291460
  77.5 34.7 %copy-start.3 = (bf16[2048,512]{1,0:T(8,128)(2,1)S(1)}, bf16[2048,512]{1,0:T(8,128)(2,1)}, u32[]{:S(2)}) copy-start(bf16[2048,512]{1,0:T(8,128)(2,1)} %w3_ref.3) | copy-start | bytes 6291460
  77.5 34.7 %copy-start.4 = (bf16[512,2048]{1,0:T(8,128)(2,1)S(1)}, bf16[512,2048]{1,0:T(8,128)(2,1)}, u32[]{:S(2)}) copy-start(bf16[512,2048]{1,0:T(8,128)(2,1)} %w2_ref.3) | copy-start | bytes 6291460
  108.3 4.0 %copy-start = (bf16[128,2048]{1,0:T(8,128)(2,1)S(1)}, bf16[128,2048]{1,0:T(8,128)(2,1)}, u32[]{:S(2)}) copy-start(bf16[128,2048]{1,0:T(8,128)(2,1)} %x_ref.2) | copy-start | bytes 1572868
  108.3 4.0 %copy-start.1 = (bf16[128,2048]{1,0:T(8,128)(2,1)S(1)}, bf16[128,2048]{1,0:T(8,128)(2,1)}, u32[]{:S(2)}) copy-start(bf16[128,2048]{1,0:T(8,128)(2,1)} %dy_ref.2) | copy-start | bytes 1572868
  108.3 4.0 %copy-start.2 = (bf16[2048,512]{1,0:T(8,128)(2,1)S(1)}, bf16[2048,512]{1,0:T(8,128)(2,1)}, u32[]{:S(2)}) copy-start(bf16[2048,512]{1,0:T(8,128)(2,1)} %w1_ref.3) | copy-start | bytes 6291460
  108.3 1.3 %copy-start.9 = (f32[2,2,128,1024]{3,2,1,0:T(8,128)}, f32[2,2,128,1024]{3,2,1,0:T(8,128)S(1)}, u32[]{:S(2)}) copy-start(f32[2,2,128,1024]{3,2,1,0:T(8,128)S(1)} %collective-permute-done) | copy-start | bytes 6291460
  109.6 15.4 %collective-permute-start.1 = (f32[2,128,1024]{2,1,0:T(8,128)S(1)}, f32[2,128,1024]{2,1,0:T(8,128)S(1)}, u32[]{:S(2)}, u32[]{:S(2)}) collective-permute-start(f32[2,128,1024]{2,1,0:T(8,128)S(1)} %add_bitcast_fusion), channel_id=1, source_target_pairs={{0,4},{1,3},{2,6},{3,1},{4,0},{5,7},{6,2},{7,5},{8,12},{9,11},{10,... | collective-permute-start | bytes 3145736 | tf_op jit(solution)/shard_map/ppermute | solution.py:458
  112.3 12.8 %copy-start.10 = (f32[2,2,128,1024]{3,2,1,0:T(8,128)S(1)}, f32[2,2,128,1024]{3,2,1,0:T(8,128)}, u32[]{:S(2)}) copy-start(f32[2,2,128,1024]{3,2,1,0:T(8,128)} %copy-done.9) | copy-start | bytes 6291460
  125.3 1.9 %collective-permute-start.2 = (f32[128,1024]{1,0:T(8,128)S(1)}, f32[128,1024]{1,0:T(8,128)S(1)}, u32[]{:S(2)}, u32[]{:S(2)}) collective-permute-start(f32[128,1024]{1,0:T(8,128)S(1)} %slice_bitcast_fusion), channel_id=1, source_target_pairs={{0,1},{1,0},{2,3},{3,2},{4,5},{5,4},{6,7},{7,6},{8,9},{9,8},{10,11... | collective-permute-start | bytes 1572872 | tf_op jit(solution)/shard_map/ppermute | solution.py:463

commit v5 on v4

--- a/solution.py
+++ b/solution.py
@@ -218,44 +218,47 @@
     own(3).wait()
     pl.semaphore_wait(barrier, 7)
 
+    for role in range(1, 8):
+        for which in range(2):
+            meta(which, role).start()
     for part in range(2):
         trip(0, part, 0).start()
     for array in range(2):
         for part in range(2):
             trip(array, part, 2).start()
-    for role in range(1, 8):
-        for which in range(2):
-            meta(which, role).start()
-
-    relay_first(0, 0)
+
+    pick_x(0, 0, 1)
+    pick_z(0, 0, 1)
     for role in range(1, 8):
         for which in range(2):
             meta(which, role).wait_recv()
     arrived(0, 2)
-    pick_x(0, 0, 2)
+    pick_x(0, 1, 2)
+    relay_first(0, 0)
+    arrived(1, 2)
+    pick_z(0, 1, 2)
     relay_first(0, 1)
+    trip(1, 0, 0).start()
     arrived(0, 4)
     pick_x(0, 2, 4)
 
-    def rest_x(part):
-        relay_rest(0, part)
-        trip(1, part, 0).start()
-
-    activations(0, {1: lambda: rest_x(0)})
-    arrived(1, 2)
-    pick_z(0, 0, 2)
-    rest_x(1)
+    def rest_x():
+        relay_rest(0, 0)
+        trip(1, 1, 0).start()
+
+    activations(0, {1: rest_x, 3: lambda: relay_first(1, 0)})
+    relay_rest(0, 1)
     for at in range(4):
         rows_out(0, 0, at).wait()
     arrived(0, 5)
     pick_x(1, 0, 2)
     arrived(0, 6)
     pick_x(1, 2, 4)
-    relay_first(1, 0)
-    activations(1, {0: lambda: relay_first(1, 1)})
+    relay_first(1, 1)
+    activations(1, {2: lambda: relay_rest(1, 0)})
     arrived(1, 4)
     pick_z(0, 2, 4)
-    back(0, {0: lambda: relay_rest(1, 0), 2: lambda: relay_rest(1, 1)})
+    back(0, {2: lambda: relay_rest(1, 1)})
     total(0)
     for at in range(4):
         rows_out(1, 0, at).wait()
@@ -332,7 +335,7 @@
     )(x_tokens, dy_tokens, code, gate, w_gate, w_up, w_down)
 
 
-TILES = 4
+WEIGHT_TILES = 1
 
 
 def weight_kernel(x_ref, z_ref, h_ref, da_ref, db_ref, dw1_ref, dw3_ref, dw2_ref, hidden_t):
@@ -343,11 +346,14 @@
     def _():
         hidden_t[...] = h_ref[:, 0].reshape(rows, 512).T
 
-    cols = pl.ds(pl.multiple_of(tile * 512, 512), 512)
-    x_cols_t = x_ref[:, 0, :, cols].reshape(rows, 512).T
-    dw1_ref[0] = dot_nn(x_cols_t, da_ref[:, 0].reshape(rows, 512))
-    dw3_ref[0] = dot_nn(x_cols_t, db_ref[:, 0].reshape(rows, 512))
-    dw2_ref[0] = dot_nn(hidden_t[...], z_ref[:, 0, :, cols].reshape(rows, 512))
+    wide = 2048 // WEIGHT_TILES
+    for piece in range(wide // 512):
+        at = slice(piece * 512, piece * 512 + 512)
+        cols = pl.ds(pl.multiple_of(tile * wide + piece * 512, 512), 512)
+        x_cols_t = x_ref[:, 0, :, cols].reshape(rows, 512).T
+        dw1_ref[0, at, :] = dot_nn(x_cols_t, da_ref[:, 0].reshape(rows, 512))
+        dw3_ref[0, at, :] = dot_nn(x_cols_t, db_ref[:, 0].reshape(rows, 512))
+        dw2_ref[0, :, at] = dot_nn(hidden_t[...], z_ref[:, 0, :, cols].reshape(rows, 512))
 
 
 def weight_grads(x_rows, z_rows, hidden, d_gate, d_up):
@@ -358,7 +364,7 @@
     act_spec = pl.BlockSpec((8, 1, SLOT, inner), by_expert)
     return pl.pallas_call(
         weight_kernel,
-        grid=(experts, TILES),
+        grid=(experts, WEIGHT_TILES),
         out_shape=(
             jax.ShapeDtypeStruct((experts, width, inner), F32),
             jax.ShapeDtypeStruct((experts, width, inner), F32),
@@ -366,15 +372,18 @@
         ),
         in_specs=[row_spec, row_spec, act_spec, act_spec, act_spec],
         out_specs=(
-            pl.BlockSpec((1, width // TILES, inner), lambda e, t: (e, t, 0)),
-            pl.BlockSpec((1, width // TILES, inner), lambda e, t: (e, t, 0)),
-            pl.BlockSpec((1, inner, width // TILES), lambda e, t: (e, 0, t)),
+            pl.BlockSpec((1, width // WEIGHT_TILES, inner), lambda e, t: (e, t, 0)),
+            pl.BlockSpec((1, width // WEIGHT_TILES, inner), lambda e, t: (e, t, 0)),
+            pl.BlockSpec((1, inner, width // WEIGHT_TILES), lambda e, t: (e, 0, t)),
         ),
         scratch_shapes=[pltpu.VMEM((inner, 8 * SLOT), BF16)],
-        compiler_params=pltpu.CompilerParams(dimension_semantics=('arbitrary', 'arbitrary'), vmem_limit_bytes=50000000),
+        compiler_params=pltpu.CompilerParams(dimension_semantics=('arbitrary', 'arbitrary'), vmem_limit_bytes=67000000),
         cost_estimate=pl.CostEstimate(flops=12_900_000_000, bytes_accessed=70_000_000, transcendentals=0),
         name='weight_grads',
     )(x_rows, z_rows, hidden, d_gate, d_up)
+
+
+SHARED_TILES = 4
 
 
 def shared_kernel(x_ref, dy_ref, w1_ref, w3_ref, w2_ref, dx_ref, dw1_ref, dw3_ref, dw2_ref, hidden_t, grad_gate, grad_up):
@@ -401,10 +410,10 @@
     tokens, width = x_tokens.shape
     inner = shared_gate.shape[1]
     vmem = pl.BlockSpec(memory_space=pltpu.VMEM)
-    step = width // TILES
+    step = width // SHARED_TILES
     return pl.pallas_call(
         shared_kernel,
-        grid=(TILES,),
+        grid=(SHARED_TILES,),
         out_shape=(
             jax.ShapeDtypeStruct((tokens, width), F32),
             jax.ShapeDtypeStruct((1, width, inner), F32),
@@ -423,7 +432,7 @@
             pltpu.VMEM((tokens, inner), BF16),
             pltpu.VMEM((tokens, inner), BF16),
         ],
-        compiler_params=pltpu.CompilerParams(dimension_semantics=('arbitrary',), vmem_limit_bytes=40000000),
+        compiler_params=pltpu.CompilerParams(dimension_semantics=('arbitrary',), vmem_limit_bytes=67000000),
         cost_estimate=pl.CostEstimate(flops=6_000_000_000, bytes_accessed=20_000_000, transcendentals=0),
         name='shared_backward',
     )(x_tokens, dy_tokens, shared_gate, shared_up, shared_down)

time: 129 us -> 125 us (0.969)
  local copies, waits for them, and re-layouts: 7.92 us -> 1.95 us
  other arithmetic: 2.13 us -> 6.56 us
  waiting for transfers between devices: 7.09 us -> 5.78 us
    unnamed x22 -> x2, local copies, waits for them, and re-layouts: 5.98 us -> 0.01 us
    add x1, other arithmetic: 0.14 us -> 2.71 us  [local_backward(): onward = keep[0] + got[0]]
    pallas_call x1, Pallas kernels: 69.1 us -> 71.1 us  [rows_backward(): pl.pallas_call(rows_kernel, out_shape=tuple((jax.ShapeDtypeStruct(s, BF16...]
    ppermute x1, starting transfers between devices: 2.6 us -> 0.69 us  [local_backward(): got_second = lax.ppermute(onward, 'ep', partners('second'))]
    add x1, other arithmetic: 0.27 us -> 2.12 us  [local_backward(): mine = keep[1] + got[1] + got_second]
    pallas_call x2, Pallas kernels: 38.3 us -> 36.5 us  [the longest x1 26.3 us: weight_grads(): pl.pallas_call(weight_kernel, grid=(experts, WEIGHT_TILES), out_shape=(ja...]
    ppermute x1, waiting for transfers between devices: 5.2 us -> 3.89 us  [local_backward(): got_second = lax.ppermute(onward, 'ep', partners('second'))]
  transfers between devices with their start and end apart: 3 -> 3, of which waited for: 2 -> 2; matrix products, arithmetic and copies ran while one was open for 0% -> 0% of each run, Pallas kernels for 30% -> 29%
where the time goes in v5:
time: 125 us
  Pallas kernels  108 us (86%)
  other arithmetic  6.56 us (5%)
  waiting for transfers between devices  5.78 us (5%)
  local copies, waits for them, and re-layouts  1.95 us (2%)
  starting transfers between devices  1.88 us (2%)
    pallas_call x1, Pallas kernels, rows_backward(): pl.pallas_call(rows_kernel, out_shape=tuple((jax.ShapeDtypeStruct(s, BF16...  71.1 us
    pallas_call x1, Pallas kernels, weight_grads(): pl.pallas_call(weight_kernel, grid=(experts, WEIGHT_TILES), out_shape=(ja...  26.3 us
    pallas_call x1, Pallas kernels, shared_backward(): pl.pallas_call(shared_kernel, grid=(SHARED_TILES,), out_shape=(jax.ShapeD...  10.2 us
    ppermute x1, waiting for transfers between devices, local_backward(): got_second = lax.ppermute(onward, 'ep', partners('second'))  3.89 us
    add x1, other arithmetic, local_backward(): onward = keep[0] + got[0]  2.71 us
  transfers between devices with their start and end apart: 3, of which 2 were waited for; matrix products, arithmetic and copies ran while one was open for 0% of the time, Pallas kernels for 29%

profile of v5, /device:TPU:0, one launch (start us, length us, event | category | flops | bytes accessed | tf_op | source)
XLA Modules:
  0.0 124.5 jit_solution(12894482097415182747)
XLA Ops:
  0.6 0.7 select_bitcast_fusion
  1.4 0.6 pad.8.code_ref
  2.0 1.3 %pad.9.gate_ref = f32[16,128]{1,0:T(8,128)} pad(f32[10,128]{1,0:T(8,128)} %bitcast.20, f32[]{:T(128)} %constant.16.clone.1), padding=0_6x0_0 | pad | bytes 13316 | tf_op jit(solution)/shard_map/jit(_pad)/pad | solution.py:460
  3.3 71.1 %rows_backward.1 = (bf16[2,4,4,64,2048]{4,3,2,1,0:T(8,128)(2,1)}, bf16[2,4,4,64,2048]{4,3,2,1,0:T(8,128)(2,1)}, bf16[2,4,4,64,512]{4,3,2,1,0:T(8,128)(2,1)}, bf1...) custom-call(bf16[128,2048]{1,0:T(8,128)(2,1)} %x_ref.2, ...), custom_call_target="tpu_custom_call" | custom-call | tf_op jit(solution)/shard_map/rows_backward/pallas_call | solution.py:298
  74.4 1.1 collective-permute-start
  75.5 26.3 %weight_grads.1 = (f32[4,2048,512]{2,1,0:T(8,128)}, f32[4,2048,512]{2,1,0:T(8,128)}, f32[4,512,2048]{2,1,0:T(8,128)}) custom-call(bf16[8,4,64,2048]{3,2,1,0:T(8,128)(2,1)} %bitcast.21, bf16[8,4,64,2048]{3,2,1,0:T(8,128)(2,1)} %bitcast.22, bf16[8,4,64,512]{3,2,1,0:T(8,128)(2,1)} %bitcast.23, bf16[8,4,64,512]{3,2,1,0:T(8,128)(2,1)} %bitcast.24, ...), custom_call_target="tpu_custom_call" | custom-call | flops 12899999744 | bytes 70000000 | tf_op jit(solution)/shard_map/weight_grads/pallas_call | solution.py:365
  101.8 0.0 collective-permute-done
  101.8 2.7 %add_bitcast_fusion = f32[2,128,1024]{2,1,0:T(8,128)} fusion(f32[2,2,128,1024]{3,2,1,0:T(8,128)} %collective-permute-done, f32[2,2,128,1024]{3,2,1,0:T(8,128)} %get-tuple-element.29), kind=kLoop, calls=%fused_computation.3 | loop fusion | flops 262144 | bytes 3145728 | tf_op jit(solution)/shard_map/add | solution.py:466
  104.5 0.7 collective-permute-start.1
  105.2 10.2 %shared_backward.1 = (f32[128,2048]{1,0:T(8,128)}, f32[1,2048,512]{2,1,0:T(8,128)}, f32[1,2048,512]{2,1,0:T(8,128)}, f32[1,512,2048]{2,1,0:T(8,128)}) custom-call(bf16[128,2048]{1,0:T(8,128)(2,1)} %x_ref.2, bf16[128,2048]{1,0:T(8,128)(2,1)} %dy_ref.2, bf16[2048,512]{1,0:T(8,128)(2,1)} %w1_ref.3, bf16[2048,512]{1,0:T(8,128)(2,1)} %w3_ref.3, ...), custom_call_target="tpu_custom_call" | custom-call | flops 6000000000 | bytes 20000000 | tf_op jit(solution)/shard_map/shared_backward/pallas_call | solution.py:414
  115.5 3.9 %collective-permute-done.1 = f32[2,128,1024]{2,1,0:T(8,128)} collective-permute-done((f32[2,128,1024]{2,1,0:T(8,128)}, f32[2,128,1024]{2,1,0:T(8,128)}, u32[]{:S(2)}, u32[]{:S(2)}) %collective-permute-start.1) | collective-permute-done | bytes 1048608 | tf_op jit(solution)/shard_map/ppermute | solution.py:467
  119.3 2.1 %bitcast_add_fusion = f32[2,128,1024]{2,1,0:T(8,128)S(1)} fusion(f32[2,128,1024]{2,1,0:T(8,128)} %collective-permute-done.1, f32[2,2,128,1024]{3,2,1,0:T(8,128)} %collective-permute-done, f32[2,2,128,1024]{3,2,1,0:T(8,128)} %get-tuple-element.29), kind=kLoop, calls=%fused_computation.2 | loop fusion | flops 524288 | bytes 4194304 | tf_op jit(solution)/shard_map/add | solution.py:471
  121.5 0.0 copy-start
  121.5 0.0 collective-permute-start.2
  121.6 1.9 %collective-permute-done.2 = f32[128,1024]{1,0:T(8,128)S(1)} collective-permute-done((f32[128,1024]{1,0:T(8,128)S(1)}, f32[128,1024]{1,0:T(8,128)S(1)}, u32[]{:S(2)}, u32[]{:S(2)}) %collective-permute-start.2) | collective-permute-done | bytes 524320 | tf_op jit(solution)/shard_map/ppermute | solution.py:472
  123.5 0.1 fusion.2
  123.6 0.0 copy-done
  123.6 0.9 fusion
  (1 shorter events, 0.0 us)
Async XLA Ops:
  74.4 27.5 %collective-permute-start = (f32[2,2,128,1024]{3,2,1,0:T(8,128)}, f32[2,2,128,1024]{3,2,1,0:T(8,128)}, u32[]{:S(2)}, u32[]{:S(2)}) collective-permute-start(f32[2,2,128,1024]{3,2,1,0:T(8,128)} %get-tuple-element.30), channel_id=1, source_target_pairs={{0,2},{1,5},{2,0},{3,7},{4,6},{5,1},{6,4},{7,3},{8,10},{9,13},{10,... | collective-permute-start | bytes 6291464 | tf_op jit(solution)/shard_map/ppermute | solution.py:463
  104.5 14.8 %collective-permute-start.1 = (f32[2,128,1024]{2,1,0:T(8,128)}, f32[2,128,1024]{2,1,0:T(8,128)}, u32[]{:S(2)}, u32[]{:S(2)}) collective-permute-start(f32[2,128,1024]{2,1,0:T(8,128)} %add_bitcast_fusion), channel_id=1, source_target_pairs={{0,4},{1,3},{2,6},{3,1},{4,0},{5,7},{6,2},{7,5},{8,12},{9,11},{10,... | collective-permute-start | bytes 3145736 | tf_op jit(solution)/shard_map/ppermute | solution.py:467
  121.5 2.1 %copy-start = (f32[128,2048]{1,0:T(8,128)S(1)}, f32[128,2048]{1,0:T(8,128)}, u32[]{:S(2)}) copy-start(f32[128,2048]{1,0:T(8,128)} %get-tuple-element.44) | copy-start | bytes 3145732
  121.5 1.9 %collective-permute-start.2 = (f32[128,1024]{1,0:T(8,128)S(1)}, f32[128,1024]{1,0:T(8,128)S(1)}, u32[]{:S(2)}, u32[]{:S(2)}) collective-permute-start(f32[128,1024]{1,0:T(8,128)S(1)} %slice_bitcast_fusion), channel_id=1, source_target_pairs={{0,1},{1,0},{2,3},{3,2},{4,5},{5,4},{6,7},{7,6},{8,9},{9,8},{10,11... | collective-permute-start | bytes 1572872 | tf_op jit(solution)/shard_map/ppermute | solution.py:472

commit v6 on v5

--- a/solution.py
+++ b/solution.py
@@ -62,13 +62,13 @@
 PART = 64
 
 
-def rows_kernel(x_ref, dy_ref, code_ref, gate_ref, w1_ref, w3_ref, w2_ref, xr_ref, zr_ref, h_ref, da_ref, db_ref, give_ref, keep_ref, xbuf, dybuf, codes, gates, picks, picks_partner, x_rows, z_rows, w1_buf, w3_buf, w2_buf, acts, grads, r_send, r_mine, r_got, sums, own_sem, send_sem, recv_sem, meta_send, meta_recv, load_sem, rows_sem, grads_sem, swap_send, swap_recv, sums_sem):
+def rows_kernel(x_ref, dy_ref, ids_ref, pos_ref, gate_ref, w1_ref, w3_ref, w2_ref, xr_ref, zr_ref, h_ref, da_ref, db_ref, give_ref, keep_ref, xbuf, dybuf, codes, gates, picks, picks_partner, x_rows, z_rows, w1_buf, w3_buf, w2_buf, acts, grads, r_send, r_mine, r_got, sums, own_sem, send_sem, recv_sem, meta_send, meta_recv, load_sem, rows_sem, grads_sem, swap_send, swap_recv, sums_sem):
     me, core, first, second, diag, partner = places()
     other = 1 - core
     bufs = (xbuf, dybuf)
 
     def own(which):
-        src, dst = ((x_ref, xbuf.at[0]), (dy_ref, dybuf.at[0]), (code_ref, codes.at[0]), (gate_ref, gates.at[0]))[which]
+        src, dst = ((x_ref, xbuf.at[0]), (dy_ref, dybuf.at[0]))[which]
         return pltpu.make_async_copy(src, dst, own_sem.at[which])
 
     def load(which, expert):
@@ -202,33 +202,35 @@
             sums[at] = dot_tn(picks[role], r_mine[half, :, at].reshape(256, 1024)) + dot_tn(picks_partner[role], r_got[half, :, at ^ 1].reshape(256, 1024))
             sums_out(role).start()
 
-    for which in range(4):
+    for which in range(2):
         own(which).start()
+    barrier = pltpu.get_barrier_semaphore()
+    for step in range(1, 8):
+        pl.semaphore_signal(barrier, inc=1, device_id={'ep': lax.rem(me + step, 8)}, device_id_type=MESH)
+    code = jnp.where(pos_ref[...] >= 0, ids_ref[...] * SLOT + pos_ref[...], -1)
+    codes[0] = jnp.zeros((16, 128), jnp.int32)
+    gates[0] = jnp.zeros((16, 128), F32)
+    codes[0, 0:10, :] = code.T
+    gates[0, 0:10, :] = gate_ref[...].T
+    own(0).wait()
+    own(1).wait()
+    pl.semaphore_wait(barrier, 7)
+
+    for role in range(1, 8):
+        for which in range(2):
+            meta(which, role).start()
+    for array in range(2):
+        for part in range(2):
+            trip(array, part, 0).start()
+    for array in range(2):
+        for part in range(2):
+            trip(array, part, 2).start()
+
+    pick_x(0, 0, 1)
+    pick_z(0, 0, 1)
     for expert in range(4):
         load(0, expert).start()
         load(1, expert).start()
-    for expert in range(4):
-        load(2, expert).start()
-    barrier = pltpu.get_barrier_semaphore()
-    for step in range(1, 8):
-        pl.semaphore_signal(barrier, inc=1, device_id={'ep': lax.rem(me + step, 8)}, device_id_type=MESH)
-    own(0).wait()
-    own(1).wait()
-    own(2).wait()
-    own(3).wait()
-    pl.semaphore_wait(barrier, 7)
-
-    for role in range(1, 8):
-        for which in range(2):
-            meta(which, role).start()
-    for part in range(2):
-        trip(0, part, 0).start()
-    for array in range(2):
-        for part in range(2):
-            trip(array, part, 2).start()
-
-    pick_x(0, 0, 1)
-    pick_z(0, 0, 1)
     for role in range(1, 8):
         for which in range(2):
             meta(which, role).wait_recv()
@@ -238,28 +240,24 @@
     arrived(1, 2)
     pick_z(0, 1, 2)
     relay_first(0, 1)
-    trip(1, 0, 0).start()
+    for expert in range(4):
+        load(2, expert).start()
     arrived(0, 4)
     pick_x(0, 2, 4)
-
-    def rest_x():
-        relay_rest(0, 0)
-        trip(1, 1, 0).start()
-
-    activations(0, {1: rest_x, 3: lambda: relay_first(1, 0)})
-    relay_rest(0, 1)
+    activations(0, {1: lambda: relay_first(1, 0)})
+    relay_first(1, 1)
+    arrived(1, 4)
+    pick_z(0, 2, 4)
+    back(0, {1: lambda: relay_rest(0, 0), 3: lambda: relay_rest(0, 1)})
+    total(0)
     for at in range(4):
         rows_out(0, 0, at).wait()
     arrived(0, 5)
     pick_x(1, 0, 2)
     arrived(0, 6)
     pick_x(1, 2, 4)
-    relay_first(1, 1)
-    activations(1, {2: lambda: relay_rest(1, 0)})
-    arrived(1, 4)
-    pick_z(0, 2, 4)
-    back(0, {2: lambda: relay_rest(1, 1)})
-    total(0)
+    activations(1, {1: lambda: relay_rest(1, 0)})
+    relay_rest(1, 1)
     for at in range(4):
         rows_out(1, 0, at).wait()
     arrived(1, 5)
@@ -286,7 +284,7 @@
         sums_out(4 + at).wait()
 
 
-def rows_backward(x_tokens, dy_tokens, code, gate, w_gate, w_up, w_down):
+def rows_backward(x_tokens, dy_tokens, expert_ids, slot_pos, gate_vals, w_gate, w_up, w_down):
     tokens, width = x_tokens.shape
     experts, _, inner = w_gate.shape
     hbm = pl.BlockSpec(memory_space=pl.ANY)
@@ -298,13 +296,13 @@
     return pl.pallas_call(
         rows_kernel,
         out_shape=tuple(jax.ShapeDtypeStruct(s, BF16) for s in outs) + (jax.ShapeDtypeStruct(part, F32),) * 2,
-        in_specs=[hbm] * 7,
+        in_specs=[hbm] * 2 + [pl.BlockSpec(memory_space=pltpu.VMEM)] * 3 + [hbm] * 3,
         out_specs=(hbm,) * 7,
         scratch_shapes=[
             pltpu.VMEM((8, tokens, width), BF16),
             pltpu.VMEM((8, tokens, width), BF16),
-            pltpu.VMEM((8,) + code.shape, jnp.int32),
-            pltpu.VMEM((8,) + gate.shape, F32),
+            pltpu.VMEM((8, 16, tokens), jnp.int32),
+            pltpu.VMEM((8, 16, tokens), F32),
             pltpu.VMEM((8, 256, tokens), BF16),
             pltpu.VMEM((8, 256, tokens), BF16),
             pltpu.VMEM(rows[1:], BF16),
@@ -318,7 +316,7 @@
             pltpu.VMEM((2, experts, 4, SLOT, width // 2), BF16),
             pltpu.VMEM((2, experts, 4, SLOT, width // 2), BF16),
             pltpu.VMEM((4, tokens, width // 2), F32),
-            dma((4,)),
+            dma((2,)),
             dma((2, 2, 7)),
             dma((2, 2, 7)),
             dma((2, 7)),
@@ -332,7 +330,7 @@
         ],
         compiler_params=pltpu.CompilerParams(collective_id=0, has_side_effects=True, vmem_limit_bytes=67000000),
         name='rows_backward',
-    )(x_tokens, dy_tokens, code, gate, w_gate, w_up, w_down)
+    )(x_tokens, dy_tokens, expert_ids, slot_pos, gate_vals, w_gate, w_up, w_down)
 
 
 WEIGHT_TILES = 1
@@ -455,10 +453,7 @@
     grad_spec = P(('dp', 'ep'), None, None)
 
     def local_backward(x_tokens, dy_tokens, expert_ids, gate_vals, slot_pos, w_gate, w_up, w_down, shared_gate, shared_up, shared_down):
-        code = jnp.where(slot_pos >= 0, expert_ids * SLOT + slot_pos, -1)
-        code = jnp.pad(code.T, ((0, 6), (0, 0)), constant_values=-1)
-        gate = jnp.pad(gate_vals.T, ((0, 6), (0, 0)))
-        *saved, give, keep = rows_backward(x_tokens, dy_tokens, code, gate, w_gate, w_up, w_down)
+        *saved, give, keep = rows_backward(x_tokens, dy_tokens, expert_ids, slot_pos, gate_vals, w_gate, w_up, w_down)
         saved = [rows.reshape((8,) + rows.shape[2:]) for rows in saved]
         got = lax.ppermute(give, 'ep', partners('first'))
         grads = weight_grads(*saved)

time: 125 us -> 120 us (0.960)
  Pallas kernels: 108 us -> 100 us
  local copies, waits for them, and re-layouts: 1.95 us -> 4.33 us
    pallas_call x1, Pallas kernels: 71.1 us -> 63.7 us  [rows_backward(): pl.pallas_call(rows_kernel, out_shape=tuple((jax.ShapeDtypeStruct(s, BF16...]
    unnamed x2 -> x5, local copies, waits for them, and re-layouts: 0.01 us -> 4.29 us
    pad x2 -> x0, local copies, waits for them, and re-layouts: 1.9 us -> none  [the longest x1 1.3 us: local_backward(): gate = jnp.pad(gate_vals.T, ((0, 6), (0, 0)))]
  transfers between devices with their start and end apart: 3 -> 3, of which waited for: 2 -> 2; matrix products, arithmetic and copies ran while one was open for 0% -> 0% of each run, Pallas kernels for 29% -> 31%
where the time goes in v6:
time: 120 us; the launch traced here: 119 us
  Pallas kernels  100 us (83%)
  waiting for transfers between devices  6.43 us (5%)
  other arithmetic  5.84 us (5%)
  local copies, waits for them, and re-layouts  4.33 us (4%)
  starting transfers between devices  1.78 us (1%)
    pallas_call x1, Pallas kernels, rows_backward(): pl.pallas_call(rows_kernel, out_shape=tuple((jax.ShapeDtypeStruct(s, BF16...  63.7 us
    pallas_call x1, Pallas kernels, weight_grads(): pl.pallas_call(weight_kernel, grid=(experts, WEIGHT_TILES), out_shape=(ja...  26.3 us
    pallas_call x1, Pallas kernels, shared_backward(): pl.pallas_call(shared_kernel, grid=(SHARED_TILES,), out_shape=(jax.ShapeD...  10.3 us
    ppermute x1, waiting for transfers between devices, local_backward(): got_second = lax.ppermute(onward, 'ep', partners('second'))  4.54 us
    unnamed x5, local copies, waits for them, and re-layouts  4.29 us
    add x1, other arithmetic, local_backward(): onward = keep[0] + got[0]  2.71 us
  transfers between devices with their start and end apart: 3, of which 2 were waited for; matrix products, arithmetic and copies ran while one was open for 0% of the time, Pallas kernels for 31%

profile of v6, /device:TPU:0, one launch (start us, length us, event | category | flops | bytes accessed | tf_op | source)
XLA Modules:
  0.0 119.4 jit_solution(14834020816333423553)
XLA Ops:
  0.6 1.4 %copy.18.ids_ref = s32[128,10]{1,0:T(8,128)} copy(s32[128,10]{0,1:T(8,128)} %param.13) | data formatting | bytes 10240 | tf_op args[2]
  2.1 1.4 %copy.19.pos_ref = s32[128,10]{1,0:T(8,128)} copy(s32[128,10]{0,1:T(8,128)} %param.15) | data formatting | bytes 10240 | tf_op args[4]
  3.5 1.4 %copy.20.gate_ref = f32[128,10]{1,0:T(8,128)} copy(f32[128,10]{0,1:T(8,128)} %param.14) | data formatting | bytes 10240 | tf_op args[3]
  4.9 63.7 %rows_backward.1 = (bf16[2,4,4,64,2048]{4,3,2,1,0:T(8,128)(2,1)}, bf16[2,4,4,64,2048]{4,3,2,1,0:T(8,128)(2,1)}, bf16[2,4,4,64,512]{4,3,2,1,0:T(8,128)(2,1)}, bf1...) custom-call(bf16[128,2048]{1,0:T(8,128)(2,1)} %x_ref.2, ...), custom_call_target="tpu_custom_call" | custom-call | tf_op jit(solution)/shard_map/rows_backward/pallas_call | solution.py:296
  68.7 1.7 %collective-permute-start = (f32[2,2,128,1024]{3,2,1,0:T(8,128)}, f32[2,2,128,1024]{3,2,1,0:T(8,128)}, u32[]{:S(2)}, u32[]{:S(2)}) collective-permute-start(f32[2,2,128,1024]{3,2,1,0:T(8,128)} %get-tuple-element.30), channel_id=1, source_target_pairs={{0,2},{1,5},{2,0},{3,7},{4,6},{5,1},{6,4},{7,3},{8,10},{9,13},{10,... | collective-permute-start | bytes 6291464 | tf_op jit(solution)/shard_map/ppermute | solution.py:458
  70.4 26.3 %weight_grads.1 = (f32[4,2048,512]{2,1,0:T(8,128)}, f32[4,2048,512]{2,1,0:T(8,128)}, f32[4,512,2048]{2,1,0:T(8,128)}) custom-call(bf16[8,4,64,2048]{3,2,1,0:T(8,128)(2,1)} %bitcast.17, bf16[8,4,64,2048]{3,2,1,0:T(8,128)(2,1)} %bitcast.18, bf16[8,4,64,512]{3,2,1,0:T(8,128)(2,1)} %bitcast.19, bf16[8,4,64,512]{3,2,1,0:T(8,128)(2,1)} %bitcast.20, ...), custom_call_target="tpu_custom_call" | custom-call | flops 12899999744 | bytes 70000000 | tf_op jit(solution)/shard_map/weight_grads/pallas_call | solution.py:363
  96.7 0.0 collective-permute-done
  96.7 2.7 %add_bitcast_fusion = f32[2,128,1024]{2,1,0:T(8,128)} fusion(f32[2,2,128,1024]{3,2,1,0:T(8,128)} %collective-permute-done, f32[2,2,128,1024]{3,2,1,0:T(8,128)} %get-tuple-element.29), kind=kLoop, calls=%fused_computation.3 | loop fusion | flops 262144 | bytes 3145728 | tf_op jit(solution)/shard_map/add | solution.py:461
  99.4 0.0 collective-permute-start.1
  99.4 10.3 %shared_backward.1 = (f32[128,2048]{1,0:T(8,128)}, f32[1,2048,512]{2,1,0:T(8,128)}, f32[1,2048,512]{2,1,0:T(8,128)}, f32[1,512,2048]{2,1,0:T(8,128)}) custom-call(bf16[128,2048]{1,0:T(8,128)(2,1)} %x_ref.2, bf16[128,2048]{1,0:T(8,128)(2,1)} %dy_ref.2, bf16[2048,512]{1,0:T(8,128)(2,1)} %w1_ref.3, bf16[2048,512]{1,0:T(8,128)(2,1)} %w3_ref.3, ...), custom_call_target="tpu_custom_call" | custom-call | flops 6000000000 | bytes 20000000 | tf_op jit(solution)/shard_map/shared_backward/pallas_call | solution.py:412
  109.7 4.5 %collective-permute-done.1 = f32[2,128,1024]{2,1,0:T(8,128)} collective-permute-done((f32[2,128,1024]{2,1,0:T(8,128)}, f32[2,128,1024]{2,1,0:T(8,128)}, u32[]{:S(2)}, u32[]{:S(2)}) %collective-permute-start.1) | collective-permute-done | bytes 1048608 | tf_op jit(solution)/shard_map/ppermute | solution.py:462
  114.2 2.1 %bitcast_add_fusion = f32[2,128,1024]{2,1,0:T(8,128)S(1)} fusion(f32[2,128,1024]{2,1,0:T(8,128)} %collective-permute-done.1, f32[2,2,128,1024]{3,2,1,0:T(8,128)} %collective-permute-done, f32[2,2,128,1024]{3,2,1,0:T(8,128)} %get-tuple-element.29), kind=kLoop, calls=%fused_computation.2 | loop fusion | flops 524288 | bytes 4194304 | tf_op jit(solution)/shard_map/add | solution.py:466
  116.4 0.0 copy-start
  116.4 0.0 collective-permute-start.2
  116.5 1.9 %collective-permute-done.2 = f32[128,1024]{1,0:T(8,128)S(1)} collective-permute-done((f32[128,1024]{1,0:T(8,128)S(1)}, f32[128,1024]{1,0:T(8,128)S(1)}, u32[]{:S(2)}, u32[]{:S(2)}) %collective-permute-start.2) | collective-permute-done | bytes 524320 | tf_op jit(solution)/shard_map/ppermute | solution.py:467
  118.4 0.1 fusion.2
  118.4 0.0 copy-done
  118.5 0.9 fusion
  (1 shorter events, 0.0 us)
Async XLA Ops:
  68.7 28.1 %collective-permute-start = (f32[2,2,128,1024]{3,2,1,0:T(8,128)}, f32[2,2,128,1024]{3,2,1,0:T(8,128)}, u32[]{:S(2)}, u32[]{:S(2)}) collective-permute-start(f32[2,2,128,1024]{3,2,1,0:T(8,128)} %get-tuple-element.30), channel_id=1, source_target_pairs={{0,2},{1,5},{2,0},{3,7},{4,6},{5,1},{6,4},{7,3},{8,10},{9,13},{10,... | collective-permute-start | bytes 6291464 | tf_op jit(solution)/shard_map/ppermute | solution.py:458
  99.4 14.8 %collective-permute-start.1 = (f32[2,128,1024]{2,1,0:T(8,128)}, f32[2,128,1024]{2,1,0:T(8,128)}, u32[]{:S(2)}, u32[]{:S(2)}) collective-permute-start(f32[2,128,1024]{2,1,0:T(8,128)} %add_bitcast_fusion), channel_id=1, source_target_pairs={{0,4},{1,3},{2,6},{3,1},{4,0},{5,7},{6,2},{7,5},{8,12},{9,11},{10,... | collective-permute-start | bytes 3145736 | tf_op jit(solution)/shard_map/ppermute | solution.py:462
  116.4 2.1 %copy-start = (f32[128,2048]{1,0:T(8,128)S(1)}, f32[128,2048]{1,0:T(8,128)}, u32[]{:S(2)}) copy-start(f32[128,2048]{1,0:T(8,128)} %get-tuple-element.44) | copy-start | bytes 3145732
  116.4 1.9 %collective-permute-start.2 = (f32[128,1024]{1,0:T(8,128)S(1)}, f32[128,1024]{1,0:T(8,128)S(1)}, u32[]{:S(2)}, u32[]{:S(2)}) collective-permute-start(f32[128,1024]{1,0:T(8,128)S(1)} %slice_bitcast_fusion), channel_id=1, source_target_pairs={{0,1},{1,0},{2,3},{3,2},{4,5},{5,4},{6,7},{7,6},{8,9},{9,8},{10,11... | collective-permute-start | bytes 1572872 | tf_op jit(solution)/shard_map/ppermute | solution.py:467

commit v7 on v0

v7 whole, which is shorter than its diff:
```python
import jax
import jax.numpy as jnp
from jax import lax
from jax.experimental import pallas as pl
from jax.experimental.pallas import tpu as pltpu
from jax.sharding import PartitionSpec as P

MESH = pl.DeviceIdType.MESH
BF16 = jnp.bfloat16
F32 = jnp.float32
TOKENS, TOP_K, EXPERTS, ROLES, PARTS = 128, 10, 4, 8, 2
WIDTH, HALF, INNER, SLOT, PART = 2048, 1024, 512, 64, 64
ROWS = 256
X, DY = range(2)
EARLY, LATE = range(2)
TO_FIRST, TO_SECOND, TO_PARTNER, FIRST_ON, FIRST_OVER, SECOND_OVER, DIAG_OVER = range(7)
TRIPS = 7
SEEN_AS = {1: 1, 2: 2, 3: 5, 4: 4, 5: 3, 6: 6, 7: 7}


def swiglu_parts(act_gate, act_up, grad_hidden):
    gate_f32 = act_gate.astype(F32)
    up_f32 = act_up.astype(F32)
    sigma = jax.nn.sigmoid(gate_f32)
    silu_gate = gate_f32 * sigma
    hidden = (silu_gate * up_f32).astype(BF16)
    grad_gate = (grad_hidden * up_f32 * sigma * (1.0 + gate_f32 * (1.0 - sigma))).astype(BF16)
    grad_up = (grad_hidden * silu_gate).astype(BF16)
    return hidden, grad_gate, grad_up


def dot_nn(a, b):
    return lax.dot_general(a, b, (((1,), (0,)), ((), ())), preferred_element_type=F32)


def dot_nt(a, b):
    return lax.dot_general(a, b, (((1,), (1,)), ((), ())), preferred_element_type=F32)


def dot_tn(a, b):
    return lax.dot_general(a, b, (((0,), (0,)), ((), ())), preferred_element_type=F32)


def places():
    me = lax.axis_index('ep')
    core = lax.rem(me, 2)
    flip_x = 2 - 4 * lax.rem(me // 2, 2)
    flip_y = 4 - 8 * (me // 4)
    first = me + flip_x * (1 - core) + flip_y * core
    second = me + flip_y * (1 - core) + flip_x * core
    diag = me + flip_x + flip_y
    partner = me + 1 - 2 * core
    return me, core, first, second, diag, partner


def remote(src, dst, send_sem, recv_sem, device):
    return pltpu.make_async_remote_copy(src_ref=src, dst_ref=dst, send_sem=send_sem, recv_sem=recv_sem, device_id={'ep': device}, device_id_type=MESH)


def one_hot(code, base):
    slot = lax.broadcasted_iota(jnp.int32, (ROWS, TOKENS), 0) + base
    hits = jnp.zeros((ROWS, TOKENS), F32)
    for choice in range(TOP_K):
        hits = jnp.where(slot == code[choice:choice + 1, :], 1.0, hits)
    return hits.astype(BF16)


def rows_kernel(x_ref, dy_ref, ids_ref, pos_ref, gate_ref, w1_ref, w3_ref, w2_ref, s1_ref, s3_ref, s2_ref, xr_ref, zr_ref, h_ref, da_ref, db_ref, far_ref, cross_ref, near_ref, base_ref, leaf_ref, dx_ref, parts_ref, xbuf, dybuf, codes, gates, picks, picks_partner, x_rows, z_rows, w1_buf, w3_buf, w2_buf, acts, grads, r_send, r_mine, r_got, sums, own_sem, send_sem, recv_sem, meta_send, meta_recv, load_sem, rows_sem, grads_sem, swap_send, swap_recv, sums_sem, leaf_send, leaf_recv, shared_sem, shared_out):
    me, core, first, second, diag, partner = places()
    other = 1 - core
    bufs = (xbuf, dybuf)

    def own(which):
        return pltpu.make_async_copy((x_ref, dy_ref)[which], bufs[which].at[0], own_sem.at[which])

    def load(which, expert):
        src, dst = ((w1_ref, w1_buf), (w3_ref, w3_buf), (w2_ref, w2_buf))[which]
        return pltpu.make_async_copy(src.at[expert], dst.at[expert], load_sem.at[which, expert])

    def trip(array, part, kind):
        src, dst, device = ((0, 2, first), (0, 4, second), (0, 1, partner), (2, 6, second), (2, 3, partner), (4, 5, partner), (6, 7, partner))[kind]
        rows = pl.ds(part * PART, PART)
        return remote(bufs[array].at[src, rows], bufs[array].at[dst, rows], send_sem.at[array, part, kind], recv_sem.at[array, part, kind], device)

    def meta(which, role):
        device = (me, partner, first, partner + second - me, second, partner + first - me, diag, partner + diag - me)[role]
        table = (codes, gates)[which]
        seen = SEEN_AS[role]
        return remote(table.at[0], table.at[seen], meta_send.at[which, role], meta_recv.at[which, seen], device)

    def start(array, part, kind):
        trip(array, part, kind).start()

    def pass_over(array, part, kind, over):
        trip(array, part, kind).wait_recv()
        trip(array, part, over).start()

    def first_in(array, part):
        pass_over(array, part, TO_FIRST, FIRST_OVER)

    def second_in(array, part):
        pass_over(array, part, TO_SECOND, SECOND_OVER)

    def diag_in(array, part):
        pass_over(array, part, FIRST_ON, DIAG_OVER)

    def arrived(array, kind):
        for part in range(PARTS):
            trip(array, part, kind).wait_recv()

    def rows_out(array, half, at):
        return pltpu.make_async_copy((x_rows, z_rows)[array].at[at], (xr_ref, zr_ref)[array].at[half, at], rows_sem.at[array, half, at])

    def pick_x(half, low, high):
        def one(at, carry):
            role = half * 4 + at
            select = one_hot(codes[role], me * ROWS)
            picks[role] = select
            picks_partner[role] = one_hot(codes[role], partner * ROWS)
            for tile in range(4):
                cols = slice(tile * INNER, tile * INNER + INNER)
                x_rows[at, :, :, cols] = dot_nn(select, xbuf[role, :, cols]).astype(BF16).reshape(EXPERTS, SLOT, INNER)
            rows_out(X, half, at).start()
            return carry

        lax.fori_loop(low, high, one, 0)

    def pick_z(half, low, high):
        def one(at, carry):
            role = half * 4 + at
            slot = lax.broadcasted_iota(jnp.int32, (ROWS, TOKENS), 0) + me * ROWS
            spread = jnp.zeros((ROWS, TOKENS), F32)
            for choice in range(TOP_K):
                spread = jnp.where(slot == codes[role, choice:choice + 1, :], gates[role, choice:choice + 1, :], spread)
            scale = jnp.sum(spread, axis=1, keepdims=True)
            select = picks[role]
            for tile in range(4):
                cols = slice(tile * INNER, tile * INNER + INNER)
                value = dot_nn(select, dybuf[role, :, cols]) * scale
                z_rows[at, :, :, cols] = value.astype(BF16).reshape(EXPERTS, SLOT, INNER)
            rows_out(DY, half, at).start()
            return carry

        lax.fori_loop(low, high, one, 0)

    def activations(half, after):
        def one(expert, carry):
            if half == EARLY:
                load(0, expert).wait()
                load(1, expert).wait()
            rows = x_rows[:, expert].reshape(ROWS, WIDTH)
            acts[0, half, expert] = dot_nn(rows, w1_buf[expert]).astype(BF16)
            acts[1, half, expert] = dot_nn(rows, w3_buf[expert]).astype(BF16)
            for step, action in after.items():
                pl.when(expert == step)(action)
            return carry

        lax.fori_loop(0, EXPERTS, one, 0)

    def grads_out(which, half, expert):
        return pltpu.make_async_copy(grads.at[which, expert], (h_ref, da_ref, db_ref)[which].at[half, :, expert], grads_sem.at[which, half, expert])

    def sent_rows(expert):
        return r_send.at[pl.ds(expert * 4, 4)]

    def swap(half, expert):
        return remote(sent_rows(expert), r_got.at[half, expert], swap_send.at[half, expert], swap_recv.at[half, expert], partner)

    def rows_back(d_gate, d_up, expert, side, tile):
        at = pl.ds(pl.multiple_of(side * HALF + tile * INNER, INNER), INNER)
        value = dot_nt(d_gate, w1_buf[expert, at, :]) + dot_nt(d_up, w3_buf[expert, at, :])
        return value.astype(BF16).reshape(4, SLOT, INNER)

    def back(half, after):
        def send_side(expert, carry):
            if half == EARLY:
                load(2, expert).wait()
            grad_hidden = dot_nt(z_rows[:, expert].reshape(ROWS, WIDTH), w2_buf[expert])
            parts = swiglu_parts(acts[0, half, expert], acts[1, half, expert], grad_hidden)
            for which in range(3):
                if half == LATE:
                    grads_out(which, EARLY, expert).wait()
                grads[which, expert] = parts[which].reshape(4, SLOT, INNER)
                grads_out(which, half, expert).start()
            if half == LATE:
                swap(EARLY, expert).wait_send()
            for tile in range(2):
                r_send[pl.ds(expert * 4, 4), :, tile * INNER:(tile + 1) * INNER] = rows_back(parts[1], parts[2], expert, other, tile)
            swap(half, expert).start()
            for step, action in after.items():
                pl.when(expert == step)(action)
            return carry

        def own_side(expert, carry):
            d_gate = grads[1, expert].reshape(ROWS, INNER)
            d_up = grads[2, expert].reshape(ROWS, INNER)
            for tile in range(2):
                value = rows_back(d_gate, d_up, expert, core, tile)
                for at in range(4):
                    r_mine[(half * 4 + at) * EXPERTS + expert, :, tile * INNER:(tile + 1) * INNER] = value[at]
            return carry

        lax.fori_loop(0, EXPERTS, send_side, 0)
        lax.fori_loop(0, EXPERTS, own_side, 0)

    def sums_out(role):
        ref = {6: far_ref, 7: cross_ref, 4: near_ref.at[0], 5: near_ref.at[1], 0: base_ref.at[0], 1: base_ref.at[1]}[role]
        return pltpu.make_async_copy(sums.at[role % 4], ref, sums_sem.at[role])

    def leaf(which):
        return remote(sums.at[2 + which], leaf_ref.at[which], leaf_send.at[which], leaf_recv.at[which], (first, second)[which])

    def total(half):
        for expert in range(EXPERTS):
            swap(half, expert).wait_recv()
        for at in range(4):
            role = half * 4 + at
            if half == LATE:
                if at < 2:
                    sums_out(at).wait()
                else:
                    leaf(at - 2).wait_send()
            else:
                if at < 2:
                    shared_rows_out(at).wait()
            mine = r_mine[role * EXPERTS:(role + 1) * EXPERTS].reshape(ROWS, HALF)
            sums[at] = dot_tn(picks[role], mine) + dot_tn(picks_partner[role], r_got[half, :, at ^ 1].reshape(ROWS, HALF))
            if half == LATE or at < 2:
                sums_out(role).start()

    def shared_load(which):
        src, dst = ((s1_ref, r_mine.at[:, :, :INNER]), (s3_ref, r_mine.at[:, :, INNER:]), (s2_ref.at[:, :, :HALF], r_send.at[:8]), (s2_ref.at[:, :, HALF:], r_send.at[8:]))[which]
        return pltpu.make_async_copy(src, dst, shared_sem.at[which])

    def shared_rows_out(which):
        return pltpu.make_async_copy(sums.at[which], dx_ref.at[which], shared_out.at[which])

    def shared_parts_out(which):
        return pltpu.make_async_copy(acts.at[1, LATE, which, :TOKENS], parts_ref.at[which], shared_out.at[2 + which])

    def shared_chain():
        for which in range(4):
            shared_load(which).wait()
        x, dy = xbuf[0], dybuf[0]
        act_gate = dot_nn(x, r_mine[:, :, :INNER].reshape(WIDTH, INNER)).astype(BF16)
        act_up = dot_nn(x, r_mine[:, :, INNER:].reshape(WIDTH, INNER)).astype(BF16)
        grad_hidden = dot_nt(dy[:, :HALF], r_send[:8].reshape(INNER, HALF)) + dot_nt(dy[:, HALF:], r_send[8:].reshape(INNER, HALF))
        parts = swiglu_parts(act_gate, act_up, grad_hidden)
        for which in range(3):
            acts[1, LATE, which, :TOKENS] = parts[which]
            shared_parts_out(which).start()
        for which in range(2):
            for tile in range(2):
                at = slice((which * 2 + tile) * 8, (which * 2 + tile) * 8 + 8)
                gate_w = r_mine[at, :, :INNER].reshape(INNER, INNER)
                up_w = r_mine[at, :, INNER:].reshape(INNER, INNER)
                sums[which, :, tile * INNER:(tile + 1) * INNER] = dot_nt(parts[1], gate_w) + dot_nt(parts[2], up_w)
            shared_rows_out(which).start()

    for which in range(2):
        own(which).start()
    barrier = pltpu.get_barrier_semaphore()
    for step in range(1, ROLES):
        pl.semaphore_signal(barrier, inc=1, device_id={'ep': lax.rem(me + step, ROLES)}, device_id_type=MESH)
    codes[0] = jnp.zeros((16, TOKENS), jnp.int32)
    gates[0] = jnp.zeros((16, TOKENS), F32)
    codes[0, :TOP_K, :] = jnp.where(pos_ref[...] >= 0, ids_ref[...] * SLOT + pos_ref[...], -1)
    gates[0, :TOP_K, :] = gate_ref[...]
    for which in range(2):
        own(which).wait()
    pl.semaphore_wait(barrier, ROLES - 1)

    for role in SEEN_AS:
        for which in range(2):
            meta(which, role).start()
    for kind in (TO_FIRST, TO_PARTNER):
        for array in (X, DY):
            for part in range(PARTS):
                start(array, part, kind)
    for which in range(4):
        shared_load(which).start()
    for expert in range(EXPERTS):
        load(0, expert).start()
        load(1, expert).start()
    pick_x(EARLY, 0, 1)
    pick_z(EARLY, 0, 1)
    for role in SEEN_AS:
        for which in range(2):
            meta(which, role).wait_recv()
    arrived(X, TO_PARTNER)
    pick_x(EARLY, 1, 2)
    shared_chain()
    arrived(DY, TO_PARTNER)
    pick_z(EARLY, 1, 2)
    for part in range(PARTS):
        first_in(X, part)
    for expert in range(EXPERTS):
        load(2, expert).start()
    start(X, 0, TO_SECOND)
    arrived(X, FIRST_OVER)
    pick_x(EARLY, 2, 4)

    def queue_x():
        start(X, 1, TO_SECOND)
        start(X, 0, FIRST_ON)

    def queue_both():
        start(X, 1, FIRST_ON)
        first_in(DY, 0)
        start(DY, 0, TO_SECOND)

    def queue_dy():
        first_in(DY, 1)
        start(DY, 1, TO_SECOND)
        start(DY, 0, FIRST_ON)
        start(DY, 1, FIRST_ON)

    activations(EARLY, {0: queue_x, 1: queue_both, 3: queue_dy})
    arrived(DY, FIRST_OVER)
    pick_z(EARLY, 2, 4)

    def rest_x():
        second_in(X, 1)
        diag_in(X, 0)

    back(EARLY, {1: lambda: second_in(X, 0), 3: rest_x})
    total(EARLY)
    diag_in(X, 1)
    for array in (X, DY):
        for at in range(4):
            rows_out(array, EARLY, at).wait()
    arrived(X, SECOND_OVER)
    pick_x(LATE, 0, 2)
    arrived(X, DIAG_OVER)
    pick_x(LATE, 2, 4)
    for which in range(3):
        shared_parts_out(which).wait()
    activations(LATE, {1: lambda: second_in(DY, 0), 3: lambda: second_in(DY, 1)})
    diag_in(DY, 0)
    arrived(DY, SECOND_OVER)
    pick_z(LATE, 0, 2)
    diag_in(DY, 1)
    for which in range(2):
        leaf(which).start()
    arrived(DY, DIAG_OVER)
    pick_z(LATE, 2, 4)
    back(LATE, {})
    total(LATE)

    for array in (X, DY):
        for part in range(PARTS):
            for kind in range(TRIPS):
                trip(array, part, kind).wait_send()
    for role in SEEN_AS:
        for which in range(2):
            meta(which, role).wait_send()
    for expert in range(EXPERTS):
        swap(LATE, expert).wait_send()
        for which in range(3):
            grads_out(which, LATE, expert).wait()
    for which in range(2):
        leaf(which).wait_recv()
    for at in range(4):
        for array in (X, DY):
            rows_out(array, LATE, at).wait()
        sums_out(4 + at).wait()


def rows_backward(x_tokens, dy_tokens, expert_ids, slot_pos, gate_vals, w_gate, w_up, w_down, shared_gate, shared_up, shared_down):
    hbm = pl.BlockSpec(memory_space=pl.ANY)
    vmem = pl.BlockSpec(memory_space=pltpu.VMEM)
    rows = (2, 4, EXPERTS, SLOT, WIDTH)
    grads = (2, 4, EXPERTS, SLOT, INNER)
    pair = (2, TOKENS, HALF)
    parts = (3, TOKENS, INNER)
    blocks = (ROLES, TOKENS, WIDTH)
    tables = (ROLES, 16, TOKENS)
    select = (ROLES, ROWS, TOKENS)
    dma = pltpu.SemaphoreType.DMA
    outs = [(s, BF16) for s in (rows, rows, grads, grads, grads)] + [(pair[1:], F32)] * 2 + [(pair, F32)] * 4 + [(parts, BF16)]
    scratch = [(blocks, BF16), (blocks, BF16), (tables, jnp.int32), (tables, F32), (select, BF16), (select, BF16), (rows[1:], BF16), (rows[1:], BF16)]
    scratch += [(w.shape, BF16) for w in (w_gate, w_up, w_down)]
    scratch += [((2, 2, EXPERTS, ROWS, INNER), BF16), ((3, EXPERTS, 4, SLOT, INNER), BF16), ((16, SLOT, HALF), BF16), ((32, SLOT, HALF), BF16)]
    scratch += [((2, EXPERTS, 4, SLOT, HALF), BF16), ((4, TOKENS, HALF), F32)]
    trips = (2, PARTS, TRIPS)
    sems = [(2,), trips, trips, (2, ROLES), (2, ROLES), (3, EXPERTS), (2, 2, 4), (3, 2, EXPERTS), (2, EXPERTS), (2, EXPERTS), (ROLES,), (2,), (2,), (4,), (5,)]
    return pl.pallas_call(
        rows_kernel,
        out_shape=tuple(jax.ShapeDtypeStruct(s, d) for s, d in outs),
        in_specs=[hbm] * 2 + [vmem] * 3 + [hbm] * 6,
        out_specs=(hbm,) * len(outs),
        scratch_shapes=[pltpu.VMEM(s, d) for s, d in scratch] + [dma(s) for s in sems],
        compiler_params=pltpu.CompilerParams(collective_id=0, has_side_effects=True, vmem_limit_bytes=67000000),
        name='rows_backward',
    )(x_tokens, dy_tokens, expert_ids.T, slot_pos.T, gate_vals.T, w_gate, w_up, w_down, shared_gate.reshape(32, SLOT, INNER), shared_up.reshape(32, SLOT, INNER), shared_down.reshape(8, SLOT, WIDTH))


def down_kernel(z_ref, h_ref, x_ref, dy_ref, parts_ref, dw2_ref, s1_ref, s3_ref, s2_ref, s1_buf, s3_buf, s2_buf, sem):
    expert = pl.program_id(0)

    def shared_out(which):
        src, dst = ((s1_buf, s1_ref), (s3_buf, s3_ref), (s2_buf, s2_ref))[which]
        return pltpu.make_async_copy(src, dst.at[0], sem.at[which])

    @pl.when(expert == 0)
    def _():
        x_t = x_ref[...].T
        s1_buf[...] = dot_nn(x_t, parts_ref[1])
        shared_out(0).start()
        s3_buf[...] = dot_nn(x_t, parts_ref[2])
        shared_out(1).start()
        s2_buf[...] = dot_nn(parts_ref[0].T, dy_ref[...])
        shared_out(2).start()

    hidden_t = h_ref[:, 0].reshape(INNER, INNER).T
    for tile in range(4):
        cols = slice(tile * INNER, tile * INNER + INNER)
        dw2_ref[0, :, cols] = dot_nn(hidden_t, z_ref[:, 0, :, cols].reshape(INNER, INNER))

    @pl.when(expert == EXPERTS - 1)
    def _():
        for which in range(3):
            shared_out(which).wait()


def by_expert(inner):
    return pl.BlockSpec((ROLES, 1, SLOT, inner), lambda e: (0, e, 0, 0))


def down_grads(z_rows, hidden, x_tokens, dy_tokens, parts):
    vmem = pl.BlockSpec(memory_space=pltpu.VMEM)
    hbm = pl.BlockSpec(memory_space=pl.ANY)
    wide, tall = (1, INNER, WIDTH), (1, WIDTH, INNER)
    return pl.pallas_call(
        down_kernel,
        grid=(EXPERTS,),
        out_shape=(jax.ShapeDtypeStruct((EXPERTS, INNER, WIDTH), F32),) + tuple(jax.ShapeDtypeStruct(s, F32) for s in (tall, tall, wide)),
        in_specs=[by_expert(WIDTH), by_expert(INNER), vmem, vmem, vmem],
        out_specs=(pl.BlockSpec(wide, lambda e: (e, 0, 0)), hbm, hbm, hbm),
        scratch_shapes=[pltpu.VMEM(s[1:], F32) for s in (tall, tall, wide)] + [pltpu.SemaphoreType.DMA((3,))],
        compiler_params=pltpu.CompilerParams(dimension_semantics=('arbitrary',), vmem_limit_bytes=67000000),
        cost_estimate=pl.CostEstimate(flops=5_000_000_000, bytes_accessed=40_000_000, transcendentals=0),
        name='down_grads',
    )(z_rows, hidden, x_tokens, dy_tokens, parts)


def up_kernel(x_ref, da_ref, db_ref, dw1_ref, dw3_ref):
    for tile in range(4):
        cols = slice(tile * INNER, tile * INNER + INNER)
        x_t = x_ref[:, 0, :, cols].reshape(INNER, INNER).T
        dw1_ref[0, cols, :] = dot_nn(x_t, da_ref[:, 0].reshape(INNER, INNER))
        dw3_ref[0, cols, :] = dot_nn(x_t, db_ref[:, 0].reshape(INNER, INNER))


def up_grads(x_rows, d_gate, d_up):
    tall = pl.BlockSpec((1, WIDTH, INNER), lambda e: (e, 0, 0))
    return pl.pallas_call(
        up_kernel,
        grid=(EXPERTS,),
        out_shape=(jax.ShapeDtypeStruct((EXPERTS, WIDTH, INNER), F32),) * 2,
        in_specs=[by_expert(WIDTH), by_expert(INNER), by_expert(INNER)],
        out_specs=(tall, tall),
        compiler_params=pltpu.CompilerParams(dimension_semantics=('arbitrary',), vmem_limit_bytes=67000000),
        cost_estimate=pl.CostEstimate(flops=9_000_000_000, bytes_accessed=44_000_000, transcendentals=0),
        name='up_grads',
    )(x_rows, d_gate, d_up)


def partners(kind):
    pairs = []
    for me in range(8):
        core = me % 2
        along_x, along_y = me ^ 2, me ^ 4
        first, second = (along_x, along_y) if core == 0 else (along_y, along_x)
        pairs.append((me, {'first': first, 'second': second, 'chip': me ^ 1}[kind]))
    return pairs


def solution(mesh):
    token_spec = P(('dp', 'ep'), None)
    expert_spec = P('ep', None, None)
    whole_spec = P(None, None)
    grad_spec = P(('dp', 'ep'), None, None)

    def local_backward(x_tokens, dy_tokens, expert_ids, gate_vals, slot_pos, w_gate, w_up, w_down, shared_gate, shared_up, shared_down):
        *saved, far, cross, near, base, leaf, shared_dx, parts = rows_backward(x_tokens, dy_tokens, expert_ids, slot_pos, gate_vals, w_gate, w_up, w_down, shared_gate, shared_up, shared_down)
        x_rows, z_rows, hidden, d_gate, d_up = [rows.reshape((ROLES,) + rows.shape[2:]) for rows in saved]
        far = (lax.ppermute(far, 'ep', partners('first')), lax.ppermute(cross, 'ep', partners('second')))
        down = down_grads(z_rows, hidden, x_tokens, dy_tokens, parts)
        far, down = lax.optimization_barrier((far, down))
        last = (lax.ppermute(near[0] + far[0], 'ep', partners('second')), lax.ppermute(near[1] + far[1], 'ep', partners('first')))
        d_gate, *_ = lax.optimization_barrier((d_gate,) + tuple(far))
        up = up_grads(x_rows, d_gate, d_up)
        last, up = lax.optimization_barrier((last, up))
        own = base[0] + leaf[0] + last[0]
        swapped = lax.ppermute(base[1] + leaf[1] + last[1], 'ep', partners('chip'))
        core = lax.rem(lax.axis_index('ep'), 2)
        left = jnp.where(core == 0, own, swapped)
        right = jnp.where(core == 0, swapped, own)
        grad_x = jnp.concatenate((left + shared_dx[0], right + shared_dx[1]), axis=1).astype(BF16)
        return grad_x, up[0], up[1], down[0], down[1], down[2], down[3]

    return jax.shard_map(local_backward, mesh=mesh, in_specs=(token_spec, token_spec, token_spec, token_spec, token_spec, expert_spec, expert_spec, expert_spec, whole_spec, whole_spec, whole_spec), out_specs=(token_spec, grad_spec, grad_spec, grad_spec, grad_spec, grad_spec, grad_spec), check_vma=False)
```

time: 487 us -> 109 us (0.22); the launches traced: 480 us -> 109 us
  matrix products: 173 us -> 0 us
  local copies, waits for them, and re-layouts: 147 us -> 0 us
  waiting for transfers between devices: 118 us -> 1.9 us
  Pallas kernels: 0 us -> 94.9 us
  other arithmetic: 25.5 us -> 6.96 us
  starting transfers between devices: 16 us -> 4.13 us
    dot_general x16 -> x0, matrix products: 173 us -> none  [the longest x1 31.5 us: local_backward(): jnp.einsum('erd,erf->edf', x_exp, grad_gate, preferred_element_type=jnp.f...]
    all_to_all x3 -> x0, waiting for transfers between devices: 118 us -> none  [the longest x1 63.6 us: local_backward(): x_exp = lax.all_to_all(send_x, 'ep', 0, 1, tiled=True)]
    pallas_call x0 -> x3, Pallas kernels: none -> 94.9 us  [the longest x1 61.8 us: rows_backward(): pl.pallas_call(rows_kernel, out_shape=tuple((jax.ShapeDtypeStruct(s, d) f...]
    gather x4 -> x0, local copies, waits for them, and re-layouts: 50.9 us -> none  [take_rows(): return jnp.take(rows, row_index, axis=0, mode='fill', fill_value=0)]
    all_to_all x3 -> x0, local copies, waits for them, and re-layouts: 32.4 us -> none  [the longest x1 11.6 us: local_backward(): dz_exp = lax.all_to_all(send_dz, 'ep', 0, 1, tiled=True)]
    reshape x6 -> x0, local copies, waits for them, and re-layouts: 27.8 us -> none  [the longest x1 9.18 us: local_backward(): lax.all_to_all(grad_exp, 'ep', 1, 0, tiled=True)]
    all_to_all x3 -> x0, starting transfers between devices: 16 us -> none  [the longest x1 5.59 us: local_backward(): x_exp = lax.all_to_all(send_x, 'ep', 0, 1, tiled=True)]
    convert_element_type x1 -> x0, local copies, waits for them, and re-layouts: 12.5 us -> none  [local_backward(): (jnp.einsum('erf,edf->erd', grad_gate, w_gate, preferred_element_type=jnp...]
  transfers between devices with their start and end apart: 3 -> 5, of which waited for: 2 -> 1; matrix products, arithmetic and copies ran while one was open for 36% -> 0% of each run, Pallas kernels for 0% -> 30%
where the time goes in v7:
time: 109 us
  Pallas kernels  94.9 us (87%)
  other arithmetic  6.96 us (6%)
  starting transfers between devices  4.13 us (4%)
  waiting for transfers between devices  1.9 us (2%)
    pallas_call x1, Pallas kernels, rows_backward(): pl.pallas_call(rows_kernel, out_shape=tuple((jax.ShapeDtypeStruct(s, d) f...  61.8 us
    pallas_call x1, Pallas kernels, up_grads(): pl.pallas_call(up_kernel, grid=(EXPERTS,), out_shape=(jax.ShapeDtypeStruc...  17.2 us
    pallas_call x1, Pallas kernels, down_grads(): pl.pallas_call(down_kernel, grid=(EXPERTS,), out_shape=(jax.ShapeDtypeStr...  15.9 us
    add x1, other arithmetic, local_backward(): near[1] + far[1]  2.69 us
  transfers between devices with their start and end apart: 5, of which 1 were waited for; matrix products, arithmetic and copies ran while one was open for 0% of the time, Pallas kernels for 30%

profile of v7, /device:TPU:0, one launch (start us, length us, event | category | flops | bytes accessed | tf_op | source)
XLA Modules:
  0.0 108.6 jit_solution(4994386850509802775)
XLA Ops:
  0.6 61.8 %rows_backward.1 = (bf16[2,4,4,64,2048]{4,3,2,1,0:T(8,128)(2,1)}, bf16[2,4,4,64,2048]{4,3,2,1,0:T(8,128)(2,1)}, bf16[2,4,4,64,512]{4,3,2,1,0:T(8,128)(2,1)}, bf1...) custom-call(bf16[128,2048]{1,0:T(8,128)(2,1)} %x_ref.3, ...), custom_call_target="tpu_custom_call" | custom-call | tf_op jit(solution)/shard_map/rows_backward/pallas_call | solution.py:387
  62.5 0.6 collective-permute-start
  63.1 1.2 %collective-permute-start.1 = (f32[128,1024]{1,0:T(8,128)}, f32[128,1024]{1,0:T(8,128)}, u32[]{:S(2)}, u32[]{:S(2)}) collective-permute-start(f32[128,1024]{1,0:T(8,128)} %get-tuple-element.40), channel_id=1, source_target_pairs={{0,4},{1,3},{2,6},{3,1},{4,0},{5,7},{6,2},{7,5},{8,12},{9,11},{10,... | collective-permute-start | bytes 1572872 | tf_op jit(solution)/shard_map/ppermute | solution.py:488
  64.3 15.9 %down_grads.1 = (f32[4,512,2048]{2,1,0:T(8,128)}, f32[1,2048,512]{2,1,0:T(8,128)}, f32[1,2048,512]{2,1,0:T(8,128)}, f32[1,512,2048]{2,1,0:T(8,128)}) custom-call(bf16[8,4,64,2048]{3,2,1,0:T(8,128)(2,1)} %bitcast.38, bf16[8,4,64,512]{3,2,1,0:T(8,128)(2,1)} %bitcast.41, bf16[128,2048]{1,0:T(8,128)(2,1)} %x_ref.3, bf16[128,2048]{1,0:T(8,128)(2,1)} %dy_ref.3, ...), custom_call_target="tpu_custom_call" | custom-call | flops 5000000000 | bytes 40000000 | tf_op jit(solution)/shard_map/down_grads/pallas_call | solution.py:434
  80.2 0.0 collective-permute-done
  80.2 0.0 collective-permute-done.1
  80.2 2.7 %bitcast_add_fusion.3 = (f32[128,1024]{1,0:T(8,128)}, f32[128,1024]{1,0:T(8,128)}) fusion(f32[128,1024]{1,0:T(8,128)} %collective-permute-done.1, f32[2,128,1024]{2,1,0:T(8,128)} %get-tuple-element.38, f32[128,1024]{1,0:T(8,128)} %collective-permute-done), kind=kLoop, calls=%fused_computation.6 | loop fusion | flops 262144 | bytes 3145728 | tf_op jit(solution)/shard_map/add | solution.py:491
  82.9 0.8 collective-permute-start.2
  83.7 1.5 %collective-permute-start.3 = (f32[128,1024]{1,0:T(8,128)}, f32[128,1024]{1,0:T(8,128)}, u32[]{:S(2)}, u32[]{:S(2)}) collective-permute-start(f32[128,1024]{1,0:T(8,128)} %get-tuple-element.67), channel_id=1, source_target_pairs={{0,2},{1,5},{2,0},{3,7},{4,6},{5,1},{6,4},{7,3},{8,10},{9,13},{10,... | collective-permute-start | bytes 1572872 | tf_op jit(solution)/shard_map/ppermute | solution.py:491
  85.1 17.2 %up_grads.1 = (f32[4,2048,512]{2,1,0:T(8,128)}, f32[4,2048,512]{2,1,0:T(8,128)}) custom-call(bf16[8,4,64,2048]{3,2,1,0:T(8,128)(2,1)} %bitcast.37, bf16[8,4,64,512]{3,2,1,0:T(8,128)(2,1)} %bitcast.39, bf16[8,4,64,512]{3,2,1,0:T(8,128)(2,1)} %bitcast.40), custom_call_target="tpu_custom_call" | custom-call | flops 8999999488 | bytes 44000000 | tf_op jit(solution)/shard_map/up_grads/pallas_call | solution.py:457
  102.4 0.0 collective-permute-done.2
  102.4 0.0 collective-permute-done.3
  102.4 1.4 %bitcast_add_fusion.2 = f32[128,1024]{1,0:T(8,128)S(1)} fusion(f32[128,1024]{1,0:T(8,128)} %collective-permute-done.3, f32[2,128,1024]{2,1,0:T(8,128)} %get-tuple-element.37, f32[2,128,1024]{2,1,0:T(8,128)} %get-tuple-element.36), kind=kLoop, calls=%fused_computation.5 | loop fusion | flops 262144 | bytes 2097152 | tf_op jit(solution)/shard_map/add | solution.py:496
  103.8 0.0 collective-permute-start.4
  103.9 1.9 %collective-permute-done.4 = f32[128,1024]{1,0:T(8,128)S(1)} collective-permute-done((f32[128,1024]{1,0:T(8,128)S(1)}, f32[128,1024]{1,0:T(8,128)S(1)}, u32[]{:S(2)}, u32[]{:S(2)}) %collective-permute-start.4) | collective-permute-done | bytes 524320 | tf_op jit(solution)/shard_map/ppermute | solution.py:496
  105.8 2.0 %fusion.1 = (bf16[128,1024]{1,0:T(8,128)(2,1)S(1)}, bf16[128,1024]{1,0:T(8,128)(2,1)S(1)}) fusion(f32[2,128,1024]{2,1,0:T(8,128)} %get-tuple-element.58, f32[128,1024]{1,0:T(8,128)S(1)} %collective-permute-done.4, pred[]{:T(512)S(6)} %eq.4, f32[128,1024]{1,0:T(8,128)} %collective-permute-done.2, f32[2,128,1024]{2,1,0:T(8,128)} %get-tuple-element.37, ...), kind=kLoop, calls=%fused_computation.4 | loop fusion | flops 1048576 | bytes 3670017 | tf_op jit(solution)/shard_map/convert
  107.8 0.8 pad_maximum_fusion
Async XLA Ops:
  62.5 17.7 %collective-permute-start = (f32[128,1024]{1,0:T(8,128)}, f32[128,1024]{1,0:T(8,128)}, u32[]{:S(2)}, u32[]{:S(2)}) collective-permute-start(f32[128,1024]{1,0:T(8,128)} %get-tuple-element.39), channel_id=1, source_target_pairs={{0,2},{1,5},{2,0},{3,7},{4,6},{5,1},{6,4},{7,3},{8,10},{9,13},{10,... | collective-permute-start | bytes 1572872 | tf_op jit(solution)/shard_map/ppermute | solution.py:488
  63.1 17.1 %collective-permute-start.1 = (f32[128,1024]{1,0:T(8,128)}, f32[128,1024]{1,0:T(8,128)}, u32[]{:S(2)}, u32[]{:S(2)}) collective-permute-start(f32[128,1024]{1,0:T(8,128)} %get-tuple-element.40), channel_id=1, source_target_pairs={{0,4},{1,3},{2,6},{3,1},{4,0},{5,7},{6,2},{7,5},{8,12},{9,11},{10,... | collective-permute-start | bytes 1572872 | tf_op jit(solution)/shard_map/ppermute | solution.py:488
  82.9 19.5 %collective-permute-start.2 = (f32[128,1024]{1,0:T(8,128)}, f32[128,1024]{1,0:T(8,128)}, u32[]{:S(2)}, u32[]{:S(2)}) collective-permute-start(f32[128,1024]{1,0:T(8,128)} %get-tuple-element.68), channel_id=1, source_target_pairs={{0,4},{1,3},{2,6},{3,1},{4,0},{5,7},{6,2},{7,5},{8,12},{9,11},{10,... | collective-permute-start | bytes 1572872 | tf_op jit(solution)/shard_map/ppermute | solution.py:491
  83.7 18.7 %collective-permute-start.3 = (f32[128,1024]{1,0:T(8,128)}, f32[128,1024]{1,0:T(8,128)}, u32[]{:S(2)}, u32[]{:S(2)}) collective-permute-start(f32[128,1024]{1,0:T(8,128)} %get-tuple-element.67), channel_id=1, source_target_pairs={{0,2},{1,5},{2,0},{3,7},{4,6},{5,1},{6,4},{7,3},{8,10},{9,13},{10,... | collective-permute-start | bytes 1572872 | tf_op jit(solution)/shard_map/ppermute | solution.py:491
  103.8 1.9 %collective-permute-start.4 = (f32[128,1024]{1,0:T(8,128)S(1)}, f32[128,1024]{1,0:T(8,128)S(1)}, u32[]{:S(2)}, u32[]{:S(2)}) collective-permute-start(f32[128,1024]{1,0:T(8,128)S(1)} %bitcast_add_fusion.2), channel_id=1, source_target_pairs={{0,1},{1,0},{2,3},{3,2},{4,5},{5,4},{6,7},{7,6},{8,9},{9,8},{10,11... | collective-permute-start | bytes 1572872 | tf_op jit(solution)/shard_map/ppermute | solution.py:496

commit v8 on v7

--- a/solution.py
+++ b/solution.py
@@ -233,14 +233,12 @@
         return pltpu.make_async_copy(src, dst, shared_sem.at[which])
 
     def shared_rows_out(which):
-        return pltpu.make_async_copy(sums.at[which], dx_ref.at[which], shared_out.at[which])
+        return pltpu.make_async_copy(sums.at[which], dx_ref.at[:, which * HALF:(which + 1) * HALF], shared_out.at[which])
 
     def shared_parts_out(which):
         return pltpu.make_async_copy(acts.at[1, LATE, which, :TOKENS], parts_ref.at[which], shared_out.at[2 + which])
 
     def shared_chain():
-        for which in range(4):
-            shared_load(which).wait()
         x, dy = xbuf[0], dybuf[0]
         act_gate = dot_nn(x, r_mine[:, :, :INNER].reshape(WIDTH, INNER)).astype(BF16)
         act_up = dot_nn(x, r_mine[:, :, INNER:].reshape(WIDTH, INNER)).astype(BF16)
@@ -279,24 +277,26 @@
                 start(array, part, kind)
     for which in range(4):
         shared_load(which).start()
+    pick_x(EARLY, 0, 1)
+    pick_z(EARLY, 0, 1)
+    for which in range(4):
+        shared_load(which).wait()
     for expert in range(EXPERTS):
         load(0, expert).start()
         load(1, expert).start()
-    pick_x(EARLY, 0, 1)
-    pick_z(EARLY, 0, 1)
+    shared_chain()
+    first_in(X, 0)
+    start(X, 0, TO_SECOND)
     for role in SEEN_AS:
         for which in range(2):
             meta(which, role).wait_recv()
     arrived(X, TO_PARTNER)
     pick_x(EARLY, 1, 2)
-    shared_chain()
+    first_in(X, 1)
+    for expert in range(EXPERTS):
+        load(2, expert).start()
     arrived(DY, TO_PARTNER)
     pick_z(EARLY, 1, 2)
-    for part in range(PARTS):
-        first_in(X, part)
-    for expert in range(EXPERTS):
-        load(2, expert).start()
-    start(X, 0, TO_SECOND)
     arrived(X, FIRST_OVER)
     pick_x(EARLY, 2, 4)
 
@@ -377,7 +377,7 @@
     tables = (ROLES, 16, TOKENS)
     select = (ROLES, ROWS, TOKENS)
     dma = pltpu.SemaphoreType.DMA
-    outs = [(s, BF16) for s in (rows, rows, grads, grads, grads)] + [(pair[1:], F32)] * 2 + [(pair, F32)] * 4 + [(parts, BF16)]
+    outs = [(s, BF16) for s in (rows, rows, grads, grads, grads)] + [(pair[1:], F32)] * 2 + [(pair, F32)] * 3 + [((TOKENS, WIDTH), F32), (parts, BF16)]
     scratch = [(blocks, BF16), (blocks, BF16), (tables, jnp.int32), (tables, F32), (select, BF16), (select, BF16), (rows[1:], BF16), (rows[1:], BF16)]
     scratch += [(w.shape, BF16) for w in (w_gate, w_up, w_down)]
     scratch += [((2, 2, EXPERTS, ROWS, INNER), BF16), ((3, EXPERTS, 4, SLOT, INNER), BF16), ((16, SLOT, HALF), BF16), ((32, SLOT, HALF), BF16)]
@@ -497,7 +497,7 @@
         core = lax.rem(lax.axis_index('ep'), 2)
         left = jnp.where(core == 0, own, swapped)
         right = jnp.where(core == 0, swapped, own)
-        grad_x = jnp.concatenate((left + shared_dx[0], right + shared_dx[1]), axis=1).astype(BF16)
+        grad_x = (jnp.concatenate((left, right), axis=1) + shared_dx).astype(BF16)
         return grad_x, up[0], up[1], down[0], down[1], down[2], down[3]
 
     return jax.shard_map(local_backward, mesh=mesh, in_specs=(token_spec, token_spec, token_spec, token_spec, token_spec, expert_spec, expert_spec, expert_spec, whole_spec, whole_spec, whole_spec), out_specs=(token_spec, grad_spec, grad_spec, grad_spec, grad_spec, grad_spec, grad_spec), check_vma=False)

time: 109 us -> 109 us (level)
    another operation x1 -> x0, other arithmetic: 1.99 us -> none
    select_n x0 -> x1, other arithmetic: none -> 1.52 us  [local_backward(): left = jnp.where(core == 0, own, swapped)]
    ppermute x1, starting transfers between devices: 1.47 us -> 0.33 us  [local_backward(): lax.ppermute(near[1] + far[1], 'ep', partners('first'))]
    ppermute x1, starting transfers between devices: 0.59 us -> 1.73 us  [local_backward(): lax.ppermute(far, 'ep', partners('first'))]
  transfers between devices with their start and end apart: 5 -> 5, of which waited for: 1 -> 1; matrix products, arithmetic and copies ran while one was open for 0% -> 0% of each run, Pallas kernels for 30% -> 31%
where the time goes in v8:
time: 109 us
  Pallas kernels  95.1 us (87%)
  other arithmetic  6.67 us (6%)
  starting transfers between devices  4.12 us (4%)
  waiting for transfers between devices  1.9 us (2%)
    pallas_call x1, Pallas kernels, rows_backward(): pl.pallas_call(rows_kernel, out_shape=tuple((jax.ShapeDtypeStruct(s, d) f...  62 us
    pallas_call x1, Pallas kernels, up_grads(): pl.pallas_call(up_kernel, grid=(EXPERTS,), out_shape=(jax.ShapeDtypeStruc...  17.2 us
    pallas_call x1, Pallas kernels, down_grads(): pl.pallas_call(down_kernel, grid=(EXPERTS,), out_shape=(jax.ShapeDtypeStr...  15.9 us
    add x1, other arithmetic, local_backward(): near[1] + far[1]  2.69 us
  transfers between devices with their start and end apart: 5, of which 1 were waited for; matrix products, arithmetic and copies ran while one was open for 0% of the time, Pallas kernels for 31%

profile of v8, /device:TPU:0, one launch (start us, length us, event | category | flops | bytes accessed | tf_op | source)
XLA Modules:
  0.0 108.5 jit_solution(15746746430283758058)
XLA Ops:
  0.6 62.0 %rows_backward.1 = (bf16[2,4,4,64,2048]{4,3,2,1,0:T(8,128)(2,1)}, bf16[2,4,4,64,2048]{4,3,2,1,0:T(8,128)(2,1)}, bf16[2,4,4,64,512]{4,3,2,1,0:T(8,128)(2,1)}, bf1...) custom-call(bf16[128,2048]{1,0:T(8,128)(2,1)} %x_ref.3, ...), custom_call_target="tpu_custom_call" | custom-call | tf_op jit(solution)/shard_map/rows_backward/pallas_call | solution.py:387
  62.6 1.7 %collective-permute-start = (f32[128,1024]{1,0:T(8,128)}, f32[128,1024]{1,0:T(8,128)}, u32[]{:S(2)}, u32[]{:S(2)}) collective-permute-start(f32[128,1024]{1,0:T(8,128)} %get-tuple-element.39), channel_id=1, source_target_pairs={{0,2},{1,5},{2,0},{3,7},{4,6},{5,1},{6,4},{7,3},{8,10},{9,13},{10,... | collective-permute-start | bytes 1572872 | tf_op jit(solution)/shard_map/ppermute | solution.py:488
  64.4 0.3 collective-permute-start.1
  64.7 15.9 %down_grads.1 = (f32[4,512,2048]{2,1,0:T(8,128)}, f32[1,2048,512]{2,1,0:T(8,128)}, f32[1,2048,512]{2,1,0:T(8,128)}, f32[1,512,2048]{2,1,0:T(8,128)}) custom-call(bf16[8,4,64,2048]{3,2,1,0:T(8,128)(2,1)} %bitcast.30, bf16[8,4,64,512]{3,2,1,0:T(8,128)(2,1)} %bitcast.33, bf16[128,2048]{1,0:T(8,128)(2,1)} %x_ref.3, bf16[128,2048]{1,0:T(8,128)(2,1)} %dy_ref.3, ...), custom_call_target="tpu_custom_call" | custom-call | flops 5000000000 | bytes 40000000 | tf_op jit(solution)/shard_map/down_grads/pallas_call | solution.py:434
  80.6 0.0 collective-permute-done
  80.6 0.0 collective-permute-done.1
  80.6 2.7 %bitcast_add_fusion.1 = (f32[128,1024]{1,0:T(8,128)}, f32[128,1024]{1,0:T(8,128)}) fusion(f32[128,1024]{1,0:T(8,128)} %collective-permute-done.1, f32[2,128,1024]{2,1,0:T(8,128)} %get-tuple-element.38, f32[128,1024]{1,0:T(8,128)} %collective-permute-done), kind=kLoop, calls=%fused_computation.3 | loop fusion | flops 262144 | bytes 3145728 | tf_op jit(solution)/shard_map/add | solution.py:491
  83.3 1.7 %collective-permute-start.2 = (f32[128,1024]{1,0:T(8,128)}, f32[128,1024]{1,0:T(8,128)}, u32[]{:S(2)}, u32[]{:S(2)}) collective-permute-start(f32[128,1024]{1,0:T(8,128)} %get-tuple-element.68), channel_id=1, source_target_pairs={{0,4},{1,3},{2,6},{3,1},{4,0},{5,7},{6,2},{7,5},{8,12},{9,11},{10,... | collective-permute-start | bytes 1572872 | tf_op jit(solution)/shard_map/ppermute | solution.py:491
  85.0 0.3 collective-permute-start.3
  85.3 17.2 %up_grads.1 = (f32[4,2048,512]{2,1,0:T(8,128)}, f32[4,2048,512]{2,1,0:T(8,128)}) custom-call(bf16[8,4,64,2048]{3,2,1,0:T(8,128)(2,1)} %bitcast.29, bf16[8,4,64,512]{3,2,1,0:T(8,128)(2,1)} %bitcast.31, bf16[8,4,64,512]{3,2,1,0:T(8,128)(2,1)} %bitcast.32), custom_call_target="tpu_custom_call" | custom-call | flops 8999999488 | bytes 44000000 | tf_op jit(solution)/shard_map/up_grads/pallas_call | solution.py:457
  102.6 0.0 copy-start
  102.6 0.0 collective-permute-done.2
  102.6 0.0 collective-permute-done.3
  102.6 1.5 %bitcast_add_fusion = f32[128,1024]{1,0:T(8,128)S(1)} fusion(f32[128,1024]{1,0:T(8,128)} %collective-permute-done.3, f32[2,128,1024]{2,1,0:T(8,128)} %get-tuple-element.37, f32[2,128,1024]{2,1,0:T(8,128)} %get-tuple-element.36), kind=kLoop, calls=%fused_computation.2 | loop fusion | flops 262144 | bytes 2097152 | tf_op jit(solution)/shard_map/add | solution.py:496
  104.1 0.0 collective-permute-start.4
  104.2 1.9 %collective-permute-done.4 = f32[128,1024]{1,0:T(8,128)S(1)} collective-permute-done((f32[128,1024]{1,0:T(8,128)S(1)}, f32[128,1024]{1,0:T(8,128)S(1)}, u32[]{:S(2)}, u32[]{:S(2)}) %collective-permute-start.4) | collective-permute-done | bytes 524320 | tf_op jit(solution)/shard_map/ppermute | solution.py:496
  106.1 1.5 %broadcast_select_fusion.1 = (f32[128,1024]{1,0:T(8,128)S(1)}, f32[128,1024]{1,0:T(8,128)S(1)}) fusion(f32[128,1024]{1,0:T(8,128)S(1)} %collective-permute-done.4, pred[]{:T(512)S(6)} %eq.4, f32[128,1024]{1,0:T(8,128)} %collective-permute-done.2, f32[2,128,1024]{2,1,0:T(8,128)} %get-tuple-element.37, f32[2,128,1024]{2,1,0:T(8,128)} %get-tuple-element.36), kind=kLoop, calls=%fused_computation.7 | loop fusion | flops 524288 | bytes 3145729 | tf_op jit(solution)/shard_map/jit(_where)/select_n | solution.py:498
  107.6 0.0 copy-done
  107.6 0.9 fusion
Async XLA Ops:
  62.6 17.9 %collective-permute-start = (f32[128,1024]{1,0:T(8,128)}, f32[128,1024]{1,0:T(8,128)}, u32[]{:S(2)}, u32[]{:S(2)}) collective-permute-start(f32[128,1024]{1,0:T(8,128)} %get-tuple-element.39), channel_id=1, source_target_pairs={{0,2},{1,5},{2,0},{3,7},{4,6},{5,1},{6,4},{7,3},{8,10},{9,13},{10,... | collective-permute-start | bytes 1572872 | tf_op jit(solution)/shard_map/ppermute | solution.py:488
  64.4 16.2 %collective-permute-start.1 = (f32[128,1024]{1,0:T(8,128)}, f32[128,1024]{1,0:T(8,128)}, u32[]{:S(2)}, u32[]{:S(2)}) collective-permute-start(f32[128,1024]{1,0:T(8,128)} %get-tuple-element.40), channel_id=1, source_target_pairs={{0,4},{1,3},{2,6},{3,1},{4,0},{5,7},{6,2},{7,5},{8,12},{9,11},{10,... | collective-permute-start | bytes 1572872 | tf_op jit(solution)/shard_map/ppermute | solution.py:488
  83.3 19.3 %collective-permute-start.2 = (f32[128,1024]{1,0:T(8,128)}, f32[128,1024]{1,0:T(8,128)}, u32[]{:S(2)}, u32[]{:S(2)}) collective-permute-start(f32[128,1024]{1,0:T(8,128)} %get-tuple-element.68), channel_id=1, source_target_pairs={{0,4},{1,3},{2,6},{3,1},{4,0},{5,7},{6,2},{7,5},{8,12},{9,11},{10,... | collective-permute-start | bytes 1572872 | tf_op jit(solution)/shard_map/ppermute | solution.py:491
  85.0 17.6 %collective-permute-start.3 = (f32[128,1024]{1,0:T(8,128)}, f32[128,1024]{1,0:T(8,128)}, u32[]{:S(2)}, u32[]{:S(2)}) collective-permute-start(f32[128,1024]{1,0:T(8,128)} %get-tuple-element.67), channel_id=1, source_target_pairs={{0,2},{1,5},{2,0},{3,7},{4,6},{5,1},{6,4},{7,3},{8,10},{9,13},{10,... | collective-permute-start | bytes 1572872 | tf_op jit(solution)/shard_map/ppermute | solution.py:491
  102.6 5.0 %copy-start = (f32[128,2048]{1,0:T(8,128)S(1)}, f32[128,2048]{1,0:T(8,128)}, u32[]{:S(2)}) copy-start(f32[128,2048]{1,0:T(8,128)} %get-tuple-element.58) | copy-start | bytes 3145732
  104.1 1.9 %collective-permute-start.4 = (f32[128,1024]{1,0:T(8,128)S(1)}, f32[128,1024]{1,0:T(8,128)S(1)}, u32[]{:S(2)}, u32[]{:S(2)}) collective-permute-start(f32[128,1024]{1,0:T(8,128)S(1)} %bitcast_add_fusion), channel_id=1, source_target_pairs={{0,1},{1,0},{2,3},{3,2},{4,5},{5,4},{6,7},{7,6},{8,9},{9,8},{10,11... | collective-permute-start | bytes 1572872 | tf_op jit(solution)/shard_map/ppermute | solution.py:496

commit v9 on v8

--- a/solution.py
+++ b/solution.py
@@ -65,6 +65,11 @@
     return hits.astype(BF16)
 
 
+def unrolled(low, high, step):
+    for index in range(low, high):
+        step(index, 0)
+
+
 def rows_kernel(x_ref, dy_ref, ids_ref, pos_ref, gate_ref, w1_ref, w3_ref, w2_ref, s1_ref, s3_ref, s2_ref, xr_ref, zr_ref, h_ref, da_ref, db_ref, far_ref, cross_ref, near_ref, base_ref, leaf_ref, dx_ref, parts_ref, xbuf, dybuf, codes, gates, picks, picks_partner, x_rows, z_rows, w1_buf, w3_buf, w2_buf, acts, grads, r_send, r_mine, r_got, sums, own_sem, send_sem, recv_sem, meta_send, meta_recv, load_sem, rows_sem, grads_sem, swap_send, swap_recv, sums_sem, leaf_send, leaf_recv, shared_sem, shared_out):
     me, core, first, second, diag, partner = places()
     other = 1 - core
@@ -123,7 +128,7 @@
             rows_out(X, half, at).start()
             return carry
 
-        lax.fori_loop(low, high, one, 0)
+        unrolled(low, high, one)
 
     def pick_z(half, low, high):
         def one(at, carry):
@@ -141,7 +146,7 @@
             rows_out(DY, half, at).start()
             return carry
 
-        lax.fori_loop(low, high, one, 0)
+        unrolled(low, high, one)
 
     def activations(half, after):
         def one(expert, carry):
@@ -151,11 +156,10 @@
             rows = x_rows[:, expert].reshape(ROWS, WIDTH)
             acts[0, half, expert] = dot_nn(rows, w1_buf[expert]).astype(BF16)
             acts[1, half, expert] = dot_nn(rows, w3_buf[expert]).astype(BF16)
-            for step, action in after.items():
-                pl.when(expert == step)(action)
-            return carry
-
-        lax.fori_loop(0, EXPERTS, one, 0)
+            if expert in after:
+                after[expert]()
+
+        unrolled(0, EXPERTS, one)
 
     def grads_out(which, half, expert):
         return pltpu.make_async_copy(grads.at[which, expert], (h_ref, da_ref, db_ref)[which].at[half, :, expert], grads_sem.at[which, half, expert])
@@ -337,11 +341,11 @@
         shared_parts_out(which).wait()
     activations(LATE, {1: lambda: second_in(DY, 0), 3: lambda: second_in(DY, 1)})
     diag_in(DY, 0)
-    arrived(DY, SECOND_OVER)
-    pick_z(LATE, 0, 2)
     diag_in(DY, 1)
     for which in range(2):
         leaf(which).start()
+    arrived(DY, SECOND_OVER)
+    pick_z(LATE, 0, 2)
     arrived(DY, DIAG_OVER)
     pick_z(LATE, 2, 4)
     back(LATE, {})
@@ -492,8 +496,8 @@
         d_gate, *_ = lax.optimization_barrier((d_gate,) + tuple(far))
         up = up_grads(x_rows, d_gate, d_up)
         last, up = lax.optimization_barrier((last, up))
-        own = base[0] + leaf[0] + last[0]
-        swapped = lax.ppermute(base[1] + leaf[1] + last[1], 'ep', partners('chip'))
+        own, given = lax.optimization_barrier((base[0] + leaf[0] + last[0], base[1] + leaf[1] + last[1]))
+        swapped = lax.ppermute(given, 'ep', partners('chip'))
         core = lax.rem(lax.axis_index('ep'), 2)
         left = jnp.where(core == 0, own, swapped)
         right = jnp.where(core == 0, swapped, own)

time: 109 us -> 106 us (0.972)
  Pallas kernels: 95.1 us -> 93.1 us
    pallas_call x1, Pallas kernels: 62 us -> 60 us  [rows_backward(): pl.pallas_call(rows_kernel, out_shape=tuple((jax.ShapeDtypeStruct(s, d) f...]
    select_n x1, other arithmetic: 1.52 us -> 0.09 us  [local_backward(): left = jnp.where(core == 0, own, swapped)]
where the time goes in v9:
time: 106 us
  Pallas kernels  93.1 us (88%)
  other arithmetic  5.88 us (6%)
  starting transfers between devices  4.13 us (4%)
  waiting for transfers between devices  1.9 us (2%)
    pallas_call x1, Pallas kernels, rows_backward(): pl.pallas_call(rows_kernel, out_shape=tuple((jax.ShapeDtypeStruct(s, d) f...  60 us
    pallas_call x1, Pallas kernels, up_grads(): pl.pallas_call(up_kernel, grid=(EXPERTS,), out_shape=(jax.ShapeDtypeStruc...  17.2 us
    pallas_call x1, Pallas kernels, down_grads(): pl.pallas_call(down_kernel, grid=(EXPERTS,), out_shape=(jax.ShapeDtypeStr...  15.9 us
    add x1, other arithmetic, local_backward(): near[1] + far[1]  2.68 us
    add x1, other arithmetic, local_backward(): base[1] + leaf[1] + last[1]  2.19 us
  transfers between devices with their start and end apart: 5, of which 1 were waited for; matrix products, arithmetic and copies ran while one was open for 0% of the time, Pallas kernels for 31%

profile of v9, /device:TPU:0, one launch (start us, length us, event | category | flops | bytes accessed | tf_op | source)
XLA Modules:
  0.0 105.7 jit_solution(17441965761802444324)
XLA Ops:
  0.6 60.0 %rows_backward.1 = (bf16[2,4,4,64,2048]{4,3,2,1,0:T(8,128)(2,1)}, bf16[2,4,4,64,2048]{4,3,2,1,0:T(8,128)(2,1)}, bf16[2,4,4,64,512]{4,3,2,1,0:T(8,128)(2,1)}, bf1...) custom-call(bf16[128,2048]{1,0:T(8,128)(2,1)} %x_ref.3, ...), custom_call_target="tpu_custom_call" | custom-call | tf_op jit(solution)/shard_map/rows_backward/pallas_call | solution.py:391
  60.6 1.9 %collective-permute-start = (f32[128,1024]{1,0:T(8,128)}, f32[128,1024]{1,0:T(8,128)}, u32[]{:S(2)}, u32[]{:S(2)}) collective-permute-start(f32[128,1024]{1,0:T(8,128)} %get-tuple-element.41), channel_id=1, source_target_pairs={{0,2},{1,5},{2,0},{3,7},{4,6},{5,1},{6,4},{7,3},{8,10},{9,13},{10,... | collective-permute-start | bytes 1572872 | tf_op jit(solution)/shard_map/ppermute | solution.py:492
  62.6 0.1 collective-permute-start.1
  62.7 15.9 %down_grads.1 = (f32[4,512,2048]{2,1,0:T(8,128)}, f32[1,2048,512]{2,1,0:T(8,128)}, f32[1,2048,512]{2,1,0:T(8,128)}, f32[1,512,2048]{2,1,0:T(8,128)}) custom-call(bf16[8,4,64,2048]{3,2,1,0:T(8,128)(2,1)} %bitcast.26, bf16[8,4,64,512]{3,2,1,0:T(8,128)(2,1)} %bitcast.29, bf16[128,2048]{1,0:T(8,128)(2,1)} %x_ref.3, bf16[128,2048]{1,0:T(8,128)(2,1)} %dy_ref.3, ...), custom_call_target="tpu_custom_call" | custom-call | flops 5000000000 | bytes 40000000 | tf_op jit(solution)/shard_map/down_grads/pallas_call | solution.py:438
  78.5 0.0 collective-permute-done
  78.5 0.0 collective-permute-done.1
  78.6 2.7 %bitcast_add_fusion.1 = (f32[128,1024]{1,0:T(8,128)}, f32[128,1024]{1,0:T(8,128)}) fusion(f32[128,1024]{1,0:T(8,128)} %collective-permute-done.1, f32[2,128,1024]{2,1,0:T(8,128)} %get-tuple-element.40, f32[128,1024]{1,0:T(8,128)} %collective-permute-done), kind=kLoop, calls=%fused_computation.3 | loop fusion | flops 262144 | bytes 3145728 | tf_op jit(solution)/shard_map/add | solution.py:495
  81.2 1.9 %collective-permute-start.2 = (f32[128,1024]{1,0:T(8,128)}, f32[128,1024]{1,0:T(8,128)}, u32[]{:S(2)}, u32[]{:S(2)}) collective-permute-start(f32[128,1024]{1,0:T(8,128)} %get-tuple-element.74), channel_id=1, source_target_pairs={{0,4},{1,3},{2,6},{3,1},{4,0},{5,7},{6,2},{7,5},{8,12},{9,11},{10,... | collective-permute-start | bytes 1572872 | tf_op jit(solution)/shard_map/ppermute | solution.py:495
  83.2 0.1 collective-permute-start.3
  83.3 17.2 %up_grads.1 = (f32[4,2048,512]{2,1,0:T(8,128)}, f32[4,2048,512]{2,1,0:T(8,128)}) custom-call(bf16[8,4,64,2048]{3,2,1,0:T(8,128)(2,1)} %bitcast.25, bf16[8,4,64,512]{3,2,1,0:T(8,128)(2,1)} %bitcast.27, bf16[8,4,64,512]{3,2,1,0:T(8,128)(2,1)} %bitcast.28), custom_call_target="tpu_custom_call" | custom-call | flops 8999999488 | bytes 44000000 | tf_op jit(solution)/shard_map/up_grads/pallas_call | solution.py:461
  100.5 0.0 copy-start
  100.5 0.0 collective-permute-done.2
  100.5 0.0 collective-permute-done.3
  100.5 2.2 %bitcast_add_fusion = (f32[128,1024]{1,0:T(8,128)S(1)}, f32[128,1024]{1,0:T(8,128)S(1)}) fusion(f32[128,1024]{1,0:T(8,128)} %collective-permute-done.3, f32[2,128,1024]{2,1,0:T(8,128)} %get-tuple-element.39, f32[2,128,1024]{2,1,0:T(8,128)} %get-tuple-element.38, f32[128,1024]{1,0:T(8,128)} %collective-permute-done.2), kind=kLoop, calls=%fused_computation.2 | loop fusion | flops 524288 | bytes 4194304 | tf_op jit(solution)/shard_map/add | solution.py:499
  102.7 0.0 collective-permute-start.4
  102.8 1.9 %collective-permute-done.4 = f32[128,1024]{1,0:T(8,128)S(1)} collective-permute-done((f32[128,1024]{1,0:T(8,128)S(1)}, f32[128,1024]{1,0:T(8,128)S(1)}, u32[]{:S(2)}, u32[]{:S(2)}) %collective-permute-start.4) | collective-permute-done | bytes 524320 | tf_op jit(solution)/shard_map/ppermute | solution.py:500
  104.7 0.1 broadcast_select_fusion.1
  104.8 0.0 copy-done
  104.8 0.9 fusion
Async XLA Ops:
  60.6 17.9 %collective-permute-start = (f32[128,1024]{1,0:T(8,128)}, f32[128,1024]{1,0:T(8,128)}, u32[]{:S(2)}, u32[]{:S(2)}) collective-permute-start(f32[128,1024]{1,0:T(8,128)} %get-tuple-element.41), channel_id=1, source_target_pairs={{0,2},{1,5},{2,0},{3,7},{4,6},{5,1},{6,4},{7,3},{8,10},{9,13},{10,... | collective-permute-start | bytes 1572872 | tf_op jit(solution)/shard_map/ppermute | solution.py:492
  62.6 16.0 %collective-permute-start.1 = (f32[128,1024]{1,0:T(8,128)}, f32[128,1024]{1,0:T(8,128)}, u32[]{:S(2)}, u32[]{:S(2)}) collective-permute-start(f32[128,1024]{1,0:T(8,128)} %get-tuple-element.42), channel_id=1, source_target_pairs={{0,4},{1,3},{2,6},{3,1},{4,0},{5,7},{6,2},{7,5},{8,12},{9,11},{10,... | collective-permute-start | bytes 1572872 | tf_op jit(solution)/shard_map/ppermute | solution.py:492
  81.2 19.3 %collective-permute-start.2 = (f32[128,1024]{1,0:T(8,128)}, f32[128,1024]{1,0:T(8,128)}, u32[]{:S(2)}, u32[]{:S(2)}) collective-permute-start(f32[128,1024]{1,0:T(8,128)} %get-tuple-element.74), channel_id=1, source_target_pairs={{0,4},{1,3},{2,6},{3,1},{4,0},{5,7},{6,2},{7,5},{8,12},{9,11},{10,... | collective-permute-start | bytes 1572872 | tf_op jit(solution)/shard_map/ppermute | solution.py:495
  83.2 17.4 %collective-permute-start.3 = (f32[128,1024]{1,0:T(8,128)}, f32[128,1024]{1,0:T(8,128)}, u32[]{:S(2)}, u32[]{:S(2)}) collective-permute-start(f32[128,1024]{1,0:T(8,128)} %get-tuple-element.73), channel_id=1, source_target_pairs={{0,2},{1,5},{2,0},{3,7},{4,6},{5,1},{6,4},{7,3},{8,10},{9,13},{10,... | collective-permute-start | bytes 1572872 | tf_op jit(solution)/shard_map/ppermute | solution.py:495
  100.5 4.3 %copy-start = (f32[128,2048]{1,0:T(8,128)S(1)}, f32[128,2048]{1,0:T(8,128)}, u32[]{:S(2)}) copy-start(f32[128,2048]{1,0:T(8,128)} %get-tuple-element.62) | copy-start | bytes 3145732
  102.7 1.9 %collective-permute-start.4 = (f32[128,1024]{1,0:T(8,128)S(1)}, f32[128,1024]{1,0:T(8,128)S(1)}, u32[]{:S(2)}, u32[]{:S(2)}) collective-permute-start(f32[128,1024]{1,0:T(8,128)S(1)} %get-tuple-element.61), channel_id=1, source_target_pairs={{0,1},{1,0},{2,3},{3,2},{4,5},{5,4},{6,7},{7,6},{8,9},{9,8},{10,11... | collective-permute-start | bytes 1572872 | tf_op jit(solution)/shard_map/ppermute | solution.py:500

commit v10 on v9

--- a/solution.py
+++ b/solution.py
@@ -408,11 +408,16 @@
 
     @pl.when(expert == 0)
     def _():
-        x_t = x_ref[...].T
-        s1_buf[...] = dot_nn(x_t, parts_ref[1])
+        s1_buf[...] = dot_nn(x_ref[...].T, parts_ref[1])
         shared_out(0).start()
-        s3_buf[...] = dot_nn(x_t, parts_ref[2])
+
+    @pl.when(expert == 1)
+    def _():
+        s3_buf[...] = dot_nn(x_ref[...].T, parts_ref[2])
         shared_out(1).start()
+
+    @pl.when(expert == 2)
+    def _():
         s2_buf[...] = dot_nn(parts_ref[0].T, dy_ref[...])
         shared_out(2).start()
 

time: 106 us -> 104 us (0.981)
  Pallas kernels: 93.1 us -> 91 us
    pallas_call x1, Pallas kernels: 15.9 us -> 13.8 us  [down_grads(): pl.pallas_call(down_kernel, grid=(EXPERTS,), out_shape=(jax.ShapeDtypeStr...]
  transfers between devices with their start and end apart: 5 -> 5, of which waited for: 1 -> 1; matrix products, arithmetic and copies ran while one was open for 0% -> 0% of each run, Pallas kernels for 31% -> 30%
where the time goes in v10:
time: 104 us
  Pallas kernels  91 us (88%)
  other arithmetic  5.88 us (6%)
  starting transfers between devices  4.13 us (4%)
  waiting for transfers between devices  1.9 us (2%)
    pallas_call x1, Pallas kernels, rows_backward(): pl.pallas_call(rows_kernel, out_shape=tuple((jax.ShapeDtypeStruct(s, d) f...  60 us
    pallas_call x1, Pallas kernels, up_grads(): pl.pallas_call(up_kernel, grid=(EXPERTS,), out_shape=(jax.ShapeDtypeStruc...  17.2 us
    pallas_call x1, Pallas kernels, down_grads(): pl.pallas_call(down_kernel, grid=(EXPERTS,), out_shape=(jax.ShapeDtypeStr...  13.8 us
    add x1, other arithmetic, local_backward(): near[1] + far[1]  2.68 us
    add x1, other arithmetic, local_backward(): base[1] + leaf[1] + last[1]  2.19 us
  transfers between devices with their start and end apart: 5, of which 1 were waited for; matrix products, arithmetic and copies ran while one was open for 0% of the time, Pallas kernels for 30%

profile of v10, /device:TPU:0, one launch (start us, length us, event | category | flops | bytes accessed | tf_op | source)
XLA Modules:
  0.0 103.6 jit_solution(8994605143907487520)
XLA Ops:
  0.6 60.0 %rows_backward.1 = (bf16[2,4,4,64,2048]{4,3,2,1,0:T(8,128)(2,1)}, bf16[2,4,4,64,2048]{4,3,2,1,0:T(8,128)(2,1)}, bf16[2,4,4,64,512]{4,3,2,1,0:T(8,128)(2,1)}, bf1...) custom-call(bf16[128,2048]{1,0:T(8,128)(2,1)} %x_ref.3, ...), custom_call_target="tpu_custom_call" | custom-call | tf_op jit(solution)/shard_map/rows_backward/pallas_call | solution.py:391
  60.6 1.9 %collective-permute-start = (f32[128,1024]{1,0:T(8,128)}, f32[128,1024]{1,0:T(8,128)}, u32[]{:S(2)}, u32[]{:S(2)}) collective-permute-start(f32[128,1024]{1,0:T(8,128)} %get-tuple-element.41), channel_id=1, source_target_pairs={{0,2},{1,5},{2,0},{3,7},{4,6},{5,1},{6,4},{7,3},{8,10},{9,13},{10,... | collective-permute-start | bytes 1572872 | tf_op jit(solution)/shard_map/ppermute | solution.py:497
  62.6 0.1 collective-permute-start.1
  62.7 13.8 %down_grads.1 = (f32[4,512,2048]{2,1,0:T(8,128)}, f32[1,2048,512]{2,1,0:T(8,128)}, f32[1,2048,512]{2,1,0:T(8,128)}, f32[1,512,2048]{2,1,0:T(8,128)}) custom-call(bf16[8,4,64,2048]{3,2,1,0:T(8,128)(2,1)} %bitcast.26, bf16[8,4,64,512]{3,2,1,0:T(8,128)(2,1)} %bitcast.29, bf16[128,2048]{1,0:T(8,128)(2,1)} %x_ref.3, bf16[128,2048]{1,0:T(8,128)(2,1)} %dy_ref.3, ...), custom_call_target="tpu_custom_call" | custom-call | flops 5000000000 | bytes 40000000 | tf_op jit(solution)/shard_map/down_grads/pallas_call | solution.py:443
  76.4 0.0 collective-permute-done
  76.4 0.0 collective-permute-done.1
  76.4 2.7 %bitcast_add_fusion.1 = (f32[128,1024]{1,0:T(8,128)}, f32[128,1024]{1,0:T(8,128)}) fusion(f32[128,1024]{1,0:T(8,128)} %collective-permute-done.1, f32[2,128,1024]{2,1,0:T(8,128)} %get-tuple-element.40, f32[128,1024]{1,0:T(8,128)} %collective-permute-done), kind=kLoop, calls=%fused_computation.3 | loop fusion | flops 262144 | bytes 3145728 | tf_op jit(solution)/shard_map/add | solution.py:500
  79.1 1.9 %collective-permute-start.2 = (f32[128,1024]{1,0:T(8,128)}, f32[128,1024]{1,0:T(8,128)}, u32[]{:S(2)}, u32[]{:S(2)}) collective-permute-start(f32[128,1024]{1,0:T(8,128)} %get-tuple-element.74), channel_id=1, source_target_pairs={{0,4},{1,3},{2,6},{3,1},{4,0},{5,7},{6,2},{7,5},{8,12},{9,11},{10,... | collective-permute-start | bytes 1572872 | tf_op jit(solution)/shard_map/ppermute | solution.py:500
  81.1 0.1 collective-permute-start.3
  81.2 17.2 %up_grads.1 = (f32[4,2048,512]{2,1,0:T(8,128)}, f32[4,2048,512]{2,1,0:T(8,128)}) custom-call(bf16[8,4,64,2048]{3,2,1,0:T(8,128)(2,1)} %bitcast.25, bf16[8,4,64,512]{3,2,1,0:T(8,128)(2,1)} %bitcast.27, bf16[8,4,64,512]{3,2,1,0:T(8,128)(2,1)} %bitcast.28), custom_call_target="tpu_custom_call" | custom-call | flops 8999999488 | bytes 44000000 | tf_op jit(solution)/shard_map/up_grads/pallas_call | solution.py:466
  98.4 0.0 copy-start
  98.4 0.0 collective-permute-done.2
  98.4 0.0 collective-permute-done.3
  98.4 2.2 %bitcast_add_fusion = (f32[128,1024]{1,0:T(8,128)S(1)}, f32[128,1024]{1,0:T(8,128)S(1)}) fusion(f32[128,1024]{1,0:T(8,128)} %collective-permute-done.3, f32[2,128,1024]{2,1,0:T(8,128)} %get-tuple-element.39, f32[2,128,1024]{2,1,0:T(8,128)} %get-tuple-element.38, f32[128,1024]{1,0:T(8,128)} %collective-permute-done.2), kind=kLoop, calls=%fused_computation.2 | loop fusion | flops 524288 | bytes 4194304 | tf_op jit(solution)/shard_map/add | solution.py:504
  100.6 0.0 collective-permute-start.4
  100.7 1.9 %collective-permute-done.4 = f32[128,1024]{1,0:T(8,128)S(1)} collective-permute-done((f32[128,1024]{1,0:T(8,128)S(1)}, f32[128,1024]{1,0:T(8,128)S(1)}, u32[]{:S(2)}, u32[]{:S(2)}) %collective-permute-start.4) | collective-permute-done | bytes 524320 | tf_op jit(solution)/shard_map/ppermute | solution.py:505
  102.6 0.1 broadcast_select_fusion.1
  102.7 0.0 copy-done
  102.7 0.9 fusion
Async XLA Ops:
  60.6 15.8 %collective-permute-start = (f32[128,1024]{1,0:T(8,128)}, f32[128,1024]{1,0:T(8,128)}, u32[]{:S(2)}, u32[]{:S(2)}) collective-permute-start(f32[128,1024]{1,0:T(8,128)} %get-tuple-element.41), channel_id=1, source_target_pairs={{0,2},{1,5},{2,0},{3,7},{4,6},{5,1},{6,4},{7,3},{8,10},{9,13},{10,... | collective-permute-start | bytes 1572872 | tf_op jit(solution)/shard_map/ppermute | solution.py:497
  62.6 13.9 %collective-permute-start.1 = (f32[128,1024]{1,0:T(8,128)}, f32[128,1024]{1,0:T(8,128)}, u32[]{:S(2)}, u32[]{:S(2)}) collective-permute-start(f32[128,1024]{1,0:T(8,128)} %get-tuple-element.42), channel_id=1, source_target_pairs={{0,4},{1,3},{2,6},{3,1},{4,0},{5,7},{6,2},{7,5},{8,12},{9,11},{10,... | collective-permute-start | bytes 1572872 | tf_op jit(solution)/shard_map/ppermute | solution.py:497
  79.1 19.3 %collective-permute-start.2 = (f32[128,1024]{1,0:T(8,128)}, f32[128,1024]{1,0:T(8,128)}, u32[]{:S(2)}, u32[]{:S(2)}) collective-permute-start(f32[128,1024]{1,0:T(8,128)} %get-tuple-element.74), channel_id=1, source_target_pairs={{0,4},{1,3},{2,6},{3,1},{4,0},{5,7},{6,2},{7,5},{8,12},{9,11},{10,... | collective-permute-start | bytes 1572872 | tf_op jit(solution)/shard_map/ppermute | solution.py:500
  81.1 17.4 %collective-permute-start.3 = (f32[128,1024]{1,0:T(8,128)}, f32[128,1024]{1,0:T(8,128)}, u32[]{:S(2)}, u32[]{:S(2)}) collective-permute-start(f32[128,1024]{1,0:T(8,128)} %get-tuple-element.73), channel_id=1, source_target_pairs={{0,2},{1,5},{2,0},{3,7},{4,6},{5,1},{6,4},{7,3},{8,10},{9,13},{10,... | collective-permute-start | bytes 1572872 | tf_op jit(solution)/shard_map/ppermute | solution.py:500
  98.4 4.3 %copy-start = (f32[128,2048]{1,0:T(8,128)S(1)}, f32[128,2048]{1,0:T(8,128)}, u32[]{:S(2)}) copy-start(f32[128,2048]{1,0:T(8,128)} %get-tuple-element.62) | copy-start | bytes 3145732
  100.6 1.9 %collective-permute-start.4 = (f32[128,1024]{1,0:T(8,128)S(1)}, f32[128,1024]{1,0:T(8,128)S(1)}, u32[]{:S(2)}, u32[]{:S(2)}) collective-permute-start(f32[128,1024]{1,0:T(8,128)S(1)} %get-tuple-element.61), channel_id=1, source_target_pairs={{0,1},{1,0},{2,3},{3,2},{4,5},{5,4},{6,7},{7,6},{8,9},{9,8},{10,11... | collective-permute-start | bytes 1572872 | tf_op jit(solution)/shard_map/ppermute | solution.py:505
